TPU v7x, 32 devices: a whole 2x2x4 slice. The times are simulated.
32 devices in a mesh: dp: 4 (over y, core), seq: 8 (over z, x).
Axes of the slice: x: 2, y: 2, z: 4, core: 2. Of those that a mesh axis runs over, the one named last changes fastest.
Arguments:
- queries: bfloat16 [32, 2048, 512], P('dp', 'seq'), may hold values from -6 to 6
- enc_keys: bfloat16 [32, 2048, 512], P('dp', 'seq'), may hold values from -6 to 6
- enc_values: bfloat16 [32, 2048, 512], P('dp', 'seq'), may hold values from -6 to 6
- dec_ids: int32 [32, 2048], P('dp', 'seq'), may hold values from 0 to 15, never falling along the last dimension, each value on 1 to 512 neighbouring positions
- enc_ids: int32 [32, 2048], P('dp', 'seq'), may hold values from 0 to 15, never falling along the last dimension, each value on 1 to 512 neighbouring positions
Outputs:
- context: bfloat16 [32, 2048, 512], P('dp', 'seq')
Inputs may be any that keep to these rules, and one draw needn't show every extreme that they name: `dec_ids`: along each row the numbers never fall; every number from 0 to 15 occurs in every row; a document holds 1 to 512 positions of a row, and some document holds exactly 512. `enc_ids`: along each row the numbers never fall; every number from 0 to 15 occurs in every row; a document holds 1 to 512 positions of a row, and some document holds exactly 512.
All inputs are finite; a program needn't handle non-finite values.
Results may differ from a plain program's by a relative error of at most 0.0047.
Values may be sent and summed in bfloat16 or wider, within the bound.
A program may use at most 128 MiB of HBM per device.

v0:
```python
import functools

import jax
import jax.numpy as jnp
from jax import lax
from jax.experimental import pallas as pl
from jax.experimental.pallas import tpu as pltpu
from jax.sharding import PartitionSpec as P

HEAD_DIM = 64
DOCS = 16
SPAN = 256
MASKED = -8192.0


def pack_kernel(rows, q_ref, k_ref, v_ref, ids_ref, o_ref):
    group, _, count = o_ref.shape
    width = q_ref.shape[2] // group

    @pl.when(pl.program_id(0) < rows)
    def _():
        for slot, ref in enumerate((q_ref, k_ref, v_ref)):
            o_ref[:, slot * width : (slot + 1) * width] = ref[0].T.reshape(group, width, count)

    @pl.when(pl.program_id(0) == rows)
    def _():
        for target in range(group):
            o_ref[target, : ids_ref.shape[0]] = ids_ref[...]


def pack(q, k, v, ids, group, first, rows, with_ids):
    _, count, features = q.shape
    width = features // group
    spec = pl.BlockSpec((1, count, features), lambda r: (jnp.minimum(r, rows - 1) + first, 0, 0))
    more = ids.shape[0] if with_ids else 0
    return pl.pallas_call(
        functools.partial(pack_kernel, rows),
        grid=(rows + 1 if with_ids else rows,),
        in_specs=[spec] * 3 + [pl.BlockSpec(ids.shape, lambda r: (0, 0))],
        out_specs=pl.BlockSpec((group, 3 * width, count), lambda r: (0, r, 0)),
        out_shape=jax.ShapeDtypeStruct((group, rows * 3 * width + more, count), q.dtype),
        cost_estimate=pl.CostEstimate(
            flops=4 * rows * count * features, bytes_accessed=12 * rows * count * features, transcendentals=0
        ),
    )(q, k, v, ids)


def deliver_kernel(group, x_ref, q_ref, k_ref, v_ref, o_ref, p_ref, held, own_sem, send_sem, recv_sem):
    me = lax.axis_index("seq")

    def transfer(shift):
        target = lax.rem(me + shift, group)
        return pltpu.make_async_remote_copy(
            src_ref=x_ref.at[target],
            dst_ref=o_ref.at[me],
            send_sem=send_sem.at[shift - 1],
            recv_sem=recv_sem.at[shift - 1],
            device_id={"seq": target},
            device_id_type=pl.DeviceIdType.MESH,
        )

    @pl.when(pl.program_id(0) == 0)
    def _():
        barrier = pltpu.get_barrier_semaphore()
        for shift in range(1, group):
            pl.semaphore_signal(
                barrier, inc=1, device_id={"seq": lax.rem(me + shift, group)}, device_id_type=pl.DeviceIdType.MESH
            )
        pl.semaphore_wait(barrier, group - 1)
        for shift in sorted(range(1, group), key=lambda shift: abs(2 * shift - group)):
            transfer(shift).start()
        own = pltpu.make_async_copy(x_ref.at[me], held, own_sem)
        own.start()
        own.wait()
        own = pltpu.make_async_copy(held, o_ref.at[me], own_sem)
        own.start()
        own.wait()

    _, _, count = p_ref.shape
    width = q_ref.shape[2] // group
    for slot, ref in enumerate((q_ref, k_ref, v_ref)):
        p_ref[:, slot * width : (slot + 1) * width] = ref[0].T.reshape(group, width, count)

    @pl.when(pl.program_id(0) == pl.num_programs(0) - 1)
    def _():
        for shift in range(1, group):
            transfer(shift).wait()


def deliver(x, q, k, v, first, rows):
    group = x.shape[0]
    _, count, features = q.shape
    width = features // group
    spec = pl.BlockSpec((1, count, features), lambda r: (r + first, 0, 0))
    return pl.pallas_call(
        functools.partial(deliver_kernel, group),
        grid=(rows,),
        in_specs=[pl.BlockSpec(memory_space=pl.ANY)] + [spec] * 3,
        out_specs=(
            pl.BlockSpec(memory_space=pl.ANY),
            pl.BlockSpec((group, 3 * width, count), lambda r: (0, r, 0)),
        ),
        out_shape=(
            jax.ShapeDtypeStruct(x.shape, x.dtype),
            jax.ShapeDtypeStruct((group, rows * 3 * width, count), x.dtype),
        ),
        scratch_shapes=[
            pltpu.VMEM(x.shape[1:], x.dtype),
            pltpu.SemaphoreType.DMA,
            pltpu.SemaphoreType.DMA((group - 1,)),
            pltpu.SemaphoreType.DMA((group - 1,)),
        ],
        compiler_params=pltpu.CompilerParams(collective_id=0, has_side_effects=True),
    )(x, q, k, v)


def unpack_kernel(x_ref, *rest):
    o_ref = rest[-1]
    group, _, width, count = x_ref.shape
    o_ref[0] = x_ref[:, 0].reshape(group * width, count).T


def unpack(x, held, first, total):
    group, rows, width, count = x.shape
    args = (x,) if held is None else (x, held)
    in_specs = [pl.BlockSpec((group, 1, width, count), lambda r: (0, r, 0, 0))]
    if held is not None:
        in_specs.append(pl.BlockSpec(memory_space=pl.ANY))
    return pl.pallas_call(
        unpack_kernel,
        grid=(rows,),
        in_specs=in_specs,
        out_specs=pl.BlockSpec((1, count, group * width), lambda r: (r + first, 0, 0)),
        out_shape=jax.ShapeDtypeStruct((total, count, group * width), x.dtype),
        input_output_aliases={} if held is None else {1: 0},
        cost_estimate=pl.CostEstimate(
            flops=4 * rows * count * group * width, bytes_accessed=4 * rows * count * group * width, transcendentals=0
        ),
    )(*args)


def attend_kernel(heads, low_ref, high_ref, x_ref, dec_ref, enc_ref, o_ref, q_all, k_all, v_all):
    group, stacked, count = x_ref.shape
    width = stacked // 3
    length = group * count
    row = pl.program_id(0)
    span = min(SPAN, length)
    documents = lax.broadcasted_iota(jnp.int32, (DOCS, length), 0)
    dec_hot = jnp.where(documents == dec_ref[0], 1.0, 0.0).astype(jnp.bfloat16)
    enc_miss = jnp.where(documents == enc_ref[0], 0.0, MASKED).astype(jnp.bfloat16)
    for head in range(heads):
        place = pl.ds(head * HEAD_DIM, HEAD_DIM)
        for part in range(group):
            columns = pl.ds(part * count, count)
            q_all[:HEAD_DIM, columns] = x_ref[part, place]
            v_all[:, columns] = x_ref[part, pl.ds(2 * width + head * HEAD_DIM, HEAD_DIM)]
        q_all[HEAD_DIM:, :] = dec_hot
        for part in range(group):
            columns = slice(part * count, (part + 1) * count)
            both = jnp.concatenate([x_ref[part, pl.ds(width + head * HEAD_DIM, HEAD_DIM)], enc_miss[:, columns]], axis=0)
            k_all[columns, :] = both.T

        def one_span(block):
            at = pl.multiple_of(block * span, span)
            query = q_all[:, pl.ds(at, span)]
            low = low_ref[row, block]
            steps = high_ref[row, block]

            def step(index, held):
                peak, total, summed = held
                start = pl.multiple_of(low + index * span, 128)
                scores = jnp.dot(
                    k_all[pl.ds(start, span), :], query, preferred_element_type=jnp.float32
                )
                fresh = jnp.maximum(peak, jnp.max(scores, axis=0, keepdims=True))
                scale = jnp.exp(peak - fresh)
                expos = jnp.exp(scores - fresh)
                total = total * scale + jnp.sum(expos, axis=0, keepdims=True)
                summed = summed * scale + jnp.dot(
                    v_all[:, pl.ds(start, span)], expos.astype(jnp.bfloat16), preferred_element_type=jnp.float32
                )
                return fresh, total, summed

            init = (
                jnp.full((1, span), 4 * MASKED, jnp.float32),
                jnp.zeros((1, span), jnp.float32),
                jnp.zeros((HEAD_DIM, span), jnp.float32),
            )
            _, total, summed = lax.fori_loop(0, steps, step, init)
            return (summed / total).astype(jnp.bfloat16)

        if count == span:

            def each(block, carry):
                o_ref[block, 0, place] = one_span(block)
                return carry

            lax.fori_loop(0, length // span, each, 0)
        else:
            for block in range(length // span):
                result = one_span(block)
                for piece in range(0, span, count):
                    at = block * span + piece
                    width_here = min(count, span)
                    o_ref[at // count, 0, place, pl.ds(at % count, width_here)] = result[:, piece : piece + width_here]


def tables(dec_rows, enc_rows):
    rows, length = dec_rows.shape
    span = min(SPAN, length)
    docs = dec_rows.reshape(rows, length // span, span)
    before = jnp.sum(enc_rows[:, None, :] < docs[:, :, :1], axis=2, dtype=jnp.int32)
    upto = jnp.sum(enc_rows[:, None, :] <= docs[:, :, -1:], axis=2, dtype=jnp.int32)
    low = before // 128 * 128
    steps = (upto - low + span - 1) // span
    return jnp.minimum(low, length - steps * span), steps


def attend(x, width, low, steps, dec_rows, enc_rows):
    group, _, count = x.shape
    rows = low.shape[0]
    length = group * count
    heads = width // HEAD_DIM
    return pl.pallas_call(
        functools.partial(attend_kernel, heads),
        grid_spec=pltpu.PrefetchScalarGridSpec(
            num_scalar_prefetch=2,
            grid=(rows,),
            in_specs=[
                pl.BlockSpec((group, 3 * width, count), lambda r, *_: (0, r, 0)),
                pl.BlockSpec((1, 1, length), lambda r, *_: (r, 0, 0)),
                pl.BlockSpec((1, 1, length), lambda r, *_: (r, 0, 0)),
            ],
            out_specs=pl.BlockSpec((group, 1, width, count), lambda r, *_: (0, r, 0, 0)),
            scratch_shapes=[
                pltpu.VMEM((HEAD_DIM + DOCS, length), jnp.bfloat16),
                pltpu.VMEM((length, HEAD_DIM + DOCS), jnp.bfloat16),
                pltpu.VMEM((HEAD_DIM, length), jnp.bfloat16),
            ],
        ),
        out_shape=jax.ShapeDtypeStruct((group, rows, width, count), x.dtype),
        cost_estimate=pl.CostEstimate(
            flops=rows * heads * length * length * 128,
            bytes_accessed=8 * rows * width * length,
            transcendentals=rows * heads * length * length // 4,
        ),
    )(low, steps, x, dec_rows[:, None, :], enc_rows[:, None, :])


def local(queries, enc_keys, enc_values, dec_ids, enc_ids):
    group = lax.axis_size("seq")
    rows, count, features = queries.shape
    width = features // group
    early = max(1, rows * 5 // 8)
    cuts = [(0, early), (early, rows - early)] if rows > 1 else [(0, rows)]
    ids = jnp.concatenate([dec_ids, enc_ids], axis=0).astype(queries.dtype)

    def exchange(block):
        return lax.all_to_all(block, "seq", split_axis=0, concat_axis=0, tiled=True)

    packed = pack(queries, enc_keys, enc_values, ids, group, *cuts[0], True)
    if group > 1 and rows > 1:
        whole, packed = deliver(packed, queries, enc_keys, enc_values, *cuts[1])
        arrived = [whole, exchange(packed)]
    else:
        arrived = [exchange(packed)]
        arrived += [exchange(pack(queries, enc_keys, enc_values, ids, group, *cut, False)) for cut in cuts[1:]]
    spread = arrived[0][:, early * 3 * width :].astype(jnp.int32)
    whole_rows = spread.transpose(1, 0, 2).reshape(2 * rows, group * count)
    dec_rows, enc_rows = whole_rows[:rows], whole_rows[rows:]
    known = (*tables(dec_rows, enc_rows), dec_rows, enc_rows)
    out = None
    for (first, size), block in zip(cuts, arrived):
        attended = attend(block, width, *[table[first : first + size] for table in known])
        out = unpack(exchange(attended), out, first, rows)
    return out


def solution(mesh):
    in_specs = (
        P("dp", "seq", None),
        P("dp", "seq", None),
        P("dp", "seq", None),
        P("dp", "seq"),
        P("dp", "seq"),
    )
    out_specs = P("dp", "seq", None)
    return jax.shard_map(local, mesh=mesh, in_specs=in_specs, out_specs=out_specs, check_vma=False)
```

profile of v0, /device:TPU:0, one launch (start us, length us, event | category | flops | bytes accessed | tf_op | source)
XLA Modules:
  0.0 224.7 jit_solution(6140431782022257395)
XLA Ops:
  0.0 0.7 convert.7
  0.7 0.7 convert.8
  1.4 0.6 pad_maximum_fusion.ids_ref
  2.0 6.2 %shard_map.55.x_ref = bf16[8,976,256]{2,1,0:T(8,128)(2,1)} custom-call(bf16[8,256,512]{2,1,0:T(8,128)(2,1)} %q_ref.3, bf16[8,256,512]{2,1,0:T(8,128)(2,1)} %k_ref.3, bf16[8,256,512]{2,1,0:T(8,128)(2,1)} %v_ref.3, bf16[16,256]{1,0:T(8,128)(2,1)} %pad_maximum_fusion.ids_ref), custom_call_target="tpu_custom_call" | custom-call | flops 2621440 | bytes 7864320 | tf_op jit(solution)/shard_map/pallas_call | solution.py:36
  8.2 75.7 %shard_map.56 = (bf16[8,976,256]{2,1,0:T(8,128)(2,1)}, bf16[8,576,256]{2,1,0:T(8,128)(2,1)}) custom-call(bf16[8,976,256]{2,1,0:T(8,128)(2,1)} %shard_map.55.x_ref, bf16[8,256,512]{2,1,0:T(8,128)(2,1)} %q_ref.3, bf16[8,256,512]{2,1,0:T(8,128)(2,1)} %k_ref.3, bf16[8,256,512]{2,1,0:T(8,128)(2,1)} %v_ref.3), custom_call_target="tpu_custom_call" | custom-call | tf_op jit(solution)/shard_map/pallas_call | solution.py:95
  83.9 22.2 %all-to-all-start = ((bf16[8,576,256]{2,1,0:T(8,128)(2,1)}), bf16[8,576,256]{2,1,0:T(8,128)(2,1)S(1)}, u32[]{:S(2)}, u32[]{:S(2)}) async-start(bf16[8,576,256]{2,1,0:T(8,128)(2,1)} %get-tuple-element.8), calls=%async_computation | async-start | bytes 4718592 | tf_op jit(solution)/shard_map/all_to_all | solution.py:259
  106.1 0.9 convert_bitcast_fusion
  107.4 0.7 broadcast_in_dim.17.enc_ref
  108.0 0.7 broadcast_in_dim.16.dec_ref
  109.1 0.6 subtract_minimum_fusion
  109.8 36.0 %shard_map.58 = bf16[8,5,64,256]{3,2,1,0:T(8,128)(2,1)} custom-call(s32[5,8]{1,0:T(8,128)} %bitcast.11, s32[5,8]{1,0:T(8,128)} %bitcast.10, bf16[8,976,256]{2,1,0:T(8,128)(2,1)} %get-tuple-element.7.x_ref, s32[5,1,2048]{2,1,0:T(1,128)} %broadcast_in_dim.16.dec_ref, s32[5,1,2048]{2,1,0:T(1,128)} %broadcast_in_dim.17.enc_ref), custom_call_target="tpu_custom_call" | custom-call | flops 2684354560 | bytes 5242880 | tf_op jit(solution)/shard_map/pallas_call | solution.py:224
  145.8 14.4 %all-to-all-done.x_ref = bf16[8,576,256]{2,1,0:T(8,128)(2,1)S(1)} async-done(((bf16[8,576,256]{2,1,0:T(8,128)(2,1)}), bf16[8,576,256]{2,1,0:T(8,128)(2,1)S(1)}, u32[]{:S(2)}, u32[]{:S(2)}) %all-to-all-start) | async-done | bytes 2359328 | tf_op jit(solution)/shard_map/all_to_all | solution.py:259
  160.1 1.4 copy-done.2
  161.6 3.6 %all-to-all-start.2 = ((bf16[8,5,64,256]{3,2,1,0:T(8,128)(2,1)}), bf16[8,5,64,256]{3,2,1,0:T(8,128)(2,1)S(1)}, u32[]{:S(2)}, u32[]{:S(2)}) async-start(bf16[8,5,64,256]{3,2,1,0:T(8,128)(2,1)} %shard_map.58), calls=%async_computation.2 | async-start | bytes 2621440 | tf_op jit(solution)/shard_map/all_to_all | solution.py:259
  165.2 0.6 slice.53.low_ref
  166.4 0.6 broadcast_in_dim.15.enc_ref
  167.1 0.6 broadcast_in_dim.14.dec_ref
  167.7 25.2 %shard_map.57 = bf16[8,3,64,256]{3,2,1,0:T(8,128)(2,1)} custom-call(s32[3,8]{1,0:T(4,128)} %slice.53.low_ref, s32[3,8]{1,0:T(4,128)} %slice.54.high_ref, bf16[8,576,256]{2,1,0:T(8,128)(2,1)} %copy-done.2, s32[3,1,2048]{2,1,0:T(1,128)} %broadcast_in_dim.14.dec_ref, s32[3,1,2048]{2,1,0:T(1,128)} %broadcast_in_dim.15.enc_ref), custom_call_target="tpu_custom_call" | custom-call | flops 1610612736 | bytes 3145728 | tf_op jit(solution)/shard_map/pallas_call | solution.py:224
  192.9 3.9 %all-to-all-done.2.x_ref = bf16[8,5,64,256]{3,2,1,0:T(8,128)(2,1)S(1)} async-done(((bf16[8,5,64,256]{3,2,1,0:T(8,128)(2,1)}), bf16[8,5,64,256]{3,2,1,0:T(8,128)(2,1)S(1)}, u32[]{:S(2)}, u32[]{:S(2)}) %all-to-all-start.2) | async-done | bytes 1310752 | tf_op jit(solution)/shard_map/all_to_all | solution.py:259
  196.8 3.6 %all-to-all-start.1 = ((bf16[8,3,64,256]{3,2,1,0:T(8,128)(2,1)}), bf16[8,3,64,256]{3,2,1,0:T(8,128)(2,1)S(1)}, u32[]{:S(2)}, u32[]{:S(2)}) async-start(bf16[8,3,64,256]{3,2,1,0:T(8,128)(2,1)} %shard_map.57), calls=%async_computation.1 | async-start | bytes 1572864 | tf_op jit(solution)/shard_map/all_to_all | solution.py:259
  200.4 4.2 %shard_map.59.rest_0_ = bf16[8,256,512]{2,1,0:T(8,128)(2,1)} custom-call(bf16[8,5,64,256]{3,2,1,0:T(8,128)(2,1)} %copy-done), custom_call_target="tpu_custom_call" | custom-call | flops 2621440 | bytes 2621440 | tf_op jit(solution)/shard_map/pallas_call | solution.py:129
  204.6 16.1 %all-to-all-done.1.x_ref = bf16[8,3,64,256]{3,2,1,0:T(8,128)(2,1)S(1)} async-done(((bf16[8,3,64,256]{3,2,1,0:T(8,128)(2,1)}), bf16[8,3,64,256]{3,2,1,0:T(8,128)(2,1)S(1)}, u32[]{:S(2)}, u32[]{:S(2)}) %all-to-all-start.1) | async-done | bytes 786464 | tf_op jit(solution)/shard_map/all_to_all | solution.py:259
  220.8 0.9 copy-done.1
  221.7 3.0 %shard_map.60 = bf16[8,256,512]{2,1,0:T(8,128)(2,1)} custom-call(bf16[8,3,64,256]{3,2,1,0:T(8,128)(2,1)} %copy-done.1, bf16[8,256,512]{2,1,0:T(8,128)(2,1)} %shard_map.59.rest_0_), custom_call_target="tpu_custom_call", output_to_operand_aliasing={{}: (1, {})} | custom-call | flops 1572864 | bytes 1572864 | tf_op jit(solution)/shard_map/pallas_call | solution.py:129
  (20 shorter events, 1.5 us)
Async XLA Ops:
  83.9 76.2 %all-to-all-start = ((bf16[8,576,256]{2,1,0:T(8,128)(2,1)}), bf16[8,576,256]{2,1,0:T(8,128)(2,1)S(1)}, u32[]{:S(2)}, u32[]{:S(2)}) async-start(bf16[8,576,256]{2,1,0:T(8,128)(2,1)} %get-tuple-element.8), calls=%async_computation | async-start | bytes 4718592 | tf_op jit(solution)/shard_map/all_to_all | solution.py:259
  145.8 19.4 %copy-start.4 = (s32[8,8]{1,0:T(8,128)S(1)}, s32[8,8]{1,0:T(8,128)}, u32[]{:S(2)}) copy-start(s32[8,8]{1,0:T(8,128)} %get-tuple-element.11) | copy-start | bytes 772
  145.8 20.0 %copy-start.3 = (s32[8,8]{1,0:T(8,128)S(1)}, s32[8,8]{1,0:T(8,128)}, u32[]{:S(2)}) copy-start(s32[8,8]{1,0:T(8,128)} %get-tuple-element.12) | copy-start | bytes 772
  160.1 1.4 copy-start.2
  161.6 35.2 %all-to-all-start.2 = ((bf16[8,5,64,256]{3,2,1,0:T(8,128)(2,1)}), bf16[8,5,64,256]{3,2,1,0:T(8,128)(2,1)S(1)}, u32[]{:S(2)}, u32[]{:S(2)}) async-start(bf16[8,5,64,256]{3,2,1,0:T(8,128)(2,1)} %shard_map.58), calls=%async_computation.2 | async-start | bytes 2621440 | tf_op jit(solution)/shard_map/all_to_all | solution.py:259
  196.8 3.6 %copy-start = (bf16[8,5,64,256]{3,2,1,0:T(8,128)(2,1)}, bf16[8,5,64,256]{3,2,1,0:T(8,128)(2,1)S(1)}, u32[]{:S(2)}) copy-start(bf16[8,5,64,256]{3,2,1,0:T(8,128)(2,1)S(1)} %all-to-all-done.2.x_ref) | copy-start | bytes 3932164
  196.8 24.0 %all-to-all-start.1 = ((bf16[8,3,64,256]{3,2,1,0:T(8,128)(2,1)}), bf16[8,3,64,256]{3,2,1,0:T(8,128)(2,1)S(1)}, u32[]{:S(2)}, u32[]{:S(2)}) async-start(bf16[8,3,64,256]{3,2,1,0:T(8,128)(2,1)} %shard_map.57), calls=%async_computation.1 | async-start | bytes 1572864 | tf_op jit(solution)/shard_map/all_to_all | solution.py:259
  220.8 0.9 copy-start.1
where the time goes:
time: 226 us; the launch traced here: 225 us
  Pallas kernels  150 us (66%)
  waiting for transfers between devices  34.4 us (15%)
  starting transfers between devices  29.5 us (13%)
  local copies, waits for them, and re-layouts  6.47 us (3%)
  other arithmetic  3.91 us (2%)
    pallas_call x1, Pallas kernels, deliver(): pl.pallas_call(functools.partial(deliver_kernel, group), grid=(rows,), in...  75.7 us
    pallas_call x2, Pallas kernels, attend(): pl.pallas_call(functools.partial(attend_kernel, heads), grid_spec=pltpu.P...  61.2 us
    all_to_all x3, waiting for transfers between devices, exchange(): return lax.all_to_all(block, 'seq', split_axis=0, concat_axis=0, tiled=True)  34.4 us
    all_to_all x3, starting transfers between devices, exchange(): return lax.all_to_all(block, 'seq', split_axis=0, concat_axis=0, tiled=True)  29.5 us
    pallas_call x2, Pallas kernels, unpack(): pl.pallas_call(unpack_kernel, grid=(rows,), in_specs=in_specs, out_specs=...  7.27 us
    pallas_call x1, Pallas kernels, pack(): pl.pallas_call(functools.partial(pack_kernel, rows), grid=(rows + 1 if wi...  6.22 us
  transfers between devices with their start and end apart: 3, of which 3 were waited for; matrix products, arithmetic and copies ran while one was open for 3% of the time, Pallas kernels for 29%

commit v1 on v0

v1 whole, which is shorter than its diff:
```python
import functools

import jax
import jax.numpy as jnp
from jax import lax
from jax.experimental import pallas as pl
from jax.experimental.pallas import tpu as pltpu
from jax.sharding import PartitionSpec as P

HEAD_DIM = 64
DOCS = 16
LANES = 128
SPAN = 256
PIECE = 32
PAD = 128
MASKED = -8192.0
SHARE = 7


def peer(me, shift, half):
    base = me // half * half
    return base + lax.rem(me - base + shift, half)


def greet(me, others):
    barrier = pltpu.get_barrier_semaphore()
    for target in others:
        pl.semaphore_signal(barrier, inc=1, device_id={"seq": target}, device_id_type=pl.DeviceIdType.MESH)
    pl.semaphore_wait(barrier, len(others))


def remote(src, dst, send_sem, recv_sem, target):
    return pltpu.make_async_remote_copy(
        src_ref=src,
        dst_ref=dst,
        send_sem=send_sem,
        recv_sem=recv_sem,
        device_id={"seq": target},
        device_id_type=pl.DeviceIdType.MESH,
    )


def gather_kernel(
    group, k_ref, dec_ref, enc_ref, v_ref, q_ref, k_out, dec_out, enc_out, v_out, q_out, held, ids_held, own_sem, ids_sem, send_sem, recv_sem, ids_send, ids_recv
):
    me = lax.axis_index("seq")
    half = group // 2
    width = k_out.shape[3]
    place = lax.rem(me, half)

    def columns(target):
        return k_ref.at[:, :, pl.ds(pl.multiple_of(lax.rem(target, half) * width, LANES), width)]

    def keys(shift):
        target = peer(me, shift, half)
        return remote(columns(target), k_out.at[place], send_sem.at[shift - 1], recv_sem.at[shift - 1], target)

    def ids(shift, slot, src, dst):
        at = slot * (group - 1) + shift - 1
        return remote(src, dst.at[me], ids_send.at[at], ids_recv.at[at], lax.rem(me + shift, group))

    both = ((0, dec_ref, dec_out), (1, enc_ref, enc_out))

    @pl.when(pl.program_id(0) == 0)
    def _():
        greet(me, [lax.rem(me + shift, group) for shift in range(1, group)])
        for shift in range(1, group):
            for slot, src, dst in both:
                ids(shift, slot, src, dst).start()
        for shift in range(half - 1, 0, -1):
            keys(shift).start()
        own = [pltpu.make_async_copy(columns(me), held, own_sem)]
        own += [pltpu.make_async_copy(src, ids_held.at[slot], ids_sem.at[slot]) for slot, src, _ in both]
        for copy in own:
            copy.start()
        for copy in own:
            copy.wait()
        own = [pltpu.make_async_copy(held, k_out.at[place], own_sem)]
        own += [pltpu.make_async_copy(ids_held.at[slot], dst.at[me], ids_sem.at[slot]) for slot, _, dst in both]
        for copy in own:
            copy.start()
        for copy in own:
            copy.wait()

    for src, dst in ((v_ref, v_out), (q_ref, q_out)):
        for target in range(half):
            dst[target, 0] = src[0, :, target * width : (target + 1) * width]

    @pl.when(pl.program_id(0) == pl.num_programs(0) - 1)
    def _():
        for shift in range(1, group):
            for slot, src, dst in both:
                ids(shift, slot, src, dst).wait()
        for shift in range(1, half):
            keys(shift).wait()


def gather(q, k, v, dec_ids, enc_ids, group):
    rows, count, features = k.shape
    half = group // 2
    width = features // half
    anywhere = pl.BlockSpec(memory_space=pl.ANY)
    block = pl.BlockSpec((1, count, features), lambda r: (r, 0, 0))
    packed = pl.BlockSpec((half, 1, count, width), lambda r: (0, r, 0, 0))
    spread = jax.ShapeDtypeStruct((half, rows, count, width), k.dtype)
    every = jax.ShapeDtypeStruct((group, rows, count), dec_ids.dtype)
    dma = pltpu.SemaphoreType.DMA
    return pl.pallas_call(
        functools.partial(gather_kernel, group),
        grid=(rows,),
        in_specs=[anywhere] * 3 + [block] * 2,
        out_specs=[anywhere] * 3 + [packed] * 2,
        out_shape=[spread, every, every, spread, spread],
        scratch_shapes=[
            pltpu.VMEM((rows, count, width), k.dtype),
            pltpu.VMEM((2, rows, count), dec_ids.dtype),
            dma,
            dma((2,)),
            dma((half - 1,)),
            dma((half - 1,)),
            dma((2 * (group - 1),)),
            dma((2 * (group - 1),)),
        ],
        compiler_params=pltpu.CompilerParams(collective_id=0, has_side_effects=True),
    )(k, dec_ids, enc_ids, v, q)


def give_back_kernel(group, o_ref, out_ref, held, own_sem, send_sem, recv_sem):
    me = lax.axis_index("seq")
    half = group // 2
    width = o_ref.shape[3]
    place = lax.rem(me, half)
    columns = out_ref.at[:, :, pl.ds(pl.multiple_of(place * width, LANES), width)]

    def transfer(shift):
        target = peer(me, shift, half)
        return remote(o_ref.at[lax.rem(target, half)], columns, send_sem.at[shift - 1], recv_sem.at[shift - 1], target)

    greet(me, [peer(me, shift, half) for shift in range(1, half)])
    for shift in range(half - 1, 0, -1):
        transfer(shift).start()
    own = pltpu.make_async_copy(o_ref.at[place], held, own_sem)
    own.start()
    own.wait()
    own = pltpu.make_async_copy(held, columns, own_sem)
    own.start()
    own.wait()
    for shift in range(1, half):
        transfer(shift).wait()


def give_back(o, group):
    half, rows, count, width = o.shape
    return pl.pallas_call(
        functools.partial(give_back_kernel, group),
        in_specs=[pl.BlockSpec(memory_space=pl.ANY)],
        out_specs=pl.BlockSpec(memory_space=pl.ANY),
        out_shape=jax.ShapeDtypeStruct((rows, count, half * width), o.dtype),
        scratch_shapes=[
            pltpu.VMEM((rows, count, width), o.dtype),
            pltpu.SemaphoreType.DMA,
            pltpu.SemaphoreType.DMA((half - 1,)),
            pltpu.SemaphoreType.DMA((half - 1,)),
        ],
        compiler_params=pltpu.CompilerParams(collective_id=1, has_side_effects=True),
    )(o)


def pack_kernel(table_ref, x_ref, o_ref):
    _, rows, count, width = x_ref.shape
    room = o_ref.shape[0]
    o_ref[...] = jnp.zeros(o_ref.shape, o_ref.dtype)
    for row in range(rows):
        offset, start, amount = table_ref[0, row], table_ref[1, row], table_ref[2, row]
        pieces = jnp.maximum(jnp.minimum(amount, room - PAD - offset), 0) // PIECE

        def move(index, carry):
            at = start + index * PIECE
            into = pl.multiple_of(offset + index * PIECE, PIECE)
            o_ref[pl.ds(into, PIECE), :] = x_ref[at // count, row, pl.ds(pl.multiple_of(at % count, PIECE), PIECE), :]
            return carry

        lax.fori_loop(0, pieces, move, 0)


def pack(table, x, room):
    half, rows, count, width = x.shape
    return pl.pallas_call(
        pack_kernel,
        grid_spec=pltpu.PrefetchScalarGridSpec(
            num_scalar_prefetch=1,
            grid=(1,),
            in_specs=[pl.BlockSpec(x.shape, lambda r, *_: (0, 0, 0, 0))],
            out_specs=pl.BlockSpec((room, width), lambda r, *_: (0, 0)),
        ),
        out_shape=jax.ShapeDtypeStruct((room, width), x.dtype),
        cost_estimate=pl.CostEstimate(flops=2000000, bytes_accessed=4 * x.size, transcendentals=0),
    )(table, x)


def attend_kernel(mode, table_ref, q_ref, k_ref, v_ref, dec_ref, enc_ref, *rest):
    if mode:
        more_k, more_v, before_ref, o_ref, keys, values = rest
    else:
        o_ref, keys, values = rest
    half, _, count, width = q_ref.shape
    length = half * count
    span = max(SPAN, count)
    slabs = span // count
    blocks = length // span
    heads = width // HEAD_DIM
    row = pl.program_id(0)
    first = table_ref[row, 3 * blocks + 1] * length

    def entry(kind, block):
        return table_ref[row, kind * blocks + block]

    wanted = [entry(2, block) == mode for block in range(blocks)]
    begin, end = jnp.int32(2 * length), jnp.int32(0)
    for block in range(blocks):
        low = entry(0, block)
        begin = jnp.where(wanted[block], jnp.minimum(begin, low), begin)
        end = jnp.where(wanted[block], jnp.maximum(end, low + entry(1, block) * span), end)

    def place(at, key, value):
        ids = enc_ref[0, :, pl.ds(at, LANES)]
        documents = lax.broadcasted_iota(jnp.int32, (LANES, LANES), 0)
        miss = jnp.where((documents == ids) | (documents >= DOCS), 0.0, MASKED).astype(jnp.bfloat16)
        keys[pl.ds(at, LANES), :width] = key
        keys[pl.ds(at, LANES), width:] = miss.T
        values[:, pl.ds(at, LANES)] = value.T

    chunk = min(LANES, count)

    def prepare(index, carry):
        at = pl.multiple_of(index * LANES, LANES)
        local = at - first
        mine = (local >= 0) & (local < length)

        @pl.when(mine)
        def _():
            if count >= LANES:
                slab = local // count
                inside = pl.ds(pl.multiple_of(local % count, LANES), LANES)
                place(at, k_ref[slab, 0, inside, :], v_ref[slab, 0, inside, :])
            else:
                slab = pl.ds(local // count, LANES // count)
                place(at, k_ref[slab, 0].reshape(LANES, width), v_ref[slab, 0].reshape(LANES, width))

        @pl.when(jnp.logical_not(mine))
        def _():
            if mode:
                room = more_k.shape[0]
                into = jnp.clip(table_ref[row, 3 * blocks] + at, 0, room - LANES)
                into = pl.ds(pl.multiple_of(into, PIECE), LANES)
                place(at, more_k[into, :], more_v[into, :])
            else:
                nothing = jnp.zeros((LANES, width), jnp.bfloat16)
                place(at, nothing, nothing)

        return carry

    lax.fori_loop(begin // LANES, end // LANES, prepare, 0)

    for block in range(blocks):
        slab = pl.ds(block * slabs, slabs)

        @pl.when(wanted[block])
        def _():
            query = q_ref[slab, 0].reshape(span, width)
            ids = dec_ref[0, :, pl.ds(block * span, span)]
            documents = lax.broadcasted_iota(jnp.int32, (LANES, span), 0)
            hot = jnp.where(documents == ids, 1.0, 0.0).astype(jnp.bfloat16).T
            owner = lax.broadcasted_iota(jnp.int32, (span, width), 1) // HEAD_DIM
            sides = [
                jnp.concatenate([jnp.where(owner == head, query, jnp.zeros_like(query)), hot], axis=1)
                for head in range(heads)
            ]
            low = entry(0, block)

            def step(index, held):
                start = pl.multiple_of(low + index * span, LANES)
                key = keys[pl.ds(start, span), :]
                result = []
                for head in range(heads):
                    peak, total, summed = held[head]
                    scores = lax.dot_general(
                        key, sides[head], (((1,), (1,)), ((), ())), preferred_element_type=jnp.float32
                    )
                    fresh = jnp.maximum(peak, jnp.max(scores, axis=0, keepdims=True))
                    scale = jnp.exp(peak - fresh)
                    expos = jnp.exp(scores - fresh)
                    total = total * scale + jnp.sum(expos, axis=0, keepdims=True)
                    value = values[head * HEAD_DIM : (head + 1) * HEAD_DIM, pl.ds(start, span)]
                    summed = summed * scale + jnp.dot(
                        value, expos.astype(jnp.bfloat16), preferred_element_type=jnp.float32
                    )
                    result.append((fresh, total, summed))
                return tuple(result)

            init = (
                jnp.full((1, span), 4 * MASKED, jnp.float32),
                jnp.zeros((1, span), jnp.float32),
                jnp.zeros((HEAD_DIM, span), jnp.float32),
            )
            done = lax.fori_loop(0, entry(1, block), step, (init,) * heads)
            whole = jnp.concatenate([summed / total for _, total, summed in done], axis=0)
            o_ref[slab, 0] = whole.T.astype(jnp.bfloat16).reshape(slabs, count, width)

        if mode:

            @pl.when(jnp.logical_not(wanted[block]))
            def _():
                o_ref[slab, 0] = before_ref[slab, 0]


def attend(mode, table, q, k, v, dec_rows, enc_rows, *more):
    half, rows, count, width = q.shape
    length = half * count
    row_block = pl.BlockSpec((half, 1, count, width), lambda r, *_: (0, r, 0, 0))
    specs = [row_block] * 3
    specs += [pl.BlockSpec((1, 1, length), lambda r, *_: (r, 0, 0))]
    specs += [pl.BlockSpec((1, 1, 2 * length), lambda r, *_: (r, 0, 0))]
    if mode:
        specs += [pl.BlockSpec(more[0].shape, lambda r, *_: (0, 0))] * 2 + [row_block]
    return pl.pallas_call(
        functools.partial(attend_kernel, mode),
        grid_spec=pltpu.PrefetchScalarGridSpec(
            num_scalar_prefetch=1,
            grid=(rows,),
            in_specs=specs,
            out_specs=row_block,
            scratch_shapes=[
                pltpu.VMEM((2 * length, width + LANES), jnp.bfloat16),
                pltpu.VMEM((width, 2 * length), jnp.bfloat16),
            ],
        ),
        out_shape=jax.ShapeDtypeStruct(q.shape, q.dtype),
        cost_estimate=pl.CostEstimate(
            flops=rows * width // HEAD_DIM * length * length * 128,
            bytes_accessed=8 * rows * width * length,
            transcendentals=rows * length * length // 4,
        ),
    )(table, q, k, v, dec_rows, enc_rows, *more)


def tables(dec_rows, enc_rows, side):
    rows, whole = dec_rows.shape
    length = whole // 2
    mine = lax.dynamic_slice(dec_rows, (0, side * length), (rows, length))
    blocks = length // SPAN
    docs = mine.reshape(rows, blocks, SPAN)
    starts = jnp.concatenate([docs[:, :, 0], dec_rows[:, length : length + 1]], axis=1)
    ends = jnp.concatenate([docs[:, :, -1], dec_rows[:, length - 1 : length]], axis=1)
    before = jnp.sum(enc_rows[:, None, :] < starts[:, :, None], axis=2, dtype=jnp.int32)
    upto = jnp.sum(enc_rows[:, None, :] <= ends[:, :, None], axis=2, dtype=jnp.int32)
    up = jnp.maximum(length - before[:, blocks], 0)
    down = jnp.maximum(upto[:, blocks] - length, 0)
    up, down = (-(-amount // PIECE) * PIECE for amount in (up, down))
    before, upto = before[:, :blocks], upto[:, :blocks]
    crosses = jnp.where(side == 0, upto > length, before < length).astype(jnp.int32)
    low = before // LANES * LANES
    steps = (upto - low + SPAN - 1) // SPAN
    low = jnp.minimum(low, whole - steps * SPAN)
    sent, got = jnp.where(side == 0, up, down), jnp.where(side == 0, down, up)
    offset_of = [PAD + jnp.cumsum(amount) - amount for amount in (sent, got)]
    first = jnp.where(side == 0, length - sent, 0)
    send = jnp.stack([offset_of[0], first, sent])
    base = offset_of[1] - jnp.where(side == 0, length, length - got)
    known = jnp.concatenate([low, steps, crosses, base[:, None], jnp.full((rows, 1), side, jnp.int32)], axis=1)
    return send, known, mine, jnp.maximum(jnp.sum(up), jnp.sum(down))


def local(queries, enc_keys, enc_values, dec_ids, enc_ids):
    group = lax.axis_size("seq")
    half = group // 2
    rows, count, features = queries.shape
    length = half * count
    side = lax.axis_index("seq") // half
    k, dec_all, enc_all, v_packed, q_packed = gather(queries, enc_keys, enc_values, dec_ids, enc_ids, group)
    sides = [list(range(half)), list(range(half, group))]

    def exchange(block):
        return lax.all_to_all(block, "seq", split_axis=0, concat_axis=0, axis_index_groups=sides, tiled=True)

    def cross(block):
        return lax.ppermute(block, "seq", [(i, (i + half) % group) for i in range(group)])

    v = exchange(v_packed)
    q = exchange(q_packed)
    dec_rows, enc_rows = (x.transpose(1, 0, 2).reshape(rows, 2 * length) for x in (dec_all, enc_all))
    send, known, mine, most = tables(dec_rows, enc_rows, side)
    most = lax.pmax(most, "dp")
    room = rows * length * SHARE // 16 // 128 * 128 + 2 * PAD
    full = rows * length + 2 * PAD
    more_k = cross(pack(send, k, room))
    more_v = cross(pack(send, v, room))
    mine, enc_rows = mine[:, None, :], enc_rows[:, None, :]
    early = attend(0, known, q, k, v, mine, enc_rows)

    def enough(more_k, more_v):
        return attend(1, known, q, k, v, mine, enc_rows, more_k, more_v, early)

    def overflow(more_k, more_v):
        more_k, more_v = cross(pack(send, k, full)), cross(pack(send, v, full))
        return attend(1, known, q, k, v, mine, enc_rows, more_k, more_v, early)

    return give_back(lax.cond(most <= room - 2 * PAD, enough, overflow, more_k, more_v), group)


def solution(mesh):
    in_specs = (
        P("dp", "seq", None),
        P("dp", "seq", None),
        P("dp", "seq", None),
        P("dp", "seq"),
        P("dp", "seq"),
    )
    out_specs = P("dp", "seq", None)
    return jax.shard_map(local, mesh=mesh, in_specs=in_specs, out_specs=out_specs, check_vma=False)
```

time: 226 us -> 226 us (level)
  the two profiles are of different devices: /device:TPU:0 before, /device:TPU:16 now
where the time goes in v1:
time: 226 us; the launch traced here: 224 us
  Pallas kernels  145 us (64%)
  blocking collectives  33.4 us (15%)
  waiting for transfers between devices  28.2 us (12%)
  starting transfers between devices  8.56 us (4%)
  local copies, waits for them, and re-layouts  4.13 us (2%)
    pallas_call x2, Pallas kernels, attend(): pl.pallas_call(functools.partial(attend_kernel, mode), grid_spec=pltpu.Pr...  80.8 us
    pallas_call x1, Pallas kernels, gather(): pl.pallas_call(functools.partial(gather_kernel, group), grid=(rows,), in_...  30.9 us
    all_to_all x1, blocking collectives, exchange(): lax.all_to_all(block, 'seq', split_axis=0, concat_axis=0, axis_index_grou...  28.4 us
    pallas_call x1, Pallas kernels, give_back(): pl.pallas_call(functools.partial(give_back_kernel, group), in_specs=[pl.B...  27.8 us
    all_to_all x1, waiting for transfers between devices, exchange(): lax.all_to_all(block, 'seq', split_axis=0, concat_axis=0, axis_index_grou...  17.3 us
    ppermute x2, waiting for transfers between devices, cross(): lax.ppermute(block, 'seq', [(i, (i + half) % group) for i in range(group)])  10.9 us
    pallas_call x2, Pallas kernels, pack(): pl.pallas_call(pack_kernel, grid_spec=pltpu.PrefetchScalarGridSpec(num_sc...  5.67 us
    pmax x1, blocking collectives, local(): most = lax.pmax(most, 'dp')  5.06 us
  transfers between devices with their start and end apart: 3, of which 2 were waited for; matrix products, arithmetic and copies ran while one was open for 1% of the time, Pallas kernels for 22%

profile of v1, /device:TPU:16, one launch (start us, length us, event | category | flops | bytes accessed | tf_op | source)
XLA Modules:
  0.0 223.7 jit_solution(9629709378825449619)
XLA Ops:
  0.0 30.9 %shard_map.55 = (bf16[4,8,256,128]{3,2,1,0:T(8,128)(2,1)}, s32[8,8,256]{2,1,0:T(8,128)}, s32[8,8,256]{2,1,0:T(8,128)}, bf16[4,8,256,128]{3,2,1,0:T(8,128)(2,1)}, bf16[4,8,256,128]{3,2,1,0:T(8,128)(2,1)}) custom-call(bf16[8,256,512]{2,1,0:T(8,128)(2,1)} %k_ref.1, s32[8,256]{1,0:T(8,128)} %dec_ref.1, s32[8,256]{1,0:T(8,128)} %enc_ref.1, ...), custom_call_target="tpu_custom_call" | custom-call | tf_op jit(solution)/shard_map/pallas_call | solution.py:108
  30.9 28.4 %all_to_all.10.v_ref.x_ref = bf16[4,8,256,128]{3,2,1,0:T(8,128)(2,1)S(1)} all-to-all(bf16[4,8,256,128]{3,2,1,0:T(8,128)(2,1)} %get-tuple-element.67), channel_id=1, replica_groups={{0,1,2,3},{4,5,6,7},{8,9,10,11},{12,13,14,15},{16,17,18,19},{20,21,22,2..., dimensions={0} | all-to-all | bytes 4194304 | tf_op jit(solution)/shard_map/all_to_all | solution.py:384
  59.3 4.6 %all-to-all-start.1 = ((bf16[4,8,256,128]{3,2,1,0:T(8,128)(2,1)}), bf16[4,8,256,128]{3,2,1,0:T(8,128)(2,1)}, u32[]{:S(2)}, u32[]{:S(2)}) async-start(bf16[4,8,256,128]{3,2,1,0:T(8,128)(2,1)} %get-tuple-element.68), calls=%async_computation.1 | async-start | bytes 4194304 | tf_op jit(solution)/shard_map/all_to_all | solution.py:384
  64.2 0.1 copy.17
  64.3 0.1 copy.20
  64.4 0.3 convert_reduce_fusion
  64.8 0.1 copy.26
  65.0 0.2 select_reduce_fusion
  65.1 0.2 reduce-window_clone.1
  65.4 3.6 %shard_map.57 = bf16[3840,128]{1,0:T(8,128)(2,1)} custom-call(s32[3,8]{1,0:T(4,128)S(1)} %pad_add_fusion.2.table_ref, bf16[4,8,256,128]{3,2,1,0:T(8,128)(2,1)} %get-tuple-element.66.k_ref.x_ref), custom_call_target="tpu_custom_call" | custom-call | flops 2000000 | bytes 4194304 | tf_op jit(solution)/shard_map/pallas_call | solution.py:188
  69.0 3.4 %collective-permute-start.2 = (bf16[3840,128]{1,0:T(8,128)(2,1)}, bf16[3840,128]{1,0:T(8,128)(2,1)S(1)}, u32[]{:S(2)}, u32[]{:S(2)}) collective-permute-start(bf16[3840,128]{1,0:T(8,128)(2,1)} %shard_map.57), channel_id=1, source_target_pairs={{0,4},{1,5},{2,6},{3,7},{4,0},{5,1},{6,2},{7,3},{8,12},{9,13},{10,... | collective-permute-start | bytes 2949128 | tf_op jit(solution)/shard_map/ppermute | solution.py:387
  72.4 0.7 multiply_reduce_fusion
  73.1 2.0 shard_map.58
  75.1 0.6 collective-permute-start.3
  75.7 0.6 multiply_reduce_fusion.1
  77.7 5.1 %pmax.7 = s32[]{:T(128)} all-reduce(s32[]{:T(128)S(6)} %max.63), channel_id=1, replica_groups=mesh['dp'=4,'seq'=8] {'dp'}, use_global_device_ids=true, to_apply=%region_4.5 | all-reduce | flops 1 | bytes 8 | tf_op jit(solution)/shard_map/pmax | solution.py:393
  82.8 0.1 copy.28
  83.8 17.3 %all-to-all-done.1.q_ref = bf16[4,8,256,128]{3,2,1,0:T(8,128)(2,1)} async-done(((bf16[4,8,256,128]{3,2,1,0:T(8,128)(2,1)}), bf16[4,8,256,128]{3,2,1,0:T(8,128)(2,1)}, u32[]{:S(2)}, u32[]{:S(2)}) %all-to-all-start.1) | async-done | bytes 2097184 | tf_op jit(solution)/shard_map/all_to_all | solution.py:384
  101.1 43.5 %shard_map.56 = bf16[4,8,256,128]{3,2,1,0:T(8,128)(2,1)} custom-call(s32[8,14]{1,0:T(8,128)S(1)} %concatenate.11.table_ref, bf16[4,8,256,128]{3,2,1,0:T(8,128)(2,1)} %all-to-all-done.1.q_ref, bf16[4,8,256,128]{3,2,1,0:T(8,128)(2,1)} %get-tuple-element.66.k_ref.x_ref, bf16[4,8,256,128]{3,2,1,0:T(8,128)(2,1)S(1)} %all_to_all.10.v_ref.x_ref, ...), custom_call_target="tpu_custom_call" | custom-call | flops 2147483648 | bytes 8388608 | tf_op jit(solution)/shard_map/pallas_call | solution.py:326
  144.6 10.9 %collective-permute-done.3 = bf16[3840,128]{1,0:T(8,128)(2,1)} collective-permute-done((bf16[3840,128]{1,0:T(8,128)(2,1)}, bf16[3840,128]{1,0:T(8,128)(2,1)}, u32[]{:S(2)}, u32[]{:S(2)}) %collective-permute-start.3) | collective-permute-done | bytes 983072 | tf_op jit(solution)/shard_map/ppermute | solution.py:387
  155.5 37.4 %conditional.1 = (bf16[4,8,256,128]{3,2,1,0:T(8,128)(2,1)}) conditional(s32[]{:T(128)} %convert_element_type.14, (s32[3,8]{1,0:T(4,128)S(1)}, bf16[4,8,256,128]{3,2,1,0:T(8,128)(2,1)}, bf16[4,8,256,128]{3,2,1,0:T(8,128)(2,1)S(1)}, s32[8,14]{1,0:T(8,128)S(1)}, bf16[4,8,256,128]{3,2,1,0:T(8,128)(2,1)}, /*index=5*/s32[8,1,1024]{2,1,0:T(1,128)S(1)}, ...), branch_computations={%region_7.8_spmd, %region_8.9_spmd} | conditional | flops 2151483648 | bytes 34078808 | solution.py:408
  155.5 37.4 %branch_1_fun.1 = bf16[4,8,256,128]{3,2,1,0:T(8,128)(2,1)} custom-call(s32[8,14]{1,0:T(8,128)S(1)} %get-tuple-element.50.table_ref, bf16[4,8,256,128]{3,2,1,0:T(8,128)(2,1)} %get-tuple-element.51.q_ref, bf16[4,8,256,128]{3,2,1,0:T(8,128)(2,1)} %get-tuple-element.52.k_ref, bf16[4,8,256,128]{3,2,1,0:T(8,128)(2,1)S(1)} %get-tuple-element.53.v_ref, ...), custom_call_target="tpu_custom_call" | custom-call | flops 2147483648 | bytes 8388608 | tf_op jit(solution)/shard_map/cond/branch_1_fun/pallas_call | solution.py:326
  192.9 27.8 %shard_map.59 = bf16[8,256,512]{2,1,0:T(8,128)(2,1)} custom-call(bf16[4,8,256,128]{3,2,1,0:T(8,128)(2,1)} %get-tuple-element.85.o_ref), custom_call_target="tpu_custom_call" | custom-call | tf_op jit(solution)/shard_map/pallas_call | solution.py:154
  220.7 3.0 %copy.33 = bf16[8,256,512]{2,1,0:T(8,128)(2,1)} copy(bf16[8,256,512]{2,1,0:T(8,128)(2,1)} %shard_map.59) | data formatting | bytes 4194304
  (30 shorter events, 0.8 us)
Async XLA Ops:
  59.3 4.6 %copy-start.1 = (s32[8,8,256]{2,1,0:T(8,128)S(1)}, s32[8,8,256]{2,1,0:T(8,128)}, u32[]{:S(2)}) copy-start(s32[8,8,256]{2,1,0:T(8,128)} %get-tuple-element.65) | copy-start | bytes 196612
  59.3 5.2 %copy-start = (s32[8,8,256]{2,1,0:T(8,128)S(1)}, s32[8,8,256]{2,1,0:T(8,128)}, u32[]{:S(2)}) copy-start(s32[8,8,256]{2,1,0:T(8,128)} %get-tuple-element.64) | copy-start | bytes 196612
  59.3 41.9 %all-to-all-start.1 = ((bf16[4,8,256,128]{3,2,1,0:T(8,128)(2,1)}), bf16[4,8,256,128]{3,2,1,0:T(8,128)(2,1)}, u32[]{:S(2)}, u32[]{:S(2)}) async-start(bf16[4,8,256,128]{3,2,1,0:T(8,128)(2,1)} %get-tuple-element.68), calls=%async_computation.1 | async-start | bytes 4194304 | tf_op jit(solution)/shard_map/all_to_all | solution.py:384
  69.0 75.6 %collective-permute-start.2 = (bf16[3840,128]{1,0:T(8,128)(2,1)}, bf16[3840,128]{1,0:T(8,128)(2,1)S(1)}, u32[]{:S(2)}, u32[]{:S(2)}) collective-permute-start(bf16[3840,128]{1,0:T(8,128)(2,1)} %shard_map.57), channel_id=1, source_target_pairs={{0,4},{1,5},{2,6},{3,7},{4,0},{5,1},{6,2},{7,3},{8,12},{9,13},{10,... | collective-permute-start | bytes 2949128 | tf_op jit(solution)/shard_map/ppermute | solution.py:387
  75.1 80.4 %collective-permute-start.3 = (bf16[3840,128]{1,0:T(8,128)(2,1)}, bf16[3840,128]{1,0:T(8,128)(2,1)}, u32[]{:S(2)}, u32[]{:S(2)}) collective-permute-start(bf16[3840,128]{1,0:T(8,128)(2,1)} %shard_map.58), channel_id=1, source_target_pairs={{0,4},{1,5},{2,6},{3,7},{4,0},{5,1},{6,2},{7,3},{8,12},{9,13},{10,... | collective-permute-start | bytes 2949128 | tf_op jit(solution)/shard_map/ppermute | solution.py:387

commit v2 on v1

--- a/solution.py
+++ b/solution.py
@@ -7,10 +7,12 @@
 from jax.experimental.pallas import tpu as pltpu
 from jax.sharding import PartitionSpec as P
 
+
 HEAD_DIM = 64
 DOCS = 16
 LANES = 128
 SPAN = 256
+STRIDE = 512
 PIECE = 32
 PAD = 128
 MASKED = -8192.0
@@ -22,7 +24,7 @@
     return base + lax.rem(me - base + shift, half)
 
 
-def greet(me, others):
+def greet(others):
     barrier = pltpu.get_barrier_semaphore()
     for target in others:
         pl.semaphore_signal(barrier, inc=1, device_id={"seq": target}, device_id_type=pl.DeviceIdType.MESH)
@@ -63,7 +65,7 @@
 
     @pl.when(pl.program_id(0) == 0)
     def _():
-        greet(me, [lax.rem(me + shift, group) for shift in range(1, group)])
+        greet([lax.rem(me + shift, group) for shift in range(1, group)])
         for shift in range(1, group):
             for slot, src, dst in both:
                 ids(shift, slot, src, dst).start()
@@ -136,7 +138,7 @@
         target = peer(me, shift, half)
         return remote(o_ref.at[lax.rem(target, half)], columns, send_sem.at[shift - 1], recv_sem.at[shift - 1], target)
 
-    greet(me, [peer(me, shift, half) for shift in range(1, half)])
+    greet([peer(me, shift, half) for shift in range(1, half)])
     for shift in range(half - 1, 0, -1):
         transfer(shift).start()
     own = pltpu.make_async_copy(o_ref.at[place], held, own_sem)
@@ -167,7 +169,7 @@
 
 
 def pack_kernel(table_ref, x_ref, o_ref):
-    _, rows, count, width = x_ref.shape
+    _, rows, count, _ = x_ref.shape
     room = o_ref.shape[0]
     o_ref[...] = jnp.zeros(o_ref.shape, o_ref.dtype)
     for row in range(rows):
@@ -184,7 +186,7 @@
 
 
 def pack(table, x, room):
-    half, rows, count, width = x.shape
+    _, _, _, width = x.shape
     return pl.pallas_call(
         pack_kernel,
         grid_spec=pltpu.PrefetchScalarGridSpec(
@@ -198,7 +200,7 @@
     )(table, x)
 
 
-def attend_kernel(mode, table_ref, q_ref, k_ref, v_ref, dec_ref, enc_ref, *rest):
+def attend_kernel(mode, table_ref, q_ref, k_ref, v_ref, bounds_ref, *rest):
     if mode:
         more_k, more_v, before_ref, o_ref, keys, values = rest
     else:
@@ -206,6 +208,7 @@
     half, _, count, width = q_ref.shape
     length = half * count
     span = max(SPAN, count)
+    stride = min(STRIDE, length)
     slabs = span // count
     blocks = length // span
     heads = width // HEAD_DIM
@@ -220,17 +223,18 @@
     for block in range(blocks):
         low = entry(0, block)
         begin = jnp.where(wanted[block], jnp.minimum(begin, low), begin)
-        end = jnp.where(wanted[block], jnp.maximum(end, low + entry(1, block) * span), end)
+        end = jnp.where(wanted[block], jnp.maximum(end, low + entry(1, block) * stride), end)
+
+    def within(which, at, amount):
+        position = at + lax.broadcasted_iota(jnp.int32, (amount, LANES), 0)
+        return (position >= bounds_ref[0, which : which + 1]) & (position < bounds_ref[0, which + 1 : which + 2])
 
     def place(at, key, value):
-        ids = enc_ref[0, :, pl.ds(at, LANES)]
-        documents = lax.broadcasted_iota(jnp.int32, (LANES, LANES), 0)
-        miss = jnp.where((documents == ids) | (documents >= DOCS), 0.0, MASKED).astype(jnp.bfloat16)
+        documents = lax.broadcasted_iota(jnp.int32, (LANES, LANES), 1)
         keys[pl.ds(at, LANES), :width] = key
-        keys[pl.ds(at, LANES), width:] = miss.T
+        miss = jnp.where(within(0, at, LANES) | (documents >= DOCS), 0.0, MASKED)
+        keys[pl.ds(at, LANES), width:] = miss.astype(jnp.bfloat16)
         values[:, pl.ds(at, LANES)] = value.T
-
-    chunk = min(LANES, count)
 
     def prepare(index, carry):
         at = pl.multiple_of(index * LANES, LANES)
@@ -268,9 +272,7 @@
         @pl.when(wanted[block])
         def _():
             query = q_ref[slab, 0].reshape(span, width)
-            ids = dec_ref[0, :, pl.ds(block * span, span)]
-            documents = lax.broadcasted_iota(jnp.int32, (LANES, span), 0)
-            hot = jnp.where(documents == ids, 1.0, 0.0).astype(jnp.bfloat16).T
+            hot = jnp.where(within(2, first + block * span, span), 1.0, 0.0).astype(jnp.bfloat16)
             owner = lax.broadcasted_iota(jnp.int32, (span, width), 1) // HEAD_DIM
             sides = [
                 jnp.concatenate([jnp.where(owner == head, query, jnp.zeros_like(query)), hot], axis=1)
@@ -279,8 +281,8 @@
             low = entry(0, block)
 
             def step(index, held):
-                start = pl.multiple_of(low + index * span, LANES)
-                key = keys[pl.ds(start, span), :]
+                start = pl.multiple_of(low + index * stride, LANES)
+                key = keys[pl.ds(start, stride), :]
                 result = []
                 for head in range(heads):
                     peak, total, summed = held[head]
@@ -291,7 +293,7 @@
                     scale = jnp.exp(peak - fresh)
                     expos = jnp.exp(scores - fresh)
                     total = total * scale + jnp.sum(expos, axis=0, keepdims=True)
-                    value = values[head * HEAD_DIM : (head + 1) * HEAD_DIM, pl.ds(start, span)]
+                    value = values[head * HEAD_DIM : (head + 1) * HEAD_DIM, pl.ds(start, stride)]
                     summed = summed * scale + jnp.dot(
                         value, expos.astype(jnp.bfloat16), preferred_element_type=jnp.float32
                     )
@@ -314,13 +316,12 @@
                 o_ref[slab, 0] = before_ref[slab, 0]
 
 
-def attend(mode, table, q, k, v, dec_rows, enc_rows, *more):
+def attend(mode, table, q, k, v, bounds, *more):
     half, rows, count, width = q.shape
     length = half * count
     row_block = pl.BlockSpec((half, 1, count, width), lambda r, *_: (0, r, 0, 0))
     specs = [row_block] * 3
-    specs += [pl.BlockSpec((1, 1, length), lambda r, *_: (r, 0, 0))]
-    specs += [pl.BlockSpec((1, 1, 2 * length), lambda r, *_: (r, 0, 0))]
+    specs += [pl.BlockSpec((1, *bounds.shape[1:]), lambda r, *_: (r, 0, 0))]
     if mode:
         specs += [pl.BlockSpec(more[0].shape, lambda r, *_: (0, 0))] * 2 + [row_block]
     return pl.pallas_call(
@@ -341,14 +342,20 @@
             bytes_accessed=8 * rows * width * length,
             transcendentals=rows * length * length // 4,
         ),
-    )(table, q, k, v, dec_rows, enc_rows, *more)
+    )(table, q, k, v, bounds, *more)
 
 
 def tables(dec_rows, enc_rows, side):
     rows, whole = dec_rows.shape
     length = whole // 2
+    blocks = length // SPAN
+    stride = min(STRIDE, length)
+    numbers = jnp.arange(LANES, dtype=jnp.int32)[None, :, None]
+    bounds = []
+    for ids in (enc_rows, dec_rows):
+        bounds += [jnp.sum(ids[:, None, :] < numbers, axis=2), jnp.sum(ids[:, None, :] <= numbers, axis=2)]
+    bounds = jnp.stack(bounds, axis=1).astype(jnp.int32)
     mine = lax.dynamic_slice(dec_rows, (0, side * length), (rows, length))
-    blocks = length // SPAN
     docs = mine.reshape(rows, blocks, SPAN)
     starts = jnp.concatenate([docs[:, :, 0], dec_rows[:, length : length + 1]], axis=1)
     ends = jnp.concatenate([docs[:, :, -1], dec_rows[:, length - 1 : length]], axis=1)
@@ -360,21 +367,21 @@
     before, upto = before[:, :blocks], upto[:, :blocks]
     crosses = jnp.where(side == 0, upto > length, before < length).astype(jnp.int32)
     low = before // LANES * LANES
-    steps = (upto - low + SPAN - 1) // SPAN
-    low = jnp.minimum(low, whole - steps * SPAN)
+    steps = (upto - low + stride - 1) // stride
+    low = jnp.minimum(low, whole - steps * stride)
     sent, got = jnp.where(side == 0, up, down), jnp.where(side == 0, down, up)
     offset_of = [PAD + jnp.cumsum(amount) - amount for amount in (sent, got)]
     first = jnp.where(side == 0, length - sent, 0)
     send = jnp.stack([offset_of[0], first, sent])
     base = offset_of[1] - jnp.where(side == 0, length, length - got)
     known = jnp.concatenate([low, steps, crosses, base[:, None], jnp.full((rows, 1), side, jnp.int32)], axis=1)
-    return send, known, mine, jnp.maximum(jnp.sum(up), jnp.sum(down))
-
-
-def local(queries, enc_keys, enc_values, dec_ids, enc_ids):
+    return send, known, bounds, jnp.maximum(jnp.sum(up), jnp.sum(down))
+
+
+def whole(queries, enc_keys, enc_values, dec_ids, enc_ids):
     group = lax.axis_size("seq")
     half = group // 2
-    rows, count, features = queries.shape
+    rows, count, _ = queries.shape
     length = half * count
     side = lax.axis_index("seq") // half
     k, dec_all, enc_all, v_packed, q_packed = gather(queries, enc_keys, enc_values, dec_ids, enc_ids, group)
@@ -386,24 +393,25 @@
     def cross(block):
         return lax.ppermute(block, "seq", [(i, (i + half) % group) for i in range(group)])
 
-    v = exchange(v_packed)
-    q = exchange(q_packed)
     dec_rows, enc_rows = (x.transpose(1, 0, 2).reshape(rows, 2 * length) for x in (dec_all, enc_all))
-    send, known, mine, most = tables(dec_rows, enc_rows, side)
-    most = lax.pmax(most, "dp")
+    send, known, bounds, most = tables(dec_rows, enc_rows, side)
     room = rows * length * SHARE // 16 // 128 * 128 + 2 * PAD
     full = rows * length + 2 * PAD
-    more_k = cross(pack(send, k, room))
-    more_v = cross(pack(send, v, room))
-    mine, enc_rows = mine[:, None, :], enc_rows[:, None, :]
-    early = attend(0, known, q, k, v, mine, enc_rows)
+    k_packed, v_packed = lax.optimization_barrier((pack(send, k, room), v_packed))
+    more_k = cross(k_packed)
+    v = exchange(v_packed)
+    v_cross, q_packed = lax.optimization_barrier((pack(send, v, room), q_packed))
+    more_v = cross(v_cross)
+    q = exchange(q_packed)
+    most = lax.pmax(most, "dp")
+    early = attend(0, known, q, k, v, bounds)
 
     def enough(more_k, more_v):
-        return attend(1, known, q, k, v, mine, enc_rows, more_k, more_v, early)
+        return attend(1, known, q, k, v, bounds, more_k, more_v, early)
 
     def overflow(more_k, more_v):
         more_k, more_v = cross(pack(send, k, full)), cross(pack(send, v, full))
-        return attend(1, known, q, k, v, mine, enc_rows, more_k, more_v, early)
+        return attend(1, known, q, k, v, bounds, more_k, more_v, early)
 
     return give_back(lax.cond(most <= room - 2 * PAD, enough, overflow, more_k, more_v), group)
 
@@ -417,4 +425,4 @@
         P("dp", "seq"),
     )
     out_specs = P("dp", "seq", None)
-    return jax.shard_map(local, mesh=mesh, in_specs=in_specs, out_specs=out_specs, check_vma=False)
+    return jax.shard_map(whole, mesh=mesh, in_specs=in_specs, out_specs=out_specs, check_vma=False)

time: 226 us -> 215 us (0.951)
  the two profiles are of different devices: /device:TPU:16 before, /device:TPU:0 now
where the time goes in v2:
time: 215 us; the launch traced here: 212 us
  Pallas kernels  126 us (59%)
  blocking collectives  34.6 us (16%)
  waiting for transfers between devices  29.1 us (14%)
  starting transfers between devices  7.65 us (4%)
  other arithmetic  6.97 us (3%)
  local copies, waits for them, and re-layouts  5.46 us (3%)
    pallas_call x2, Pallas kernels, attend(): pl.pallas_call(functools.partial(attend_kernel, mode), grid_spec=pltpu.Pr...  63.1 us
    pallas_call x1, Pallas kernels, gather(): pl.pallas_call(functools.partial(gather_kernel, group), grid=(rows,), in_...  34 us
    all_to_all x1, blocking collectives, exchange(): lax.all_to_all(block, 'seq', split_axis=0, concat_axis=0, axis_index_grou...  29.2 us
    all_to_all x1, waiting for transfers between devices, exchange(): lax.all_to_all(block, 'seq', split_axis=0, concat_axis=0, axis_index_grou...  29.1 us
    pallas_call x1, Pallas kernels, give_back(): pl.pallas_call(functools.partial(give_back_kernel, group), in_specs=[pl.B...  24.2 us
    pmax x1, blocking collectives, whole(): most = lax.pmax(most, 'dp')  5.4 us
    all_to_all x1, starting transfers between devices, exchange(): lax.all_to_all(block, 'seq', split_axis=0, concat_axis=0, axis_index_grou...  4.62 us
    pallas_call x2, Pallas kernels, pack(): pl.pallas_call(pack_kernel, grid_spec=pltpu.PrefetchScalarGridSpec(num_sc...  4.54 us
  transfers between devices with their start and end apart: 3, of which 1 were waited for; matrix products, arithmetic and copies ran while one was open for 3% of the time, Pallas kernels for 22%

profile of v2, /device:TPU:0, one launch (start us, length us, event | category | flops | bytes accessed | tf_op | source)
XLA Modules:
  0.0 211.9 jit_solution(16967864659936428770)
XLA Ops:
  0.0 34.0 %shard_map.55 = (bf16[4,8,256,128]{3,2,1,0:T(8,128)(2,1)S(1)}, s32[8,8,256]{2,1,0:T(8,128)}, s32[8,8,256]{2,1,0:T(8,128)}, bf16[4,8,256,128]{3,2,1,0:T(8,128)(2,1)}, bf16[4,8,256,128]{3,2,1,0:T(8,128)(2,1)}) custom-call(bf16[8,256,512]{2,1,0:T(8,128)(2,1)} %k_ref.1, s32[8,256]{1,0:T(8,128)} %dec_ref.1, s32[8,256]{1,0:T(8,128)} %enc_ref.1, ...), custom_call_target="tpu_custom_call" | custom-call | tf_op jit(solution)/shard_map/pallas_call | solution.py:110
  34.0 0.8 fusion.17
  34.8 0.8 constant_dynamic-slice_fusion
  35.7 0.1 copy.15
  35.9 0.1 copy.18
  36.0 1.2 convert_reduce_fusion.4
  37.4 0.2 select_reduce_fusion
  37.5 0.2 reduce-window_clone.1
  37.8 2.3 %shard_map.56 = bf16[3840,128]{1,0:T(8,128)(2,1)} custom-call(s32[3,8]{1,0:T(4,128)S(1)} %pad_add_fusion.3.table_ref, bf16[4,8,256,128]{3,2,1,0:T(8,128)(2,1)S(1)} %get-tuple-element.64.x_ref.k_ref), custom_call_target="tpu_custom_call" | custom-call | flops 2000000 | bytes 4194304 | tf_op jit(solution)/shard_map/pallas_call | solution.py:190
  40.0 29.2 %all_to_all.10.x_ref.v_ref = bf16[4,8,256,128]{3,2,1,0:T(8,128)(2,1)S(1)} all-to-all(bf16[4,8,256,128]{3,2,1,0:T(8,128)(2,1)} %get-tuple-element.66), channel_id=1, replica_groups={{0,1,2,3},{4,5,6,7},{8,9,10,11},{12,13,14,15},{16,17,18,19},{20,21,22,2..., dimensions={0} | all-to-all | bytes 4194304 | tf_op jit(solution)/shard_map/all_to_all | solution.py:391
  69.2 2.3 %shard_map.57 = bf16[3840,128]{1,0:T(8,128)(2,1)} custom-call(s32[3,8]{1,0:T(4,128)S(1)} %pad_add_fusion.3.table_ref, bf16[4,8,256,128]{3,2,1,0:T(8,128)(2,1)S(1)} %all_to_all.10.x_ref.v_ref), custom_call_target="tpu_custom_call" | custom-call | flops 2000000 | bytes 4194304 | tf_op jit(solution)/shard_map/pallas_call | solution.py:190
  71.5 4.6 %all-to-all-start.1 = ((bf16[4,8,256,128]{3,2,1,0:T(8,128)(2,1)}), bf16[4,8,256,128]{3,2,1,0:T(8,128)(2,1)}, u32[]{:S(2)}, u32[]{:S(2)}) async-start(bf16[4,8,256,128]{3,2,1,0:T(8,128)(2,1)} %get-tuple-element.68), calls=%async_computation.1 | async-start | bytes 4194304 | tf_op jit(solution)/shard_map/all_to_all | solution.py:391
  76.4 0.7 multiply_reduce_fusion
  77.1 0.6 multiply_reduce_fusion.1
  79.1 3.0 %collective-permute-start.3 = (bf16[3840,128]{1,0:T(8,128)(2,1)}, bf16[3840,128]{1,0:T(8,128)(2,1)}, u32[]{:S(2)}, u32[]{:S(2)}) collective-permute-start(bf16[3840,128]{1,0:T(8,128)(2,1)} %shard_map.57), channel_id=1, source_target_pairs={{0,4},{1,5},{2,6},{3,7},{4,0},{5,1},{6,2},{7,3},{8,12},{9,13},{10,... | collective-permute-start | bytes 2949128 | tf_op jit(solution)/shard_map/ppermute | solution.py:394
  82.1 5.4 %pmax.7 = s32[]{:T(128)} all-reduce(s32[]{:T(128)S(6)} %max.63), channel_id=1, replica_groups=mesh['dp'=4,'seq'=8] {'dp'}, use_global_device_ids=true, to_apply=%region_4.5 | all-reduce | flops 1 | bytes 8 | tf_op jit(solution)/shard_map/pmax | solution.py:406
  88.1 2.0 convert_reduce_fusion.3
  90.1 2.0 convert_reduce_fusion.1
  92.1 29.1 %all-to-all-done.1.q_ref = bf16[4,8,256,128]{3,2,1,0:T(8,128)(2,1)} async-done(((bf16[4,8,256,128]{3,2,1,0:T(8,128)(2,1)}), bf16[4,8,256,128]{3,2,1,0:T(8,128)(2,1)}, u32[]{:S(2)}, u32[]{:S(2)}) %all-to-all-start.1) | async-done | bytes 2097184 | tf_op jit(solution)/shard_map/all_to_all | solution.py:391
  121.3 47.2 %shard_map.58 = bf16[4,8,256,128]{3,2,1,0:T(8,128)(2,1)} custom-call(s32[8,14]{1,0:T(8,128)S(1)} %concatenate.11.table_ref, bf16[4,8,256,128]{3,2,1,0:T(8,128)(2,1)} %all-to-all-done.1.q_ref, bf16[4,8,256,128]{3,2,1,0:T(8,128)(2,1)} %copy-done, bf16[4,8,256,128]{3,2,1,0:T(8,128)(2,1)S(1)} %all_to_all.10.x_ref.v_ref, s32[8,4,128]{2,1,0:T(4,128)S(1)} %pad_add_fusion.bounds_ref), custom_call_target="tpu_custom_call" | custom-call | flops 2147483648 | bytes 8388608 | tf_op jit(solution)/shard_map/pallas_call | solution.py:327
  168.5 16.1 %conditional.1 = (bf16[4,8,256,128]{3,2,1,0:T(8,128)(2,1)}) conditional(s32[]{:T(128)} %convert_element_type.26, (s32[3,8]{1,0:T(4,128)S(1)}, bf16[4,8,256,128]{3,2,1,0:T(8,128)(2,1)}, bf16[4,8,256,128]{3,2,1,0:T(8,128)(2,1)S(1)}, s32[8,14]{1,0:T(8,128)S(1)}, bf16[4,8,256,128]{3,2,1,0:T(8,128)(2,1)}, /*index=5*/s32[8,4,128]{2,1,0:T(4,128)S(1)}, ...), branch_computations={%region_11.12_spmd, %region_12.13_spmd} | conditional | flops 2151483648 | bytes 34078808 | solution.py:416
  168.8 15.9 %branch_1_fun.1 = bf16[4,8,256,128]{3,2,1,0:T(8,128)(2,1)} custom-call(s32[8,14]{1,0:T(8,128)S(1)} %get-tuple-element.45.table_ref, bf16[4,8,256,128]{3,2,1,0:T(8,128)(2,1)} %get-tuple-element.46.q_ref, bf16[4,8,256,128]{3,2,1,0:T(8,128)(2,1)} %get-tuple-element.47.k_ref, bf16[4,8,256,128]{3,2,1,0:T(8,128)(2,1)S(1)} %get-tuple-element.48.v_ref, ...), custom_call_target="tpu_custom_call" | custom-call | flops 2147483648 | bytes 8388608 | tf_op jit(solution)/shard_map/cond/branch_1_fun/pallas_call | solution.py:327
  184.6 24.2 %shard_map.59 = bf16[8,256,512]{2,1,0:T(8,128)(2,1)} custom-call(bf16[4,8,256,128]{3,2,1,0:T(8,128)(2,1)} %get-tuple-element.91.o_ref), custom_call_target="tpu_custom_call" | custom-call | tf_op jit(solution)/shard_map/pallas_call | solution.py:156
  208.9 3.0 %copy.30 = bf16[8,256,512]{2,1,0:T(8,128)(2,1)} copy(bf16[8,256,512]{2,1,0:T(8,128)(2,1)} %shard_map.59) | data formatting | bytes 4194304
  (32 shorter events, 0.9 us)
Async XLA Ops:
  34.0 6.0 %copy-start = (bf16[4,8,256,128]{3,2,1,0:T(8,128)(2,1)}, bf16[4,8,256,128]{3,2,1,0:T(8,128)(2,1)S(1)}, u32[]{:S(2)}) copy-start(bf16[4,8,256,128]{3,2,1,0:T(8,128)(2,1)S(1)} %get-tuple-element.64.x_ref.k_ref) | copy-start | bytes 6291460
  71.5 16.6 %copy-start.1 = (s32[8,8,256]{2,1,0:T(8,128)S(1)}, s32[8,8,256]{2,1,0:T(8,128)}, u32[]{:S(2)}) copy-start(s32[8,8,256]{2,1,0:T(8,128)} %get-tuple-element.62) | copy-start | bytes 196612
  71.5 18.6 %copy-start.2 = (s32[8,8,256]{2,1,0:T(8,128)S(1)}, s32[8,8,256]{2,1,0:T(8,128)}, u32[]{:S(2)}) copy-start(s32[8,8,256]{2,1,0:T(8,128)} %get-tuple-element.63) | copy-start | bytes 196612
  71.5 49.8 %all-to-all-start.1 = ((bf16[4,8,256,128]{3,2,1,0:T(8,128)(2,1)}), bf16[4,8,256,128]{3,2,1,0:T(8,128)(2,1)}, u32[]{:S(2)}, u32[]{:S(2)}) async-start(bf16[4,8,256,128]{3,2,1,0:T(8,128)(2,1)} %get-tuple-element.68), calls=%async_computation.1 | async-start | bytes 4194304 | tf_op jit(solution)/shard_map/all_to_all | solution.py:391
  76.2 92.4 %collective-permute-start.2 = (bf16[3840,128]{1,0:T(8,128)(2,1)}, bf16[3840,128]{1,0:T(8,128)(2,1)S(1)}, u32[]{:S(2)}, u32[]{:S(2)}) collective-permute-start(bf16[3840,128]{1,0:T(8,128)(2,1)} %shard_map.56), channel_id=1, source_target_pairs={{0,4},{1,5},{2,6},{3,7},{4,0},{5,1},{6,2},{7,3},{8,12},{9,13},{10,... | collective-permute-start | bytes 2949128 | tf_op jit(solution)/shard_map/ppermute | solution.py:394
  79.1 89.4 %collective-permute-start.3 = (bf16[3840,128]{1,0:T(8,128)(2,1)}, bf16[3840,128]{1,0:T(8,128)(2,1)}, u32[]{:S(2)}, u32[]{:S(2)}) collective-permute-start(bf16[3840,128]{1,0:T(8,128)(2,1)} %shard_map.57), channel_id=1, source_target_pairs={{0,4},{1,5},{2,6},{3,7},{4,0},{5,1},{6,2},{7,3},{8,12},{9,13},{10,... | collective-permute-start | bytes 2949128 | tf_op jit(solution)/shard_map/ppermute | solution.py:394

commit v3 on v2

v3 whole, which is shorter than its diff:
```python
import functools

import jax
import jax.numpy as jnp
from jax import lax
from jax.experimental import pallas as pl
from jax.experimental.pallas import tpu as pltpu
from jax.sharding import PartitionSpec as P


HEAD_DIM = 64
DOCS = 16
LANES = 128
SPAN = 256
STRIDE = 512
PIECE = 32
PAD = 128
MASKED = -8192.0
ROOM = 11
TRIP = 512


def peer(me, shift, half):
    base = me // half * half
    return base + lax.rem(me - base + shift, half)


def greet(others):
    barrier = pltpu.get_barrier_semaphore()
    for target in others:
        pl.semaphore_signal(barrier, inc=1, device_id={"seq": target}, device_id_type=pl.DeviceIdType.MESH)
    pl.semaphore_wait(barrier, len(others))


def remote(src, dst, send_sem, recv_sem, target):
    return pltpu.make_async_remote_copy(
        src_ref=src,
        dst_ref=dst,
        send_sem=send_sem,
        recv_sem=recv_sem,
        device_id={"seq": target},
        device_id_type=pl.DeviceIdType.MESH,
    )


def gather_kernel(
    group, k_ref, v_ref, dec_ref, enc_ref, q_ref, k_out, v_out, dec_out, enc_out, q_out, held, ids_held, own_sem, ids_sem, send_sem, recv_sem, ids_send, ids_recv
):
    me = lax.axis_index("seq")
    half = group // 2
    width = k_out.shape[3]
    place = lax.rem(me, half)
    large = ((0, k_ref, k_out), (1, v_ref, v_out))
    small = ((0, dec_ref, dec_out), (1, enc_ref, enc_out))

    def columns(src, target):
        return src.at[:, :, pl.ds(pl.multiple_of(lax.rem(target, half) * width, LANES), width)]

    def heads(shift, slot, src, dst):
        target = peer(me, shift, half)
        at = slot * (half - 1) + shift - 1
        return remote(columns(src, target), dst.at[place], send_sem.at[at], recv_sem.at[at], target)

    def ids(shift, slot, src, dst):
        at = slot * (group - 1) + shift - 1
        return remote(src, dst.at[me], ids_send.at[at], ids_recv.at[at], lax.rem(me + shift, group))

    @pl.when(pl.program_id(0) == 0)
    def _():
        greet([lax.rem(me + shift, group) for shift in range(1, group)])
        for shift in range(1, group):
            for each in small:
                ids(shift, *each).start()
        for each in large:
            for shift in range(half - 1, 0, -1):
                heads(shift, *each).start()
        own = [pltpu.make_async_copy(columns(src, me), held.at[slot], own_sem.at[slot]) for slot, src, _ in large]
        own += [pltpu.make_async_copy(src, ids_held.at[slot], ids_sem.at[slot]) for slot, src, _ in small]
        for copy in own:
            copy.start()
        for copy in own:
            copy.wait()
        own = [pltpu.make_async_copy(held.at[slot], dst.at[place], own_sem.at[slot]) for slot, _, dst in large]
        own += [pltpu.make_async_copy(ids_held.at[slot], dst.at[me], ids_sem.at[slot]) for slot, _, dst in small]
        for copy in own:
            copy.start()
        for copy in own:
            copy.wait()

    for target in range(half):
        q_out[target, 0] = q_ref[0, :, target * width : (target + 1) * width]

    @pl.when(pl.program_id(0) == pl.num_programs(0) - 1)
    def _():
        for shift in range(1, group):
            for each in small:
                ids(shift, *each).wait()
        for each in large:
            for shift in range(1, half):
                heads(shift, *each).wait()


def gather(q, k, v, dec_ids, enc_ids, group):
    rows, count, features = k.shape
    half = group // 2
    width = features // half
    anywhere = pl.BlockSpec(memory_space=pl.ANY)
    block = pl.BlockSpec((1, count, features), lambda r: (r, 0, 0))
    packed = pl.BlockSpec((half, 1, count, width), lambda r: (0, r, 0, 0))
    spread = jax.ShapeDtypeStruct((half, rows, count, width), k.dtype)
    every = jax.ShapeDtypeStruct((group, rows, count), dec_ids.dtype)
    dma = pltpu.SemaphoreType.DMA
    return pl.pallas_call(
        functools.partial(gather_kernel, group),
        grid=(rows,),
        in_specs=[anywhere] * 4 + [block],
        out_specs=[anywhere] * 4 + [packed],
        out_shape=[spread, spread, every, every, spread],
        scratch_shapes=[
            pltpu.VMEM((2, rows, count, width), k.dtype),
            pltpu.VMEM((2, rows, count), dec_ids.dtype),
            dma((2,)),
            dma((2,)),
            dma((2 * (half - 1),)),
            dma((2 * (half - 1),)),
            dma((2 * (group - 1),)),
            dma((2 * (group - 1),)),
        ],
        compiler_params=pltpu.CompilerParams(collective_id=0, has_side_effects=True),
    )(k, v, dec_ids, enc_ids, q)


def give_back_kernel(group, o_ref, out_ref, held, own_sem, send_sem, recv_sem):
    me = lax.axis_index("seq")
    half = group // 2
    width = o_ref.shape[3]
    place = lax.rem(me, half)
    columns = out_ref.at[:, :, pl.ds(pl.multiple_of(place * width, LANES), width)]

    def transfer(shift):
        target = peer(me, shift, half)
        return remote(o_ref.at[lax.rem(target, half)], columns, send_sem.at[shift - 1], recv_sem.at[shift - 1], target)

    greet([peer(me, shift, half) for shift in range(1, half)])
    for shift in range(half - 1, 0, -1):
        transfer(shift).start()
    own = pltpu.make_async_copy(o_ref.at[place], held, own_sem)
    own.start()
    own.wait()
    own = pltpu.make_async_copy(held, columns, own_sem)
    own.start()
    own.wait()
    for shift in range(1, half):
        transfer(shift).wait()


def give_back(o, group):
    half, rows, count, width = o.shape
    return pl.pallas_call(
        functools.partial(give_back_kernel, group),
        in_specs=[pl.BlockSpec(memory_space=pl.ANY)],
        out_specs=pl.BlockSpec(memory_space=pl.ANY),
        out_shape=jax.ShapeDtypeStruct((rows, count, half * width), o.dtype),
        scratch_shapes=[
            pltpu.VMEM((rows, count, width), o.dtype),
            pltpu.SemaphoreType.DMA,
            pltpu.SemaphoreType.DMA((half - 1,)),
            pltpu.SemaphoreType.DMA((half - 1,)),
        ],
        compiler_params=pltpu.CompilerParams(collective_id=1, has_side_effects=True),
    )(o)


def pack_kernel(table_ref, k_ref, v_ref, o_ref, rest_ref, stage):
    _, rows, count, width = k_ref.shape
    room = o_ref.shape[0]
    stage[...] = jnp.zeros(stage.shape, stage.dtype)
    for row in range(rows):
        offset, start, amount = table_ref[0, row], table_ref[1, row], table_ref[2, row]

        def move(index, carry):
            at = start + index * PIECE
            slab, inside = at // count, pl.ds(pl.multiple_of(at % count, PIECE), PIECE)
            into = pl.ds(pl.multiple_of(offset + index * PIECE, PIECE), PIECE)
            stage[into, :width] = k_ref[slab, row, inside, :]
            stage[into, width:] = v_ref[slab, row, inside, :]
            return carry

        lax.fori_loop(0, amount // PIECE, move, 0)
    o_ref[...] = stage[:room]
    rest_ref[...] = stage[room:]


def pack(table, k, v, room):
    half, rows, count, width = k.shape
    full = rows * half * count + 2 * PAD
    whole = pl.BlockSpec(k.shape, lambda r, *_: (0, 0, 0, 0))
    shapes = [(room, 2 * width), (full - room, 2 * width)]
    return pl.pallas_call(
        pack_kernel,
        grid_spec=pltpu.PrefetchScalarGridSpec(
            num_scalar_prefetch=1,
            grid=(1,),
            in_specs=[whole] * 2,
            out_specs=[pl.BlockSpec(shape, lambda r, *_: (0, 0)) for shape in shapes],
            scratch_shapes=[pltpu.VMEM((full, 2 * width), k.dtype)],
        ),
        out_shape=[jax.ShapeDtypeStruct(shape, k.dtype) for shape in shapes],
        cost_estimate=pl.CostEstimate(flops=2000000, bytes_accessed=8 * k.size, transcendentals=0),
    )(table, k, v)


def within(bounds_ref, which, at, amount):
    position = at + lax.broadcasted_iota(jnp.int32, (amount, LANES), 0)
    return (position >= bounds_ref[0, which : which + 1]) & (position < bounds_ref[0, which + 1 : which + 2])


def missing(bounds_ref, at, amount):
    documents = lax.broadcasted_iota(jnp.int32, (amount, LANES), 1)
    inside = within(bounds_ref, 0, at, amount) | (documents >= DOCS)
    return jnp.where(inside, 0.0, MASKED).astype(jnp.bfloat16)


def prepare_kernel(table_ref, k_ref, v_ref, bounds_ref, keys, values):
    half, _, count, width = k_ref.shape
    length = half * count
    keys[0, :, :width] = k_ref[:, 0].reshape(length, width)
    keys[0, :, width:] = missing(bounds_ref, table_ref[0, table_ref.shape[1] - 1] * length, length)
    values[0] = v_ref[:, 0].reshape(length, width).T


def prepare(table, k, v, bounds):
    half, rows, count, width = k.shape
    length = half * count
    row_block = pl.BlockSpec((half, 1, count, width), lambda r, *_: (0, r, 0, 0))
    shapes = [(1, length, width + LANES), (1, width, length)]
    return pl.pallas_call(
        prepare_kernel,
        grid_spec=pltpu.PrefetchScalarGridSpec(
            num_scalar_prefetch=1,
            grid=(rows,),
            in_specs=[row_block, row_block, pl.BlockSpec((1, *bounds.shape[1:]), lambda r, *_: (r, 0, 0))],
            out_specs=[pl.BlockSpec(shape, lambda r, *_: (r, 0, 0)) for shape in shapes],
        ),
        out_shape=[jax.ShapeDtypeStruct((rows, *shape[1:]), k.dtype) for shape in shapes],
        cost_estimate=pl.CostEstimate(flops=2000000, bytes_accessed=10 * k.size, transcendentals=0),
    )(table, k, v, bounds)


def attend_block(query, hot, low, steps, stride, keys, values, at):
    span, width = query.shape
    heads = width // HEAD_DIM
    owner = lax.broadcasted_iota(jnp.int32, (width, span), 0) // HEAD_DIM
    turned = query.T
    hot = hot.T
    sides = [
        jnp.concatenate([jnp.where(owner == head, turned, jnp.zeros_like(turned)), hot], axis=0)
        for head in range(heads)
    ]

    def step(index, held):
        start = pl.multiple_of(low + index * stride, LANES)
        key = keys[(*at, pl.ds(start, stride), slice(None))]
        result = []
        for head in range(heads):
            peak, total, summed = held[head]
            scores = jnp.dot(key, sides[head], preferred_element_type=jnp.float32)
            fresh = jnp.maximum(peak, jnp.max(scores, axis=0, keepdims=True))
            scale = jnp.exp(peak - fresh)
            expos = jnp.exp(scores - fresh)
            total = total * scale + jnp.sum(expos, axis=0, keepdims=True)
            value = values[(*at, slice(head * HEAD_DIM, (head + 1) * HEAD_DIM), pl.ds(start, stride))]
            summed = summed * scale + jnp.dot(value, expos.astype(jnp.bfloat16), preferred_element_type=jnp.float32)
            result.append((fresh, total, summed))
        return tuple(result)

    init = (
        jnp.full((1, span), 4 * MASKED, jnp.float32),
        jnp.zeros((1, span), jnp.float32),
        jnp.zeros((HEAD_DIM, span), jnp.float32),
    )
    done = lax.fori_loop(0, steps, step, (init,) * heads)
    whole = jnp.concatenate([summed / total for _, total, summed in done], axis=0)
    return whole.T.astype(jnp.bfloat16)


def attend_kernel(mode, table_ref, q_ref, keys_ref, values_ref, bounds_ref, *rest):
    if mode:
        more_ref, late_ref, before_ref, o_ref, keys, values, stage = rest
    else:
        o_ref = rest[0]
    half, _, count, width = q_ref.shape
    length = half * count
    span = max(SPAN, count)
    stride = min(STRIDE, length)
    slabs = span // count
    blocks = length // span
    row = pl.program_id(0)
    first = table_ref[row, 3 * blocks + 1] * length

    def entry(kind, block):
        return table_ref[row, kind * blocks + block]

    wanted = [entry(2, block) == mode for block in range(blocks)]
    if mode:
        begin, end = jnp.int32(2 * length), jnp.int32(0)
        for block in range(blocks):
            low = entry(0, block)
            begin = jnp.where(wanted[block], jnp.minimum(begin, low), begin)
            end = jnp.where(wanted[block], jnp.maximum(end, low + entry(1, block) * stride), end)

        def fetch(index, carry):
            at = pl.multiple_of(index * LANES, LANES)
            local = at - first
            mine = (local >= 0) & (local < length)

            @pl.when(mine)
            def _():
                inside = pl.ds(pl.multiple_of(local, LANES), LANES)
                keys[pl.ds(at, LANES), :] = keys_ref[0, inside, :]
                values[:, pl.ds(at, LANES)] = values_ref[0, :, inside]

            @pl.when(jnp.logical_not(mine))
            def _():
                room, extra = more_ref.shape[0], late_ref.shape[0]
                from_ = jnp.clip(table_ref[row, 3 * blocks] + at, 0, room + extra - LANES)
                for piece in range(0, LANES, PIECE):
                    one = from_ + piece

                    @pl.when(one < room)
                    def _():
                        stage[piece : piece + PIECE] = more_ref[pl.ds(pl.multiple_of(one, PIECE), PIECE), :]

                    @pl.when(one >= room)
                    def _():
                        stage[piece : piece + PIECE] = late_ref[pl.ds(pl.multiple_of(one - room, PIECE), PIECE), :]

                keys[pl.ds(at, LANES), :width] = stage[:, :width]
                keys[pl.ds(at, LANES), width:] = missing(bounds_ref, at, LANES)
                values[:, pl.ds(at, LANES)] = stage[:, width:].T

            return carry

        lax.fori_loop(begin // LANES, end // LANES, fetch, 0)

    for block in range(blocks):
        slab = pl.ds(block * slabs, slabs)

        @pl.when(wanted[block])
        def _():
            query = q_ref[slab, 0].reshape(span, width)
            hot = jnp.where(within(bounds_ref, 2, first + block * span, span), 1.0, 0.0).astype(jnp.bfloat16)
            low, steps = entry(0, block), entry(1, block)
            if mode:
                result = attend_block(query, hot, low, steps, stride, keys, values, ())
            else:
                low = jnp.minimum(low - first, length - steps * stride)
                result = attend_block(query, hot, low, steps, stride, keys_ref, values_ref, (0,))
            o_ref[slab, 0] = result.reshape(slabs, count, width)

        if mode:

            @pl.when(jnp.logical_not(wanted[block]))
            def _():
                o_ref[slab, 0] = before_ref[slab, 0]


def attend(mode, table, q, keys, values, bounds, *more):
    half, rows, count, width = q.shape
    length = half * count
    row_block = pl.BlockSpec((half, 1, count, width), lambda r, *_: (0, r, 0, 0))
    specs = [row_block]
    specs += [pl.BlockSpec((1, *x.shape[1:]), lambda r, *_: (r, 0, 0)) for x in (keys, values, bounds)]
    scratch = []
    if mode:
        specs += [pl.BlockSpec(x.shape, lambda r, *_: (0, 0)) for x in more[:2]] + [row_block]
        scratch = [
            pltpu.VMEM((2 * length, width + LANES), jnp.bfloat16),
            pltpu.VMEM((width, 2 * length), jnp.bfloat16),
            pltpu.VMEM((LANES, 2 * width), jnp.bfloat16),
        ]
    share = 4 if mode else 1
    return pl.pallas_call(
        functools.partial(attend_kernel, mode),
        grid_spec=pltpu.PrefetchScalarGridSpec(
            num_scalar_prefetch=1, grid=(rows,), in_specs=specs, out_specs=row_block, scratch_shapes=scratch
        ),
        out_shape=jax.ShapeDtypeStruct(q.shape, q.dtype),
        cost_estimate=pl.CostEstimate(
            flops=rows * width // HEAD_DIM * length * length * 128 // share,
            bytes_accessed=8 * rows * width * length,
            transcendentals=rows * length * length // 4 // share,
        ),
    )(table, q, keys, values, bounds, *more)


def tables(dec_rows, enc_rows, side):
    rows, whole = dec_rows.shape
    length = whole // 2
    blocks = length // SPAN
    stride = min(STRIDE, length)
    numbers = jnp.arange(LANES, dtype=jnp.int32)[None, :, None]
    bounds = []
    for ids in (enc_rows, dec_rows):
        bounds += [jnp.sum(ids[:, None, :] < numbers, axis=2), jnp.sum(ids[:, None, :] <= numbers, axis=2)]
    bounds = jnp.stack(bounds, axis=1).astype(jnp.int32)
    mine = lax.dynamic_slice(dec_rows, (0, side * length), (rows, length))
    docs = mine.reshape(rows, blocks, SPAN)
    starts = jnp.concatenate([docs[:, :, 0], dec_rows[:, length : length + 1]], axis=1)
    ends = jnp.concatenate([docs[:, :, -1], dec_rows[:, length - 1 : length]], axis=1)
    before = jnp.sum(enc_rows[:, None, :] < starts[:, :, None], axis=2, dtype=jnp.int32)
    upto = jnp.sum(enc_rows[:, None, :] <= ends[:, :, None], axis=2, dtype=jnp.int32)
    up = jnp.maximum(length - before[:, blocks], 0)
    down = jnp.maximum(upto[:, blocks] - length, 0)
    up, down = (-(-amount // PIECE) * PIECE for amount in (up, down))
    before, upto = before[:, :blocks], upto[:, :blocks]
    crosses = jnp.where(side == 0, upto > length, before < length).astype(jnp.int32)
    low = before // LANES * LANES
    steps = (upto - low + stride - 1) // stride
    low = jnp.minimum(low, whole - steps * stride)
    sent, got = jnp.where(side == 0, up, down), jnp.where(side == 0, down, up)
    offset_of = [PAD + jnp.cumsum(amount) - amount for amount in (sent, got)]
    first = jnp.where(side == 0, length - sent, 0)
    send = jnp.stack([offset_of[0], first, sent])
    base = offset_of[1] - jnp.where(side == 0, length, length - got)
    known = jnp.concatenate([low, steps, crosses, base[:, None], jnp.full((rows, 1), side, jnp.int32)], axis=1)
    return send, known, bounds, jnp.maximum(jnp.sum(up), jnp.sum(down))


def whole(queries, enc_keys, enc_values, dec_ids, enc_ids):
    group = lax.axis_size("seq")
    half = group // 2
    rows, count, _ = queries.shape
    length = half * count
    side = lax.axis_index("seq") // half
    k, v, dec_all, enc_all, q_packed = gather(queries, enc_keys, enc_values, dec_ids, enc_ids, group)
    sides = [list(range(half)), list(range(half, group))]

    def cross(block):
        return lax.ppermute(block, "seq", [(i, (i + half) % group) for i in range(group)])

    q = lax.all_to_all(q_packed, "seq", split_axis=0, concat_axis=0, axis_index_groups=sides, tiled=True)
    dec_rows, enc_rows = (x.transpose(1, 0, 2).reshape(rows, 2 * length) for x in (dec_all, enc_all))
    send, known, bounds, most = tables(dec_rows, enc_rows, side)
    trip = min(TRIP, length)
    full = rows * length + 2 * PAD
    room = full - (rows * length * (32 - ROOM) // 32 + trip - 1) // trip * trip
    main, rest = pack(send, k, v, room)
    more = cross(main)
    keys, values = prepare(known, k, v, bounds)
    most = lax.pmax(most, "dp")
    early = attend(0, known, q, keys, values, bounds)
    trips = (jnp.maximum(most + 2 * PAD - room, 0) + trip - 1) // trip
    more, early = lax.optimization_barrier((more, early))

    def one_trip(index, late):
        piece = cross(lax.dynamic_slice(rest, (index * trip, 0), (trip, rest.shape[1])))
        return lax.dynamic_update_slice(late, piece, (index * trip, 0))

    late = lax.fori_loop(0, trips, one_trip, jnp.zeros_like(rest))
    return give_back(attend(1, known, q, keys, values, bounds, more, late, early), group)


def solution(mesh):
    in_specs = (
        P("dp", "seq", None),
        P("dp", "seq", None),
        P("dp", "seq", None),
        P("dp", "seq"),
        P("dp", "seq"),
    )
    out_specs = P("dp", "seq", None)
    return jax.shard_map(whole, mesh=mesh, in_specs=in_specs, out_specs=out_specs, check_vma=False)
```

time: 215 us -> 189 us (0.88)
  blocking collectives: 34.6 us -> 5.8 us
  waiting for transfers between devices: 29.1 us -> 0.47 us
  Pallas kernels: 126 us -> 154 us
  local copies, waits for them, and re-layouts: 5.46 us -> 9.85 us
  starting transfers between devices: 7.65 us -> 4.21 us
  other arithmetic: 6.97 us -> 10.1 us
    all_to_all x1 -> x0, blocking collectives: 29.2 us -> none  [exchange(): lax.all_to_all(block, 'seq', split_axis=0, concat_axis=0, axis_index_grou...]
    all_to_all x1, waiting for transfers between devices: 29.1 us -> 0.47 us  [whole(): lax.all_to_all(q_packed, 'seq', split_axis=0, concat_axis=0, axis_index_g...]
    pallas_call x1, Pallas kernels: 34 us -> 56.5 us  [gather(): pl.pallas_call(functools.partial(gather_kernel, group), grid=(rows,), in_...]
    pallas_call x0 -> x1, Pallas kernels: none -> 8.63 us  [prepare(): pl.pallas_call(prepare_kernel, grid_spec=pltpu.PrefetchScalarGridSpec(num...]
    pallas_call x2, Pallas kernels: 63.1 us -> 56.6 us  [attend(): pl.pallas_call(functools.partial(attend_kernel, mode), grid_spec=pltpu.Pr...]
    unnamed x11 -> x17, local copies, waits for them, and re-layouts: 3.38 us -> 6.47 us
    ppermute x2 -> x1, starting transfers between devices: 3.03 us -> 0.46 us  [cross(): lax.ppermute(block, 'seq', [(i, (i + half) % group) for i in range(group)])]
    pallas_call x2 -> x1, Pallas kernels: 4.54 us -> 6.06 us  [pack(): pl.pallas_call(pack_kernel, grid_spec=pltpu.PrefetchScalarGridSpec(num_sc...]
  transfers between devices with their start and end apart: 3 -> 2, of which waited for: 1 -> 1; matrix products, arithmetic and copies ran while one was open for 3% -> 8% of each run, Pallas kernels for 22% -> 29%
where the time goes in v3:
time: 189 us; the launch traced here: 187 us
  Pallas kernels  154 us (81%)
  other arithmetic  10.1 us (5%)
  local copies, waits for them, and re-layouts  9.85 us (5%)
  blocking collectives  5.8 us (3%)
  starting transfers between devices  4.21 us (2%)
  between operations  2.12 us (1%)
    pallas_call x2, Pallas kernels, attend(): pl.pallas_call(functools.partial(attend_kernel, mode), grid_spec=pltpu.Pr...  56.6 us
    pallas_call x1, Pallas kernels, gather(): pl.pallas_call(functools.partial(gather_kernel, group), grid=(rows,), in_...  56.5 us
    pallas_call x1, Pallas kernels, give_back(): pl.pallas_call(functools.partial(give_back_kernel, group), in_specs=[pl.B...  26.2 us
    pallas_call x1, Pallas kernels, prepare(): pl.pallas_call(prepare_kernel, grid_spec=pltpu.PrefetchScalarGridSpec(num...  8.63 us
    unnamed x17, local copies, waits for them, and re-layouts  6.47 us
    pallas_call x1, Pallas kernels, pack(): pl.pallas_call(pack_kernel, grid_spec=pltpu.PrefetchScalarGridSpec(num_sc...  6.06 us
    pmax x1, blocking collectives, whole(): most = lax.pmax(most, 'dp')  5.8 us
    reduce_sum x2, other arithmetic, tables(): jnp.sum(ids[:, None, :] < numbers, axis=2)  5.54 us
  transfers between devices with their start and end apart: 2, of which 1 were waited for; matrix products, arithmetic and copies ran while one was open for 8% of the time, Pallas kernels for 29%

profile of v3, /device:TPU:0, one launch (start us, length us, event | category | flops | bytes accessed | tf_op | source)
XLA Modules:
  0.0 186.7 jit_solution(14999783398979895937)
XLA Ops:
  0.0 56.5 %shard_map.55 = (bf16[4,8,256,128]{3,2,1,0:T(8,128)(2,1)}, bf16[4,8,256,128]{3,2,1,0:T(8,128)(2,1)}, s32[8,8,256]{2,1,0:T(8,128)}, s32[8,8,256]{2,1,0:T(8,128)}, bf16[4,8,256,128]{3,2,1,0:T(8,128)(2,1)}) custom-call(bf16[8,256,512]{2,1,0:T(8,128)(2,1)} %k_ref.1, bf16[8,256,512]{2,1,0:T(8,128)(2,1)} %v_ref.1, s32[8,256]{1,0:T(8,128)} %dec_ref.1, ...), custom_call_target="tpu_custom_call" | custom-call | tf_op jit(solution)/shard_map/pallas_call | solution.py:113
  56.5 3.8 %all-to-all-start = ((bf16[4,8,256,128]{3,2,1,0:T(8,128)(2,1)}), bf16[4,8,256,128]{3,2,1,0:T(8,128)(2,1)S(1)}, u32[]{:S(2)}, u32[]{:S(2)}) async-start(bf16[4,8,256,128]{3,2,1,0:T(8,128)(2,1)} %get-tuple-element.41), calls=%async_computation | async-start | bytes 4194304 | tf_op jit(solution)/shard_map/all_to_all | solution.py:442
  60.9 0.3 convert_reduce_fusion.5
  61.8 0.6 pad_add_fusion.3.table_ref
  62.4 6.1 %shard_map.57 = (bf16[2816,256]{1,0:T(8,128)(2,1)}, bf16[5632,256]{1,0:T(8,128)(2,1)}) custom-call(s32[3,8]{1,0:T(4,128)} %pad_add_fusion.3.table_ref, bf16[4,8,256,128]{3,2,1,0:T(8,128)(2,1)} %get-tuple-element.42.k_ref, bf16[4,8,256,128]{3,2,1,0:T(8,128)(2,1)} %get-tuple-element.43.v_ref), custom_call_target="tpu_custom_call" | custom-call | flops 2000000 | bytes 8388608 | tf_op jit(solution)/shard_map/pallas_call | solution.py:199
  68.4 0.5 collective-permute-start.1
  68.9 1.3 multiply_reduce_fusion.1
  70.3 0.6 multiply_reduce_fusion
  72.2 5.8 %pmax.7 = s32[]{:T(128)} all-reduce(s32[]{:T(128)S(6)} %max.68), channel_id=1, replica_groups=mesh['dp'=4,'seq'=8] {'dp'}, use_global_device_ids=true, to_apply=%region_10.11 | all-reduce | flops 1 | bytes 8 | tf_op jit(solution)/shard_map/pmax | solution.py:451
  78.0 1.3 slice.26
  80.0 0.7 copy.23
  80.8 0.6 subtract_minimum_fusion
  81.4 1.4 concatenate.11.table_ref
  82.8 2.8 %convert_reduce_fusion.3 = (s32[8,128]{1,0:T(8,128)S(1)}, s32[8,128]{1,0:T(8,128)S(1)}) fusion(s32[8,2048]{1,0:T(8,128)} %bitcast.33), kind=kLoop, calls=%fused_computation.8 | loop fusion | flops 12580864 | bytes 73728 | tf_op jit(solution)/shard_map/reduce_sum | solution.py:405
  85.5 2.8 %convert_reduce_fusion.1 = (s32[8,128]{1,0:T(8,128)S(1)}, s32[8,128]{1,0:T(8,128)S(1)}) fusion(s32[8,2048]{1,0:T(8,128)} %bitcast.35), kind=kLoop, calls=%fused_computation.4 | loop fusion | flops 12580864 | bytes 73728 | tf_op jit(solution)/shard_map/reduce_sum | solution.py:405
  88.3 0.6 pad_add_fusion.bounds_ref
  88.9 8.6 %shard_map.56 = (bf16[8,1024,256]{2,1,0:T(8,128)(2,1)}, bf16[8,128,1024]{2,1,0:T(8,128)(2,1)}) custom-call(s32[8,14]{1,0:T(8,128)} %concatenate.11.table_ref, bf16[4,8,256,128]{3,2,1,0:T(8,128)(2,1)} %get-tuple-element.42.k_ref, bf16[4,8,256,128]{3,2,1,0:T(8,128)(2,1)} %get-tuple-element.43.v_ref, s32[8,4,128]{2,1,0:T(4,128)} %pad_add_fusion.bounds_ref), custom_call_target="tpu_custom_call" | custom-call | flops 2000000 | bytes 10485760 | tf_op jit(solution)/shard_map/pallas_call | solution.py:237
  97.5 0.5 all-to-all-done.q_ref
  98.0 1.3 copy-done
  99.3 40.2 %shard_map.58.rest_2_ = bf16[4,8,256,128]{3,2,1,0:T(8,128)(2,1)} custom-call(s32[8,14]{1,0:T(8,128)} %concatenate.11.table_ref, bf16[4,8,256,128]{3,2,1,0:T(8,128)(2,1)} %copy-done, bf16[8,1024,256]{2,1,0:T(8,128)(2,1)} %get-tuple-element.44.keys_ref, bf16[8,128,1024]{2,1,0:T(8,128)(2,1)} %get-tuple-element.45.values_ref, s32[8,4,128]{2,1,0:T(4,128)} %pad_add_fusion.bounds_ref), custom_call_target="tpu_custom_call" | custom-call | flops 2147483648 | bytes 8388608 | tf_op jit(solution)/shard_map/pallas_call | solution.py:383
  139.6 1.1 copy-done.1
  141.1 16.3 %shard_map.59.o_ref = bf16[4,8,256,128]{3,2,1,0:T(8,128)(2,1)} custom-call(s32[8,14]{1,0:T(8,128)} %concatenate.11.table_ref, bf16[4,8,256,128]{3,2,1,0:T(8,128)(2,1)} %copy-done, bf16[8,1024,256]{2,1,0:T(8,128)(2,1)} %get-tuple-element.44.keys_ref, bf16[8,128,1024]{2,1,0:T(8,128)(2,1)} %get-tuple-element.45.values_ref, ...), custom_call_target="tpu_custom_call" | custom-call | flops 536870912 | bytes 8388608 | tf_op jit(solution)/shard_map/pallas_call | solution.py:383
  157.4 26.2 %shard_map.60 = bf16[8,256,512]{2,1,0:T(8,128)(2,1)} custom-call(bf16[4,8,256,128]{3,2,1,0:T(8,128)(2,1)} %shard_map.59.o_ref), custom_call_target="tpu_custom_call" | custom-call | tf_op jit(solution)/shard_map/pallas_call | solution.py:159
  183.6 3.0 %copy.35 = bf16[8,256,512]{2,1,0:T(8,128)(2,1)} copy(bf16[8,256,512]{2,1,0:T(8,128)(2,1)} %shard_map.60) | data formatting | bytes 4194304
  (36 shorter events, 1.6 us)
Async XLA Ops:
  56.5 3.8 %copy-start.3 = (s32[8,8,256]{2,1,0:T(8,128)S(1)}, s32[8,8,256]{2,1,0:T(8,128)}, u32[]{:S(2)}) copy-start(s32[8,8,256]{2,1,0:T(8,128)} %get-tuple-element.40) | copy-start | bytes 196612
  56.5 4.4 %copy-start.2 = (s32[8,8,256]{2,1,0:T(8,128)S(1)}, s32[8,8,256]{2,1,0:T(8,128)}, u32[]{:S(2)}) copy-start(s32[8,8,256]{2,1,0:T(8,128)} %get-tuple-element.39) | copy-start | bytes 196612
  56.5 41.5 %all-to-all-start = ((bf16[4,8,256,128]{3,2,1,0:T(8,128)(2,1)}), bf16[4,8,256,128]{3,2,1,0:T(8,128)(2,1)S(1)}, u32[]{:S(2)}, u32[]{:S(2)}) async-start(bf16[4,8,256,128]{3,2,1,0:T(8,128)(2,1)} %get-tuple-element.41), calls=%async_computation | async-start | bytes 4194304 | tf_op jit(solution)/shard_map/all_to_all | solution.py:442
  61.2 7.2 %copy-start.4 = (s32[8,5]{0,1:T(8,128)}, s32[8,5]{0,1:T(8,128)S(1)}, u32[]{:S(2)}) copy-start(s32[8,5]{0,1:T(8,128)S(1)} %get-tuple-element.55) | copy-start | bytes 484
  61.6 7.3 %copy-start.5 = (s32[8]{0:T(128)}, s32[8]{0:T(128)S(1)}, u32[]{:S(2)}) copy-start(s32[8]{0:T(128)S(1)} %get-tuple-element.59) | copy-start | bytes 100
  68.4 71.1 %collective-permute-start.1 = (bf16[2816,256]{1,0:T(8,128)(2,1)}, bf16[2816,256]{1,0:T(8,128)(2,1)S(1)}, u32[]{:S(2)}, u32[]{:S(2)}) collective-permute-start(bf16[2816,256]{1,0:T(8,128)(2,1)} %get-tuple-element.46), channel_id=1, source_target_pairs={{0,4},{1,5},{2,6},{3,7},{4,0},{5,1},{6,2},{7,3},{8,12},{9,13},{10,... | collective-permute-start | bytes 4325384 | tf_op jit(solution)/shard_map/ppermute | solution.py:440
  98.0 1.3 copy-start
  139.6 1.1 copy-start.1

commit v4 on v3

v4 whole, which is shorter than its diff:
```python
import functools

import jax
import jax.numpy as jnp
from jax import lax
from jax.experimental import pallas as pl
from jax.experimental.pallas import tpu as pltpu
from jax.sharding import PartitionSpec as P


HEAD_DIM = 64
TALL = 80
DOCS = 16
LANES = 128
SPAN = 256
STRIDE = 512
PIECE = 32
TOGETHER = 4
MIB = 2**20
MASKED = -8192.0
ROOM = 11
TRIP = 512


def peer(me, shift, half):
    base = me // half * half
    return base + lax.rem(me - base + shift, half)


def greet(others):
    barrier = pltpu.get_barrier_semaphore()
    for target in others:
        pl.semaphore_signal(barrier, inc=1, device_id={"seq": target}, device_id_type=pl.DeviceIdType.MESH)
    pl.semaphore_wait(barrier, len(others))


def remote(src, dst, send_sem, recv_sem, target):
    return pltpu.make_async_remote_copy(
        src_ref=src,
        dst_ref=dst,
        send_sem=send_sem,
        recv_sem=recv_sem,
        device_id={"seq": target},
        device_id_type=pl.DeviceIdType.MESH,
    )


def gather_kernel(
    group, k_ref, v_ref, dec_ref, enc_ref, q_ref, k_out, v_out, dec_out, enc_out, q_out, held, ids_held, own_sem, ids_sem, send_sem, recv_sem, ids_send, ids_recv
):
    me = lax.axis_index("seq")
    half = group // 2
    width = k_out.shape[3]
    place = lax.rem(me, half)
    large = ((0, k_ref, k_out), (1, v_ref, v_out))
    small = ((0, dec_ref, dec_out), (1, enc_ref, enc_out))

    def columns(src, target):
        return src.at[:, :, pl.ds(pl.multiple_of(lax.rem(target, half) * width, LANES), width)]

    def heads(shift, slot, src, dst):
        target = peer(me, shift, half)
        at = slot * (half - 1) + shift - 1
        return remote(columns(src, target), dst.at[place], send_sem.at[at], recv_sem.at[at], target)

    def ids(shift, slot, src, dst):
        at = slot * (group - 1) + shift - 1
        return remote(src, dst.at[me], ids_send.at[at], ids_recv.at[at], lax.rem(me + shift, group))

    @pl.when(pl.program_id(0) == 0)
    def _():
        greet([lax.rem(me + shift, group) for shift in range(1, group)])
        for shift in range(1, group):
            for each in small:
                ids(shift, *each).start()
        for each in large:
            for shift in range(half - 1, 0, -1):
                heads(shift, *each).start()
        own = [pltpu.make_async_copy(columns(src, me), held.at[slot], own_sem.at[slot]) for slot, src, _ in large]
        own += [pltpu.make_async_copy(src, ids_held.at[slot], ids_sem.at[slot]) for slot, src, _ in small]
        for copy in own:
            copy.start()
        for copy in own:
            copy.wait()
        own = [pltpu.make_async_copy(held.at[slot], dst.at[place], own_sem.at[slot]) for slot, _, dst in large]
        own += [pltpu.make_async_copy(ids_held.at[slot], dst.at[me], ids_sem.at[slot]) for slot, _, dst in small]
        for copy in own:
            copy.start()
        for copy in own:
            copy.wait()

    for target in range(half):
        q_out[target, 0] = q_ref[0, :, target * width : (target + 1) * width]

    @pl.when(pl.program_id(0) == pl.num_programs(0) - 1)
    def _():
        for shift in range(1, group):
            for each in small:
                ids(shift, *each).wait()
        for each in large:
            for shift in range(1, half):
                heads(shift, *each).wait()


def gather(q, k, v, dec_ids, enc_ids, group):
    rows, count, features = k.shape
    half = group // 2
    width = features // half
    anywhere = pl.BlockSpec(memory_space=pltpu.HBM)
    block = pl.BlockSpec((1, count, features), lambda r: (r, 0, 0))
    packed = pl.BlockSpec((half, 1, count, width), lambda r: (0, r, 0, 0))
    spread = jax.ShapeDtypeStruct((half, rows, count, width), k.dtype)
    every = jax.ShapeDtypeStruct((group, rows, count), dec_ids.dtype)
    dma = pltpu.SemaphoreType.DMA
    return pl.pallas_call(
        functools.partial(gather_kernel, group),
        grid=(rows,),
        in_specs=[anywhere] * 4 + [block],
        out_specs=[anywhere] * 4 + [packed],
        out_shape=[spread, spread, every, every, spread],
        scratch_shapes=[
            pltpu.VMEM((2, rows, count, width), k.dtype),
            pltpu.VMEM((2, rows, count), dec_ids.dtype),
            dma((2,)),
            dma((2,)),
            dma((2 * (half - 1),)),
            dma((2 * (half - 1),)),
            dma((2 * (group - 1),)),
            dma((2 * (group - 1),)),
        ],
        compiler_params=pltpu.CompilerParams(collective_id=0, has_side_effects=True),
    )(k, v, dec_ids, enc_ids, q)


def give_back_kernel(group, o_ref, out_ref, held, own_sem, send_sem, recv_sem):
    me = lax.axis_index("seq")
    half = group // 2
    width = o_ref.shape[3]
    place = lax.rem(me, half)
    columns = out_ref.at[:, :, pl.ds(pl.multiple_of(place * width, LANES), width)]

    def transfer(shift):
        target = peer(me, shift, half)
        return remote(o_ref.at[lax.rem(target, half)], columns, send_sem.at[shift - 1], recv_sem.at[shift - 1], target)

    greet([peer(me, shift, half) for shift in range(1, half)])
    for shift in range(half - 1, 0, -1):
        transfer(shift).start()
    own = pltpu.make_async_copy(o_ref.at[place], held, own_sem)
    own.start()
    own.wait()
    own = pltpu.make_async_copy(held, columns, own_sem)
    own.start()
    own.wait()
    for shift in range(1, half):
        transfer(shift).wait()


def give_back(o, group):
    half, rows, count, width = o.shape
    return pl.pallas_call(
        functools.partial(give_back_kernel, group),
        in_specs=[pl.BlockSpec(memory_space=pltpu.HBM)],
        out_specs=pl.BlockSpec(memory_space=pltpu.HBM),
        out_shape=jax.ShapeDtypeStruct((rows, count, half * width), o.dtype),
        scratch_shapes=[
            pltpu.VMEM((rows, count, width), o.dtype),
            pltpu.SemaphoreType.DMA,
            pltpu.SemaphoreType.DMA((half - 1,)),
            pltpu.SemaphoreType.DMA((half - 1,)),
        ],
        compiler_params=pltpu.CompilerParams(collective_id=1, has_side_effects=True),
    )(o)


def pack_kernel(table_ref, shift_ref, k_ref, v_ref, o_ref):
    _, rows, count, width = k_ref.shape
    room = o_ref.shape[0]
    o_ref[...] = jnp.zeros(o_ref.shape, o_ref.dtype)

    def one_row(row, carry):
        offset, start, amount = table_ref[0, row] - shift_ref[0], table_ref[1, row], table_ref[2, row]

        def one(index):
            at = start + index * PIECE
            slab, inside = at // count, pl.ds(pl.multiple_of(at % count, PIECE), PIECE)
            into = pl.ds(pl.multiple_of(offset + index * PIECE, PIECE), PIECE)
            o_ref[into, :width] = k_ref[slab, row, inside, :]
            o_ref[into, width:] = v_ref[slab, row, inside, :]

        def move(index, carry):
            one(index)
            return carry

        def several(index, carry):
            for more in range(TOGETHER):
                one(lowest + index * TOGETHER + more)
            return carry

        lowest = jnp.maximum(-offset, 0) // PIECE
        highest = jnp.maximum(jnp.minimum(amount, room - offset) // PIECE, lowest)
        times = (highest - lowest) // TOGETHER
        lax.fori_loop(0, times, several, 0)
        return lax.fori_loop(lowest + times * TOGETHER, highest, move, carry)

    lax.fori_loop(0, rows, one_row, 0)


def pack(table, shift, k, v, room):
    width = k.shape[3]
    small, inside = pl.BlockSpec(memory_space=pltpu.SMEM), pl.BlockSpec(memory_space=pltpu.VMEM)
    return pl.pallas_call(
        pack_kernel,
        in_specs=[small] * 2 + [inside] * 2,
        out_specs=inside,
        out_shape=jax.ShapeDtypeStruct((room, 2 * width), k.dtype),
        cost_estimate=pl.CostEstimate(flops=2000000, bytes_accessed=8 * k.size, transcendentals=0),
    )(table, shift, k, v)


def within(low, high, at, amount):
    position = at + lax.broadcasted_iota(jnp.int32, (amount, LANES), 0)
    return (position >= low) & (position < high)


def missing(low, high, at, amount):
    documents = lax.broadcasted_iota(jnp.int32, (amount, LANES), 1)
    return jnp.where(within(low, high, at, amount) | (documents >= DOCS), 0.0, MASKED).astype(jnp.bfloat16)


def tall_values(turned):
    ones = jnp.ones((TALL - HEAD_DIM, turned.shape[1]), turned.dtype)
    return [jnp.concatenate([turned[at : at + HEAD_DIM], ones], axis=0) for at in range(0, turned.shape[0], HEAD_DIM)]


def prepare_kernel(table_ref, k_ref, v_ref, bounds_ref, keys, values, hot, _):
    half, _, count, width = k_ref.shape
    length = half * count
    first = table_ref[0, table_ref.shape[1] - 1] * length
    bounds = bounds_ref[0]
    keys[0, :, :width] = k_ref[:, 0].reshape(length, width)
    keys[0, :, width:] = missing(bounds[0:1], bounds[1:2], first, length)
    for head, part in enumerate(tall_values(v_ref[:, 0].reshape(length, width).T)):
        values[0, head * TALL : (head + 1) * TALL] = part
    here = jnp.where(within(bounds[2:3], bounds[3:4], first, length), 1.0, 0.0).astype(jnp.bfloat16).T
    hot[0] = here[:DOCS]


def prepare(table, k, v, bounds, extra):
    half, rows, count, width = k.shape
    length = half * count
    row_block = pl.BlockSpec((half, 1, count, width), lambda r, *_: (0, r, 0, 0))
    shapes = [(length, width + LANES), (width // HEAD_DIM * TALL, length), (DOCS, length)]
    return pl.pallas_call(
        prepare_kernel,
        grid_spec=pltpu.PrefetchScalarGridSpec(
            num_scalar_prefetch=1,
            grid=(rows,),
            in_specs=[row_block, row_block, pl.BlockSpec((1, *bounds.shape[1:]), lambda r, *_: (r, 0, 0))],
            out_specs=[pl.BlockSpec((1, *shape), lambda r, *_: (r, 0, 0)) for shape in shapes]
            + [pl.BlockSpec(memory_space=pltpu.HBM)],
        ),
        out_shape=[jax.ShapeDtypeStruct((rows, *shape), k.dtype) for shape in shapes]
        + [jax.ShapeDtypeStruct((extra, 2 * width), k.dtype)],
        cost_estimate=pl.CostEstimate(flops=2000000, bytes_accessed=10 * k.size, transcendentals=0),
    )(table, k, v, bounds)


def attend_kernel(mode, table_ref, *refs):
    if mode:
        trips_ref, bounds_ref, q_from, hot_from, peak_from, sum_from, more_from, late_from, _, o_to, *scratch = refs
        items, even, odd, even_peak, odd_peak, peak_of, sum_of, peak_now, sum_now, q_ref, hot_ref, o_ref, more_ref, sem = scratch
    else:
        q_ref, keys, values, hot_ref, o_ref, peak_of, sum_of, items, even, odd, even_peak, odd_peak = refs
    half, rows, count, width = q_ref.shape
    length = half * count
    heads = width // HEAD_DIM
    _, stride, span = even.shape
    slabs = span // count
    blocks = length // span
    side = table_ref[0, 4 * blocks + 1]

    def entry(row, kind, block):
        return table_ref[row, kind * blocks + block]

    def each_block(do):
        def one(number, carry):
            row, block = number // blocks, number % blocks

            @pl.when(entry(row, 3, block) > 0)
            def _():
                do(number, row, pl.ds(block * slabs, slabs))

            return carry

        lax.fori_loop(0, rows * blocks, one, 0)

    if mode:
        room = more_from.shape[0]
        avail = room + trips_ref[0] * trips_ref[1]

        def move(finish):
            def block(number, row, slab):
                for src, dst in (
                    (q_from.at[slab, row], q_ref.at[slab, row]),
                    (peak_from.at[number], peak_of.at[number]),
                    (sum_from.at[number], sum_of.at[number]),
                ):
                    copy = pltpu.make_async_copy(src, dst, sem)
                    copy.wait() if finish else copy.start()

            for src, dst in ((more_from, more_ref.at[pl.ds(0, room)]), (hot_from, hot_ref)):
                copy = pltpu.make_async_copy(src, dst, sem)
                copy.wait() if finish else copy.start()
            each_block(block)

        move(False)

    def list_block(number, total):
        row, block = number // blocks, number % blocks
        steps = entry(row, 2 * mode + 1, block)
        low = entry(row, 2 * mode, block)
        if mode:
            low = jnp.minimum(low, avail - steps * stride)
        else:

            @pl.when(steps == 0)
            def _():
                peak_of[number] = jnp.full(peak_of.shape[1:], 4 * MASKED, jnp.float32)
                sum_of[number] = jnp.zeros(sum_of.shape[1:], jnp.float32)

        def list_step(index, total):
            items[0, total] = row
            items[1, total] = block
            items[2, total] = low + index * stride
            items[3, total] = (index == 0).astype(jnp.int32)
            return total + 1

        return lax.fori_loop(0, steps, list_step, total)

    total = lax.fori_loop(0, rows * blocks, list_block, jnp.int32(1))
    if mode:

        @pl.when(trips_ref[0] > 0)
        def _():
            pltpu.sync_copy(late_from, more_ref.at[pl.ds(room, late_from.shape[0])])

        move(True)

    def score(index, scores, peaks):
        row, block = items[0, index], items[1, index]
        query = q_ref[pl.ds(block * slabs, slabs), row].reshape(span, width).T
        here = hot_ref[row, :, pl.ds(pl.multiple_of(block * span, span), span)]
        owner = lax.broadcasted_iota(jnp.int32, (width, span), 0) // HEAD_DIM
        nothing = jnp.zeros((LANES - DOCS, span), jnp.bfloat16)
        if mode:
            start = pl.multiple_of(items[2, index], PIECE)
            low, high = bounds_ref[row, 0:1], bounds_ref[row, 1:2]
            low = jnp.where(side == 0, jnp.maximum(low, length), low)
            high = jnp.where(side == 0, high, jnp.minimum(high, length))
            miss = missing(low, high, start - table_ref[row, 4 * blocks], stride)
            key = jnp.concatenate([more_ref[pl.ds(start, stride), :width], miss], axis=1)
        else:
            start = pl.multiple_of(items[2, index], LANES)
            key = keys[row, pl.ds(start, stride), :]
        for head in range(heads):
            one = jnp.where(owner == head, query, jnp.zeros_like(query))
            result = jnp.dot(key, jnp.concatenate([one, here, nothing], axis=0), preferred_element_type=jnp.float32)
            scores[head] = result
            peaks[head] = jnp.max(result, axis=0, keepdims=True)

    def weigh(index, scores, peaks):
        row, block = items[0, index], items[1, index]
        number, fresh_start = row * blocks + block, items[3, index] == 1
        if mode:
            start = pl.multiple_of(items[2, index], PIECE)
            value = tall_values(more_ref[pl.ds(start, stride), width:].T)
        else:
            start = pl.multiple_of(items[2, index], LANES)
            value = [values[row, head * TALL : (head + 1) * TALL, pl.ds(start, stride)] for head in range(heads)]
        now, at = ((peak_now, sum_now), 0) if mode else ((peak_of, sum_of), number)
        done = []
        for head in range(heads):
            peak, before = (x[at, head] for x in now)
            began = (peak_of[number, head], sum_of[number, head]) if mode else (4 * MASKED, 0.0)
            peak, before = jnp.where(fresh_start, began[0], peak), jnp.where(fresh_start, began[1], before)
            fresh = jnp.maximum(peak, peaks[head])
            now[0][at, head] = fresh
            expos = jnp.exp(scores[head] - fresh).astype(jnp.bfloat16)
            summed = before * jnp.exp(peak - fresh) + jnp.dot(value[head], expos, preferred_element_type=jnp.float32)
            now[1][at, head] = summed
            done.append(summed[:HEAD_DIM] / summed[HEAD_DIM : HEAD_DIM + 1])
        whole = jnp.concatenate(done, axis=0).T.astype(jnp.bfloat16)
        o_ref[pl.ds(block * slabs, slabs), row] = whole.reshape(slabs, count, width)

    @pl.when(total > 1)
    def _():
        begin = total % 2
        for field in range(4):
            items[field, 0] = items[field, 1]
        score(begin, even, even_peak)

        def pair(index, carry):
            at = begin + 2 * index
            score(at + 1, odd, odd_peak)
            weigh(at, even, even_peak)
            score(jnp.minimum(at + 2, total - 1), even, even_peak)
            weigh(at + 1, odd, odd_peak)
            return carry

        lax.fori_loop(0, (total - begin) // 2, pair, 0)

    if mode:

        def put(finish):
            def block(number, row, slab):
                copy = pltpu.make_async_copy(o_ref.at[slab, row], o_to.at[slab, row], sem)
                copy.wait() if finish else copy.start()

            each_block(block)

        put(False)
        put(True)


def attend(mode, table, q, *more):
    half, rows, count, width = q.shape
    length = half * count
    heads = width // HEAD_DIM
    span = max(SPAN, count)
    stride = min(STRIDE, length)
    small = pl.BlockSpec(memory_space=pltpu.SMEM)
    inside = pl.BlockSpec(memory_space=pltpu.VMEM)
    outside = pl.BlockSpec(memory_space=pltpu.HBM)
    numbers = rows * (length // span)
    state = [(numbers, heads, 1, span), (numbers, heads, TALL, span)]
    scratch = [
        pltpu.SMEM((4, numbers * (2 * length // stride + 1) + 1), jnp.int32),
        pltpu.VMEM((heads, stride, span), jnp.float32),
        pltpu.VMEM((heads, stride, span), jnp.float32),
        pltpu.VMEM((heads, 1, span), jnp.float32),
        pltpu.VMEM((heads, 1, span), jnp.float32),
    ]
    shapes = [jax.ShapeDtypeStruct(q.shape, q.dtype)]
    if mode:
        trips, bounds, hot, peak, summed, cross, late, early = more
        scratch += [pltpu.VMEM(shape, jnp.float32) for shape in state + [(1, *shape[1:]) for shape in state]]
        scratch += [
            pltpu.VMEM(q.shape, q.dtype),
            pltpu.VMEM(hot.shape, q.dtype),
            pltpu.VMEM(q.shape, q.dtype),
            pltpu.VMEM((cross.shape[0] + late.shape[0], 2 * width), q.dtype),
            pltpu.SemaphoreType.DMA,
        ]
        args = (table, trips, bounds, q, hot, peak, summed, cross, late, early)
        specs, out_specs = [small] * 2 + [inside] + [outside] * 7, [outside]
    else:
        keys, values, hot = more
        args = (table, q, keys, values, hot)
        specs, out_specs = [small] + [inside] * 4, [inside] * 3
        shapes += [jax.ShapeDtypeStruct(shape, jnp.float32) for shape in state]
    share = 4 if mode else 1
    return pl.pallas_call(
        functools.partial(attend_kernel, mode),
        in_specs=specs,
        out_specs=out_specs,
        out_shape=shapes,
        input_output_aliases={9: 0} if mode else {},
        scratch_shapes=scratch,
        compiler_params=pltpu.CompilerParams(vmem_limit_bytes=60 * MIB),
        cost_estimate=pl.CostEstimate(
            flops=rows * heads * length * length * 128 // share,
            bytes_accessed=8 * rows * width * length,
            transcendentals=rows * length * length // 4 // share,
        ),
    )(*args)


def tables(dec_rows, enc_rows, side):
    rows, whole = dec_rows.shape
    length = whole // 2
    blocks = length // SPAN
    stride = min(STRIDE, length)
    numbers = jnp.arange(LANES, dtype=jnp.int32)[None, :, None]
    bounds = []
    for ids in (enc_rows, dec_rows):
        bounds += [jnp.sum(ids[:, None, :] < numbers, axis=2), jnp.sum(ids[:, None, :] <= numbers, axis=2)]
    bounds = jnp.stack(bounds, axis=1).astype(jnp.int32)
    mine = lax.dynamic_slice(dec_rows, (0, side * length), (rows, length))
    docs = mine.reshape(rows, blocks, SPAN)
    starts = jnp.concatenate([docs[:, :, 0], dec_rows[:, length : length + 1]], axis=1)
    ends = jnp.concatenate([docs[:, :, -1], dec_rows[:, length - 1 : length]], axis=1)
    before = jnp.sum(enc_rows[:, None, :] < starts[:, :, None], axis=2, dtype=jnp.int32)
    upto = jnp.sum(enc_rows[:, None, :] <= ends[:, :, None], axis=2, dtype=jnp.int32)
    up = jnp.maximum(length - before[:, blocks], 0)
    down = jnp.maximum(upto[:, blocks] - length, 0)
    up, down = (-(-amount // PIECE) * PIECE for amount in (up, down))
    before, upto = before[:, :blocks], upto[:, :blocks]
    sent, got = jnp.where(side == 0, up, down), jnp.where(side == 0, down, up)
    offset_of = [jnp.cumsum(amount) - amount for amount in (sent, got)]
    first = jnp.where(side == 0, length - sent, 0)
    send = jnp.stack([offset_of[0], first, sent])
    base = (offset_of[1] - jnp.where(side == 0, length, length - got))[:, None]
    home = side * length
    near, far = jnp.maximum(before - home, 0), jnp.minimum(upto - home, length)
    low = near // LANES * LANES
    steps = jnp.where(far > near, (far - low + stride - 1) // stride, 0)
    low = jnp.minimum(low, length - steps * stride)
    near = base + jnp.where(side == 0, jnp.maximum(before, length), before)
    far = base + jnp.where(side == 0, upto, jnp.minimum(upto, length))
    start = near // PIECE * PIECE
    more = jnp.where(far > near, (far - start + stride - 1) // stride, 0)
    known = jnp.concatenate([low, steps, start, more, base, jnp.full((rows, 1), side, jnp.int32)], axis=1)
    return send, known, bounds, jnp.maximum(jnp.sum(up), jnp.sum(down))


def whole(queries, enc_keys, enc_values, dec_ids, enc_ids):
    group = lax.axis_size("seq")
    half = group // 2
    rows, count, _ = queries.shape
    length = half * count
    side = lax.axis_index("seq") // half
    k, v, dec_all, enc_all, q_packed = gather(queries, enc_keys, enc_values, dec_ids, enc_ids, group)
    sides = [list(range(half)), list(range(half, group))]

    def cross(block):
        return lax.ppermute(block, "seq", [(i, (i + half) % group) for i in range(group)])

    q = lax.all_to_all(q_packed, "seq", split_axis=0, concat_axis=0, axis_index_groups=sides, tiled=True)
    dec_rows, enc_rows = (x.transpose(1, 0, 2).reshape(rows, 2 * length) for x in (dec_all, enc_all))
    send, known, bounds, most = tables(dec_rows, enc_rows, side)
    trip = min(TRIP, length)
    full = rows * length
    room = full * ROOM // 32 // LANES * LANES
    extra = -(-(full - room) // trip) * trip
    more = cross(pack(send, jnp.zeros((1,), jnp.int32), k, v, room))
    q = lax.all_to_all(q_packed, "seq", split_axis=0, concat_axis=0, axis_index_groups=sides, tiled=True)
    keys, values, hot, empty = prepare(known, k, v, bounds, extra)
    most = lax.pmax(most, "dp")
    early, peak, summed = attend(0, known, q, keys, values, hot)
    trips = (jnp.maximum(most - room, 0) + trip - 1) // trip
    more, early = lax.optimization_barrier((more, early))

    def one_trip(index, late):
        piece = cross(pack(send, jnp.full((1,), room + index * trip, jnp.int32), k, v, trip))
        return lax.dynamic_update_slice(late, piece, (index * trip, 0))

    late = lax.fori_loop(0, trips, one_trip, empty)
    sent_late = jnp.stack([trips, jnp.full_like(trips, trip)])
    out = attend(1, known, q, sent_late, bounds, hot, peak, summed, more, late, early)[0]
    return give_back(out, group)


def solution(mesh):
    in_specs = (
        P("dp", "seq", None),
        P("dp", "seq", None),
        P("dp", "seq", None),
        P("dp", "seq"),
        P("dp", "seq"),
    )
    out_specs = P("dp", "seq", None)
    return jax.shard_map(whole, mesh=mesh, in_specs=in_specs, out_specs=out_specs, check_vma=False)
```

time: 189 us -> 174 us (0.921)
  Pallas kernels: 154 us -> 129 us
  waiting for transfers between devices: 0.47 us -> 11.1 us
    pallas_call x3, Pallas kernels: 62.6 us -> 36.5 us  [the longest x2 32.8 us: attend(): pl.pallas_call(functools.partial(attend_kernel, mode), in_specs=specs, ou...]
    ppermute x1, waiting for transfers between devices: 0.01 us -> 9.12 us  [cross(): lax.ppermute(block, 'seq', [(i, (i + half) % group) for i in range(group)])]
    unnamed x17 -> x11, local copies, waits for them, and re-layouts: 6.47 us -> 6.39 us
  transfers between devices with their start and end apart: 2 -> 2, of which waited for: 1 -> 2; matrix products, arithmetic and copies ran while one was open for 8% -> 9% of each run, Pallas kernels for 29% -> 22%
where the time goes in v4:
time: 174 us; the launch traced here: 173 us
  Pallas kernels  129 us (74%)
  waiting for transfers between devices  11.1 us (6%)
  other arithmetic  10.9 us (6%)
  local copies, waits for them, and re-layouts  9.49 us (5%)
  blocking collectives  5.65 us (3%)
  starting transfers between devices  5.11 us (3%)
  between operations  2.14 us (1%)
    pallas_call x1, Pallas kernels, gather(): pl.pallas_call(functools.partial(gather_kernel, group), grid=(rows,), in_...  56.5 us
    pallas_call x2, Pallas kernels, attend(): pl.pallas_call(functools.partial(attend_kernel, mode), in_specs=specs, ou...  32.8 us
    pallas_call x1, Pallas kernels, give_back(): pl.pallas_call(functools.partial(give_back_kernel, group), in_specs=[pl.B...  27.6 us
    ppermute x1, waiting for transfers between devices, cross(): lax.ppermute(block, 'seq', [(i, (i + half) % group) for i in range(group)])  9.12 us
    pallas_call x1, Pallas kernels, prepare(): pl.pallas_call(prepare_kernel, grid_spec=pltpu.PrefetchScalarGridSpec(num...  8.17 us
    unnamed x11, local copies, waits for them, and re-layouts  6.39 us
    pmax x1, blocking collectives, whole(): most = lax.pmax(most, 'dp')  5.65 us
    reduce_sum x2, other arithmetic, tables(): jnp.sum(ids[:, None, :] < numbers, axis=2)  5.54 us
  transfers between devices with their start and end apart: 2, of which 2 were waited for; matrix products, arithmetic and copies ran while one was open for 9% of the time, Pallas kernels for 22%

profile of v4, /device:TPU:0, one launch (start us, length us, event | category | flops | bytes accessed | tf_op | source)
XLA Modules:
  0.0 173.1 jit_solution(12482726163468088682)
XLA Ops:
  0.0 56.5 %shard_map.55 = (bf16[4,8,256,128]{3,2,1,0:T(8,128)(2,1)S(1)}, bf16[4,8,256,128]{3,2,1,0:T(8,128)(2,1)}, s32[8,8,256]{2,1,0:T(8,128)}, s32[8,8,256]{2,1,0:T(8,128)}, bf16[4,8,256,128]{3,2,1,0:T(8,128)(2,1)}) custom-call(bf16[8,256,512]{2,1,0:T(8,128)(2,1)} %k_ref.1, bf16[8,256,512]{2,1,0:T(8,128)(2,1)} %v_ref.1, s32[8,256]{1,0:T(8,128)} %dec_ref.1, ...), custom_call_target="tpu_custom_call" | custom-call | tf_op jit(solution)/shard_map/pallas_call | solution.py:115
  56.5 4.6 %all-to-all-start = ((bf16[4,8,256,128]{3,2,1,0:T(8,128)(2,1)}), bf16[4,8,256,128]{3,2,1,0:T(8,128)(2,1)}, u32[]{:S(2)}, u32[]{:S(2)}) async-start(bf16[4,8,256,128]{3,2,1,0:T(8,128)(2,1)} %get-tuple-element.54), calls=%async_computation | async-start | bytes 4194304 | tf_op jit(solution)/shard_map/all_to_all | solution.py:537
  62.6 0.6 multiply_reduce_fusion.1
  63.2 0.7 multiply_reduce_fusion
  65.3 3.6 %shard_map.58 = bf16[2816,256]{1,0:T(8,128)(2,1)} custom-call(s32[3,8]{1,0:T(4,128)S(1)} %pad_add_fusion.3.table_ref, s32[1]{0:T(128)} %constant.133.clone.1.shift_ref, bf16[4,8,256,128]{3,2,1,0:T(8,128)(2,1)S(1)} %get-tuple-element.145.k_ref, bf16[4,8,256,128]{3,2,1,0:T(8,128)(2,1)} %get-tuple-element.146.v_ref), custom_call_target="tpu_custom_call" | custom-call | flops 2000000 | bytes 8388608 | tf_op jit(solution)/shard_map/pallas_call | solution.py:212
  69.5 5.7 %pmax.7 = s32[]{:T(128)} all-reduce(s32[]{:T(128)S(6)} %max.78), channel_id=1, replica_groups=mesh['dp'=4,'seq'=8] {'dp'}, use_global_device_ids=true, to_apply=%region_5.6 | all-reduce | flops 1 | bytes 8 | tf_op jit(solution)/shard_map/pmax | solution.py:539
  76.4 0.7 copy.25
  77.1 1.3 copy.24
  78.4 0.7 fusion.26
  79.1 1.4 subtract_minimum_fusion
  80.5 0.6 broadcast_in_dim.11
  81.1 1.4 concatenate.11.table_ref
  82.5 2.8 %convert_reduce_fusion.3 = (s32[8,128]{1,0:T(8,128)S(1)}, s32[8,128]{1,0:T(8,128)S(1)}) fusion(s32[8,2048]{1,0:T(8,128)} %bitcast.37), kind=kLoop, calls=%fused_computation.7 | loop fusion | flops 12580864 | bytes 73728 | tf_op jit(solution)/shard_map/reduce_sum | solution.py:487
  85.2 2.8 %convert_reduce_fusion.1 = (s32[8,128]{1,0:T(8,128)S(1)}, s32[8,128]{1,0:T(8,128)S(1)}) fusion(s32[8,2048]{1,0:T(8,128)} %bitcast.39), kind=kLoop, calls=%fused_computation.3 | loop fusion | flops 12580864 | bytes 73728 | tf_op jit(solution)/shard_map/reduce_sum | solution.py:487
  88.0 0.6 pad_add_fusion.bounds_ref.refs_1_
  88.6 8.2 %shard_map.56 = (bf16[8,1024,256]{2,1,0:T(8,128)(2,1)}, bf16[8,160,1024]{2,1,0:T(8,128)(2,1)}, bf16[8,16,1024]{2,1,0:T(8,128)(2,1)}, bf16[5632,256]{1,0:T(8,128)(2,1)}) custom-call(s32[8,18]{1,0:T(8,128)} %concatenate.11.table_ref, bf16[4,8,256,128]{3,2,1,0:T(8,128)(2,1)S(1)} %get-tuple-element.145.k_ref, bf16[4,8,256,128]{3,2,1,0:T(8,128)(2,1)} %get-tuple-element.146.v_ref, ...), custom_call_target="tpu_custom_call" | custom-call | flops 2000000 | bytes 10485760 | tf_op jit(solution)/shard_map/pallas_call | solution.py:254
  96.8 0.6 pad_add_fusion.4.refs_0_
  97.4 2.0 %all-to-all-done.refs_0_.refs_2_ = bf16[4,8,256,128]{3,2,1,0:T(8,128)(2,1)} async-done(((bf16[4,8,256,128]{3,2,1,0:T(8,128)(2,1)}), bf16[4,8,256,128]{3,2,1,0:T(8,128)(2,1)}, u32[]{:S(2)}, u32[]{:S(2)}) %all-to-all-start) | async-done | bytes 2097184 | tf_op jit(solution)/shard_map/all_to_all | solution.py:537
  99.4 25.8 %shard_map.57 = (bf16[4,8,256,128]{3,2,1,0:T(8,128)(2,1)}, f32[32,2,1,256]{3,2,1,0:T(1,128)}, f32[32,2,80,256]{3,2,1,0:T(8,128)}) custom-call(s32[8,18]{1,0:T(8,128)} %concatenate.11.table_ref, bf16[4,8,256,128]{3,2,1,0:T(8,128)(2,1)} %all-to-all-done.refs_0_.refs_2_, bf16[8,1024,256]{2,1,0:T(8,128)(2,1)} %get-tuple-element.58.refs_1_, ...), custom_call_target="tpu_custom_call" | custom-call | flops 2147483648 | bytes 8388608 | tf_op jit(solution)/shard_map/pallas_call | solution.py:463
  125.2 9.1 %collective-permute-done.1.refs_6_ = bf16[2816,256]{1,0:T(8,128)(2,1)S(1)} collective-permute-done((bf16[2816,256]{1,0:T(8,128)(2,1)}, bf16[2816,256]{1,0:T(8,128)(2,1)S(1)}, u32[]{:S(2)}, u32[]{:S(2)}) %collective-permute-start.1) | collective-permute-done | bytes 1441824 | tf_op jit(solution)/shard_map/ppermute | solution.py:527
  134.3 1.2 copy-done
  135.5 7.0 %shard_map.59.o_ref = bf16[4,8,256,128]{3,2,1,0:T(8,128)(2,1)} custom-call(s32[8,18]{1,0:T(8,128)} %concatenate.11.table_ref, s32[2]{0:T(128)} %pad_add_fusion.4.refs_0_, s32[8,4,128]{2,1,0:T(4,128)} %pad_add_fusion.bounds_ref.refs_1_, bf16[4,8,256,128]{3,2,1,0:T(8,128)(2,1)} %all-to-all-done.refs_0_.refs_2_, ...), custom_call_target="tpu_custom_call", output_to_operand_aliasing={{}: (9, {})} | custom-call | flops 536870912 | bytes 8388608 | tf_op jit(solution)/shard_map/pallas_call | solution.py:463
  142.5 27.6 %shard_map.60 = bf16[8,256,512]{2,1,0:T(8,128)(2,1)} custom-call(bf16[4,8,256,128]{3,2,1,0:T(8,128)(2,1)} %shard_map.59.o_ref), custom_call_target="tpu_custom_call" | custom-call | tf_op jit(solution)/shard_map/pallas_call | solution.py:161
  170.0 3.0 %copy.37 = bf16[8,256,512]{2,1,0:T(8,128)(2,1)} copy(bf16[8,256,512]{2,1,0:T(8,128)(2,1)} %shard_map.60) | data formatting | bytes 4194304
  (29 shorter events, 2.6 us)
Async XLA Ops:
  56.5 4.6 %copy-start.2 = (s32[8,8,256]{2,1,0:T(8,128)S(1)}, s32[8,8,256]{2,1,0:T(8,128)}, u32[]{:S(2)}) copy-start(s32[8,8,256]{2,1,0:T(8,128)} %get-tuple-element.53) | copy-start | bytes 196612
  56.5 5.2 %copy-start.1 = (s32[8,8,256]{2,1,0:T(8,128)S(1)}, s32[8,8,256]{2,1,0:T(8,128)}, u32[]{:S(2)}) copy-start(s32[8,8,256]{2,1,0:T(8,128)} %get-tuple-element.52) | copy-start | bytes 196612
  56.5 42.8 %all-to-all-start = ((bf16[4,8,256,128]{3,2,1,0:T(8,128)(2,1)}), bf16[4,8,256,128]{3,2,1,0:T(8,128)(2,1)}, u32[]{:S(2)}, u32[]{:S(2)}) async-start(bf16[4,8,256,128]{3,2,1,0:T(8,128)(2,1)} %get-tuple-element.54), calls=%async_computation | async-start | bytes 4194304 | tf_op jit(solution)/shard_map/all_to_all | solution.py:537
  69.0 65.3 %collective-permute-start.1 = (bf16[2816,256]{1,0:T(8,128)(2,1)}, bf16[2816,256]{1,0:T(8,128)(2,1)S(1)}, u32[]{:S(2)}, u32[]{:S(2)}) collective-permute-start(bf16[2816,256]{1,0:T(8,128)(2,1)} %shard_map.58), channel_id=1, source_target_pairs={{0,4},{1,5},{2,6},{3,7},{4,0},{5,1},{6,2},{7,3},{8,12},{9,13},{10,... | collective-permute-start | bytes 4325384 | tf_op jit(solution)/shard_map/ppermute | solution.py:527
  134.3 1.2 copy-start

commit v5 on v4

--- a/solution.py
+++ b/solution.py
@@ -13,9 +13,9 @@
 DOCS = 16
 LANES = 128
 SPAN = 256
-STRIDE = 512
-PIECE = 32
-TOGETHER = 4
+STRIDE = (512, 256)
+PIECE = 16
+TOGETHER = 8
 MIB = 2**20
 MASKED = -8192.0
 ROOM = 11
@@ -23,8 +23,14 @@
 
 
 def peer(me, shift, half):
-    base = me // half * half
-    return base + lax.rem(me - base + shift, half)
+    base, place = me // half * half, lax.rem(me, half)
+    if half & (half - 1):
+        return base + lax.rem(place + shift, half)
+    bit, flipped = 1, 0
+    while bit < half:
+        flipped += bit * lax.rem(place // bit + shift // bit, 2)
+        bit *= 2
+    return base + flipped
 
 
 def greet(others):
@@ -46,14 +52,13 @@
 
 
 def gather_kernel(
-    group, k_ref, v_ref, dec_ref, enc_ref, q_ref, k_out, v_out, dec_out, enc_out, q_out, held, ids_held, own_sem, ids_sem, send_sem, recv_sem, ids_send, ids_recv
+    group, k_ref, v_ref, dec_ref, enc_ref, q_ref, k_out, v_out, ids_out, q_out, held, ids_held, own_sem, ids_sem, send_sem, recv_sem, ids_send, ids_recv
 ):
     me = lax.axis_index("seq")
     half = group // 2
     width = k_out.shape[3]
     place = lax.rem(me, half)
     large = ((0, k_ref, k_out), (1, v_ref, v_out))
-    small = ((0, dec_ref, dec_out), (1, enc_ref, enc_out))
 
     def columns(src, target):
         return src.at[:, :, pl.ds(pl.multiple_of(lax.rem(target, half) * width, LANES), width)]
@@ -63,27 +68,32 @@
         at = slot * (half - 1) + shift - 1
         return remote(columns(src, target), dst.at[place], send_sem.at[at], recv_sem.at[at], target)
 
-    def ids(shift, slot, src, dst):
-        at = slot * (group - 1) + shift - 1
-        return remote(src, dst.at[me], ids_send.at[at], ids_recv.at[at], lax.rem(me + shift, group))
+    def ids(shift):
+        at = shift - 1
+        return remote(ids_held, ids_out.at[me], ids_send.at[at], ids_recv.at[at], lax.rem(me + shift, group))
 
     @pl.when(pl.program_id(0) == 0)
     def _():
+        own_ids = [
+            pltpu.make_async_copy(src, ids_held.at[slot], ids_sem.at[slot]) for slot, src in enumerate((dec_ref, enc_ref))
+        ]
+        for copy in own_ids:
+            copy.start()
         greet([lax.rem(me + shift, group) for shift in range(1, group)])
+        for copy in own_ids:
+            copy.wait()
+        for shift in range(1, half):
+            for each in large:
+                heads(shift, *each).start()
         for shift in range(1, group):
-            for each in small:
-                ids(shift, *each).start()
-        for each in large:
-            for shift in range(half - 1, 0, -1):
-                heads(shift, *each).start()
+            ids(shift).start()
         own = [pltpu.make_async_copy(columns(src, me), held.at[slot], own_sem.at[slot]) for slot, src, _ in large]
-        own += [pltpu.make_async_copy(src, ids_held.at[slot], ids_sem.at[slot]) for slot, src, _ in small]
+        own += [pltpu.make_async_copy(ids_held, ids_out.at[me], ids_sem.at[0])]
         for copy in own:
             copy.start()
         for copy in own:
             copy.wait()
         own = [pltpu.make_async_copy(held.at[slot], dst.at[place], own_sem.at[slot]) for slot, _, dst in large]
-        own += [pltpu.make_async_copy(ids_held.at[slot], dst.at[me], ids_sem.at[slot]) for slot, _, dst in small]
         for copy in own:
             copy.start()
         for copy in own:
@@ -95,8 +105,7 @@
     @pl.when(pl.program_id(0) == pl.num_programs(0) - 1)
     def _():
         for shift in range(1, group):
-            for each in small:
-                ids(shift, *each).wait()
+            ids(shift).wait()
         for each in large:
             for shift in range(1, half):
                 heads(shift, *each).wait()
@@ -110,14 +119,14 @@
     block = pl.BlockSpec((1, count, features), lambda r: (r, 0, 0))
     packed = pl.BlockSpec((half, 1, count, width), lambda r: (0, r, 0, 0))
     spread = jax.ShapeDtypeStruct((half, rows, count, width), k.dtype)
-    every = jax.ShapeDtypeStruct((group, rows, count), dec_ids.dtype)
+    every = jax.ShapeDtypeStruct((group, 2, rows, count), dec_ids.dtype)
     dma = pltpu.SemaphoreType.DMA
     return pl.pallas_call(
         functools.partial(gather_kernel, group),
         grid=(rows,),
         in_specs=[anywhere] * 4 + [block],
-        out_specs=[anywhere] * 4 + [packed],
-        out_shape=[spread, spread, every, every, spread],
+        out_specs=[anywhere] * 3 + [packed],
+        out_shape=[spread, spread, every, spread],
         scratch_shapes=[
             pltpu.VMEM((2, rows, count, width), k.dtype),
             pltpu.VMEM((2, rows, count), dec_ids.dtype),
@@ -125,8 +134,8 @@
             dma((2,)),
             dma((2 * (half - 1),)),
             dma((2 * (half - 1),)),
-            dma((2 * (group - 1),)),
-            dma((2 * (group - 1),)),
+            dma((group - 1,)),
+            dma((group - 1,)),
         ],
         compiler_params=pltpu.CompilerParams(collective_id=0, has_side_effects=True),
     )(k, v, dec_ids, enc_ids, q)
@@ -144,7 +153,7 @@
         return remote(o_ref.at[lax.rem(target, half)], columns, send_sem.at[shift - 1], recv_sem.at[shift - 1], target)
 
     greet([peer(me, shift, half) for shift in range(1, half)])
-    for shift in range(half - 1, 0, -1):
+    for shift in range(1, half):
         transfer(shift).start()
     own = pltpu.make_async_copy(o_ref.at[place], held, own_sem)
     own.start()
@@ -214,6 +223,7 @@
         in_specs=[small] * 2 + [inside] * 2,
         out_specs=inside,
         out_shape=jax.ShapeDtypeStruct((room, 2 * width), k.dtype),
+        compiler_params=pltpu.CompilerParams(vmem_limit_bytes=16 * MIB),
         cost_estimate=pl.CostEstimate(flops=2000000, bytes_accessed=8 * k.size, transcendentals=0),
     )(table, shift, k, v)
 
@@ -236,7 +246,7 @@
 def prepare_kernel(table_ref, k_ref, v_ref, bounds_ref, keys, values, hot, _):
     half, _, count, width = k_ref.shape
     length = half * count
-    first = table_ref[0, table_ref.shape[1] - 1] * length
+    first = table_ref[table_ref.shape[0] - 1, 0] * length
     bounds = bounds_ref[0]
     keys[0, :, :width] = k_ref[:, 0].reshape(length, width)
     keys[0, :, width:] = missing(bounds[0:1], bounds[1:2], first, length)
@@ -278,10 +288,10 @@
     _, stride, span = even.shape
     slabs = span // count
     blocks = length // span
-    side = table_ref[0, 4 * blocks + 1]
+    side = table_ref[4 * blocks + 1, 0]
 
     def entry(row, kind, block):
-        return table_ref[row, kind * blocks + block]
+        return table_ref[kind * blocks + block, row]
 
     def each_block(do):
         def one(number, carry):
@@ -358,7 +368,7 @@
             low, high = bounds_ref[row, 0:1], bounds_ref[row, 1:2]
             low = jnp.where(side == 0, jnp.maximum(low, length), low)
             high = jnp.where(side == 0, high, jnp.minimum(high, length))
-            miss = missing(low, high, start - table_ref[row, 4 * blocks], stride)
+            miss = missing(low, high, start - table_ref[4 * blocks, row], stride)
             key = jnp.concatenate([more_ref[pl.ds(start, stride), :width], miss], axis=1)
         else:
             start = pl.multiple_of(items[2, index], LANES)
@@ -428,7 +438,7 @@
     length = half * count
     heads = width // HEAD_DIM
     span = max(SPAN, count)
-    stride = min(STRIDE, length)
+    stride = min(STRIDE[mode], length)
     small = pl.BlockSpec(memory_space=pltpu.SMEM)
     inside = pl.BlockSpec(memory_space=pltpu.VMEM)
     outside = pl.BlockSpec(memory_space=pltpu.HBM)
@@ -480,27 +490,29 @@
     rows, whole = dec_rows.shape
     length = whole // 2
     blocks = length // SPAN
-    stride = min(STRIDE, length)
-    numbers = jnp.arange(LANES, dtype=jnp.int32)[None, :, None]
+    stride, late = (min(size, length) for size in STRIDE)
+    numbers = jnp.arange(DOCS, dtype=jnp.int32)[None, :, None]
     bounds = []
     for ids in (enc_rows, dec_rows):
-        bounds += [jnp.sum(ids[:, None, :] < numbers, axis=2), jnp.sum(ids[:, None, :] <= numbers, axis=2)]
-    bounds = jnp.stack(bounds, axis=1).astype(jnp.int32)
+        start = jnp.sum(ids[:, None, :] < numbers, axis=2, dtype=jnp.int32)
+        bounds += [start, jnp.concatenate([start[:, 1:], jnp.full((rows, 1), whole, jnp.int32)], axis=1)]
+    bounds = jnp.pad(jnp.stack(bounds, axis=1), ((0, 0), (0, 0), (0, LANES - DOCS)))
     mine = lax.dynamic_slice(dec_rows, (0, side * length), (rows, length))
     docs = mine.reshape(rows, blocks, SPAN)
     starts = jnp.concatenate([docs[:, :, 0], dec_rows[:, length : length + 1]], axis=1)
     ends = jnp.concatenate([docs[:, :, -1], dec_rows[:, length - 1 : length]], axis=1)
-    before = jnp.sum(enc_rows[:, None, :] < starts[:, :, None], axis=2, dtype=jnp.int32)
-    upto = jnp.sum(enc_rows[:, None, :] <= ends[:, :, None], axis=2, dtype=jnp.int32)
-    up = jnp.maximum(length - before[:, blocks], 0)
-    down = jnp.maximum(upto[:, blocks] - length, 0)
-    up, down = (-(-amount // PIECE) * PIECE for amount in (up, down))
-    before, upto = before[:, :blocks], upto[:, :blocks]
-    sent, got = jnp.where(side == 0, up, down), jnp.where(side == 0, down, up)
-    offset_of = [jnp.cumsum(amount) - amount for amount in (sent, got)]
+    before = jnp.sum(enc_rows[:, None, :] < starts[:, :, None], axis=2, dtype=jnp.int32).T
+    upto = jnp.sum(enc_rows[:, None, :] <= ends[:, :, None], axis=2, dtype=jnp.int32).T
+    ways = jnp.stack([length - before[blocks], upto[blocks] - length])
+    ways = -(-jnp.maximum(ways, 0) // PIECE) * PIECE
+    most = jnp.max(jnp.sum(ways, axis=1))
+    before, upto = before[:blocks], upto[:blocks]
+    sent, got = (jnp.where(side == which, ways[0], ways[1]) for which in (0, 1))
+    earlier = jnp.arange(rows)[:, None] > jnp.arange(rows)[None, :]
+    offset_of = [jnp.sum(jnp.where(earlier, amount[None, :], 0), axis=1) for amount in (sent, got)]
     first = jnp.where(side == 0, length - sent, 0)
     send = jnp.stack([offset_of[0], first, sent])
-    base = (offset_of[1] - jnp.where(side == 0, length, length - got))[:, None]
+    base = (offset_of[1] - jnp.where(side == 0, length, length - got))[None, :]
     home = side * length
     near, far = jnp.maximum(before - home, 0), jnp.minimum(upto - home, length)
     low = near // LANES * LANES
@@ -509,9 +521,9 @@
     near = base + jnp.where(side == 0, jnp.maximum(before, length), before)
     far = base + jnp.where(side == 0, upto, jnp.minimum(upto, length))
     start = near // PIECE * PIECE
-    more = jnp.where(far > near, (far - start + stride - 1) // stride, 0)
-    known = jnp.concatenate([low, steps, start, more, base, jnp.full((rows, 1), side, jnp.int32)], axis=1)
-    return send, known, bounds, jnp.maximum(jnp.sum(up), jnp.sum(down))
+    more = jnp.where(far > near, (far - start + late - 1) // late, 0)
+    known = jnp.concatenate([low, steps, start, more, base, jnp.full((1, rows), side, jnp.int32)], axis=0)
+    return send, known, bounds, most
 
 
 def whole(queries, enc_keys, enc_values, dec_ids, enc_ids):
@@ -520,14 +532,14 @@
     rows, count, _ = queries.shape
     length = half * count
     side = lax.axis_index("seq") // half
-    k, v, dec_all, enc_all, q_packed = gather(queries, enc_keys, enc_values, dec_ids, enc_ids, group)
+    k, v, ids_all, q_packed = gather(queries, enc_keys, enc_values, dec_ids, enc_ids, group)
     sides = [list(range(half)), list(range(half, group))]
 
     def cross(block):
         return lax.ppermute(block, "seq", [(i, (i + half) % group) for i in range(group)])
 
     q = lax.all_to_all(q_packed, "seq", split_axis=0, concat_axis=0, axis_index_groups=sides, tiled=True)
-    dec_rows, enc_rows = (x.transpose(1, 0, 2).reshape(rows, 2 * length) for x in (dec_all, enc_all))
+    dec_rows, enc_rows = ids_all.transpose(1, 2, 0, 3).reshape(2, rows, 2 * length)
     send, known, bounds, most = tables(dec_rows, enc_rows, side)
     trip = min(TRIP, length)
     full = rows * length

time: 174 us -> 168 us (0.966)
  other arithmetic: 10.9 us -> 7.18 us
  Pallas kernels: 129 us -> 127 us
    all_to_all x1, waiting for transfers between devices: 1.95 us -> 9.57 us  [whole(): lax.all_to_all(q_packed, 'seq', split_axis=0, concat_axis=0, axis_index_g...]
    ppermute x1, waiting for transfers between devices: 9.12 us -> 2.53 us  [cross(): lax.ppermute(block, 'seq', [(i, (i + half) % group) for i in range(group)])]
    unnamed x11 -> x9, local copies, waits for them, and re-layouts: 6.39 us -> 3.06 us
    reduce_sum x4 -> x5, other arithmetic: 6.89 us -> 3.71 us  [the longest x2 2.17 us: tables(): start = jnp.sum(ids[:, None, :] < numbers, axis=2, dtype=jnp.int32)]
    concatenate x1 -> x3, local copies, waits for them, and re-layouts: 1.37 us -> 3.8 us  [the longest x1 3.79 us: tables(): jnp.concatenate([low, steps, start, more, base, jnp.full((1, rows), side,...]
  transfers between devices with their start and end apart: 2 -> 2, of which waited for: 2 -> 2; matrix products, arithmetic and copies ran while one was open for 9% -> 7% of each run, Pallas kernels for 22% -> 22%
where the time goes in v5:
time: 168 us; the launch traced here: 167 us
  Pallas kernels  127 us (76%)
  waiting for transfers between devices  12.1 us (7%)
  local copies, waits for them, and re-layouts  8.18 us (5%)
  other arithmetic  7.18 us (4%)
  starting transfers between devices  6.2 us (4%)
  blocking collectives  5.98 us (4%)
    pallas_call x1, Pallas kernels, gather(): pl.pallas_call(functools.partial(gather_kernel, group), grid=(rows,), in_...  56 us
    pallas_call x2, Pallas kernels, attend(): pl.pallas_call(functools.partial(attend_kernel, mode), in_specs=specs, ou...  31.9 us
    pallas_call x1, Pallas kernels, give_back(): pl.pallas_call(functools.partial(give_back_kernel, group), in_specs=[pl.B...  27.6 us
    all_to_all x1, waiting for transfers between devices, whole(): lax.all_to_all(q_packed, 'seq', split_axis=0, concat_axis=0, axis_index_g...  9.57 us
    pallas_call x1, Pallas kernels, prepare(): pl.pallas_call(prepare_kernel, grid_spec=pltpu.PrefetchScalarGridSpec(num...  8.31 us
    pmax x1, blocking collectives, whole(): most = lax.pmax(most, 'dp')  5.98 us
    all_to_all x1, starting transfers between devices, whole(): lax.all_to_all(q_packed, 'seq', split_axis=0, concat_axis=0, axis_index_g...  4.59 us
    concatenate x1, local copies, waits for them, and re-layouts, tables(): jnp.concatenate([low, steps, start, more, base, jnp.full((1, rows), side,...  3.79 us
  transfers between devices with their start and end apart: 2, of which 2 were waited for; matrix products, arithmetic and copies ran while one was open for 7% of the time, Pallas kernels for 22%

profile of v5, /device:TPU:0, one launch (start us, length us, event | category | flops | bytes accessed | tf_op | source)
XLA Modules:
  0.0 167.3 jit_solution(7158812875797997702)
XLA Ops:
  0.0 56.0 %shard_map.55 = (bf16[4,8,256,128]{3,2,1,0:T(8,128)(2,1)S(1)}, bf16[4,8,256,128]{3,2,1,0:T(8,128)(2,1)}, s32[8,2,8,256]{3,2,1,0:T(8,128)}, bf16[4,8,256,128]{3,2,1,0:T(8,128)(2,1)}) custom-call(bf16[8,256,512]{2,1,0:T(8,128)(2,1)} %k_ref.1, bf16[8,256,512]{2,1,0:T(8,128)(2,1)} %v_ref.1, s32[8,256]{1,0:T(8,128)} %dec_ref.1, s32[8,256]{1,0:T(8,128)} %enc_ref.1, ...), custom_call_target="tpu_custom_call" | custom-call | tf_op jit(solution)/shard_map/pallas_call | solution.py:124
  56.0 4.6 %all-to-all-start = ((bf16[4,8,256,128]{3,2,1,0:T(8,128)(2,1)}), bf16[4,8,256,128]{3,2,1,0:T(8,128)(2,1)}, u32[]{:S(2)}, u32[]{:S(2)}) async-start(bf16[4,8,256,128]{3,2,1,0:T(8,128)(2,1)} %get-tuple-element.52), calls=%async_computation | async-start | bytes 4194304 | tf_op jit(solution)/shard_map/all_to_all | solution.py:549
  61.2 0.3 convert_reduce_fusion.3
  61.6 0.7 fusion.15
  62.3 0.6 broadcast_select_fusion
  62.8 0.1 select_reduce_fusion
  63.0 3.1 %shard_map.58 = bf16[2816,256]{1,0:T(8,128)(2,1)S(1)} custom-call(s32[3,8]{1,0:T(4,128)S(1)} %pad_add_fusion.3.table_ref, s32[1]{0:T(128)} %constant.130.clone.1.shift_ref, bf16[4,8,256,128]{3,2,1,0:T(8,128)(2,1)S(1)} %get-tuple-element.140.k_ref, bf16[4,8,256,128]{3,2,1,0:T(8,128)(2,1)} %get-tuple-element.141.v_ref), custom_call_target="tpu_custom_call" | custom-call | flops 2000000 | bytes 8388608 | tf_op jit(solution)/shard_map/pallas_call | solution.py:221
  66.1 1.6 collective-permute-start.1
  67.7 1.2 reduce_max.9
  69.0 6.0 %pmax.7 = s32[]{:T(128)} all-reduce(s32[]{:T(128)} %reduce_max.9), channel_id=1, replica_groups=mesh['dp'=4,'seq'=8] {'dp'}, use_global_device_ids=true, to_apply=%region_5.6 | all-reduce | flops 1 | bytes 8 | tf_op jit(solution)/shard_map/pmax | solution.py:551
  75.5 1.1 convert_reduce_fusion
  76.7 1.1 convert_reduce_fusion.1
  77.9 0.6 pad.6.bounds_ref.refs_1_
  78.5 0.8 select_reduce_fusion.1
  79.3 0.6 fusion.8
  79.9 3.8 %concatenate.17.table_ref = s32[18,8]{1,0:T(8,128)} concatenate(s32[4,8]{1,0:T(4,128)} %get-tuple-element.93, s32[4,8]{1,0:T(4,128)} %get-tuple-element.94, s32[4,8]{1,0:T(4,128)} %get-tuple-element.84, s32[4,8]{1,0:T(4,128)S(1)} %get-tuple-element.83, s32[1,8]{1,0:T(1,128)} %copy-done.3, s32[1,8]{1,0:T(1,128)S(1)} %broadcast_in_dim.48), dimensions={0} | concatenate | bytes 1152 | tf_op jit(solution)/shard_map/concatenate | solution.py:525
  83.7 8.3 %shard_map.56 = (bf16[8,1024,256]{2,1,0:T(8,128)(2,1)}, bf16[8,160,1024]{2,1,0:T(8,128)(2,1)}, bf16[8,16,1024]{2,1,0:T(8,128)(2,1)}, bf16[5632,256]{1,0:T(8,128)(2,1)}) custom-call(s32[18,8]{1,0:T(8,128)} %concatenate.17.table_ref, bf16[4,8,256,128]{3,2,1,0:T(8,128)(2,1)S(1)} %get-tuple-element.140.k_ref, bf16[4,8,256,128]{3,2,1,0:T(8,128)(2,1)} %get-tuple-element.141.v_ref, ...), custom_call_target="tpu_custom_call" | custom-call | flops 2000000 | bytes 10485760 | tf_op jit(solution)/shard_map/pallas_call | solution.py:264
  92.0 0.6 pad_add_fusion.4.refs_0_
  92.6 9.6 %all-to-all-done.refs_0_.refs_2_ = bf16[4,8,256,128]{3,2,1,0:T(8,128)(2,1)} async-done(((bf16[4,8,256,128]{3,2,1,0:T(8,128)(2,1)}), bf16[4,8,256,128]{3,2,1,0:T(8,128)(2,1)}, u32[]{:S(2)}, u32[]{:S(2)}) %all-to-all-start) | async-done | bytes 2097184 | tf_op jit(solution)/shard_map/all_to_all | solution.py:549
  102.2 25.8 %shard_map.57 = (bf16[4,8,256,128]{3,2,1,0:T(8,128)(2,1)}, f32[32,2,1,256]{3,2,1,0:T(1,128)}, f32[32,2,80,256]{3,2,1,0:T(8,128)}) custom-call(s32[18,8]{1,0:T(8,128)} %concatenate.17.table_ref, bf16[4,8,256,128]{3,2,1,0:T(8,128)(2,1)} %all-to-all-done.refs_0_.refs_2_, bf16[8,1024,256]{2,1,0:T(8,128)(2,1)} %get-tuple-element.56.refs_1_, ...), custom_call_target="tpu_custom_call" | custom-call | flops 2147483648 | bytes 8388608 | tf_op jit(solution)/shard_map/pallas_call | solution.py:473
  128.0 2.5 %collective-permute-done.1.refs_6_ = bf16[2816,256]{1,0:T(8,128)(2,1)} collective-permute-done((bf16[2816,256]{1,0:T(8,128)(2,1)S(1)}, bf16[2816,256]{1,0:T(8,128)(2,1)}, u32[]{:S(2)}, u32[]{:S(2)}) %collective-permute-start.1) | collective-permute-done | bytes 1441824 | tf_op jit(solution)/shard_map/ppermute | solution.py:539
  130.6 6.1 %shard_map.59.o_ref = bf16[4,8,256,128]{3,2,1,0:T(8,128)(2,1)} custom-call(s32[18,8]{1,0:T(8,128)} %concatenate.17.table_ref, s32[2]{0:T(128)} %pad_add_fusion.4.refs_0_, s32[8,4,128]{2,1,0:T(4,128)} %pad.6.bounds_ref.refs_1_, bf16[4,8,256,128]{3,2,1,0:T(8,128)(2,1)} %all-to-all-done.refs_0_.refs_2_, ...), custom_call_target="tpu_custom_call", output_to_operand_aliasing={{}: (9, {})} | custom-call | flops 536870912 | bytes 8388608 | tf_op jit(solution)/shard_map/pallas_call | solution.py:473
  136.7 27.6 %shard_map.60 = bf16[8,256,512]{2,1,0:T(8,128)(2,1)} custom-call(bf16[4,8,256,128]{3,2,1,0:T(8,128)(2,1)} %shard_map.59.o_ref), custom_call_target="tpu_custom_call" | custom-call | tf_op jit(solution)/shard_map/pallas_call | solution.py:170
  164.3 3.0 %copy.59 = bf16[8,256,512]{2,1,0:T(8,128)(2,1)} copy(bf16[8,256,512]{2,1,0:T(8,128)(2,1)} %shard_map.60) | data formatting | bytes 4194304
  (29 shorter events, 0.8 us)
Async XLA Ops:
  56.0 4.6 %copy-start.2 = (s32[8,2,8,256]{3,2,1,0:T(8,128)S(1)}, s32[8,2,8,256]{3,2,1,0:T(8,128)}, u32[]{:S(2)}) copy-start(s32[8,2,8,256]{3,2,1,0:T(8,128)} %get-tuple-element.51) | copy-start | bytes 393220
  56.0 46.2 %all-to-all-start = ((bf16[4,8,256,128]{3,2,1,0:T(8,128)(2,1)}), bf16[4,8,256,128]{3,2,1,0:T(8,128)(2,1)}, u32[]{:S(2)}, u32[]{:S(2)}) async-start(bf16[4,8,256,128]{3,2,1,0:T(8,128)(2,1)} %get-tuple-element.52), calls=%async_computation | async-start | bytes 4194304 | tf_op jit(solution)/shard_map/all_to_all | solution.py:549
  60.6 2.4 %copy-start = (s32[1,8,8,256]{3,1,0,2:T(8,128)}, s32[1,8,8,256]{3,1,0,2:T(8,128)S(1)}, u32[]{:S(2)}) copy-start(s32[1,8,8,256]{3,1,0,2:T(8,128)S(1)} %get-tuple-element.87) | copy-start | bytes 196612
  60.6 2.4 %copy-start.1 = (s32[1,8,8,256]{3,1,0,2:T(8,128)}, s32[1,8,8,256]{3,1,0,2:T(8,128)S(1)}, u32[]{:S(2)}) copy-start(s32[1,8,8,256]{3,1,0,2:T(8,128)S(1)} %get-tuple-element.88) | copy-start | bytes 196612
  66.1 64.5 %collective-permute-start.1 = (bf16[2816,256]{1,0:T(8,128)(2,1)S(1)}, bf16[2816,256]{1,0:T(8,128)(2,1)}, u32[]{:S(2)}, u32[]{:S(2)}) collective-permute-start(bf16[2816,256]{1,0:T(8,128)(2,1)S(1)} %shard_map.58), channel_id=1, source_target_pairs={{0,4},{1,5},{2,6},{3,7},{4,0},{5,1},{6,2},{7,3},{8,12},{9,13},{10,... | collective-permute-start | bytes 4325384 | tf_op jit(solution)/shard_map/ppermute | solution.py:539
  79.3 0.6 copy-start.3

commit v6 on v5

--- a/solution.py
+++ b/solution.py
@@ -16,6 +16,7 @@
 STRIDE = (512, 256)
 PIECE = 16
 TOGETHER = 8
+UNROLL = (8, 4)
 MIB = 2**20
 MASKED = -8192.0
 ROOM = 11
@@ -287,6 +288,7 @@
     heads = width // HEAD_DIM
     _, stride, span = even.shape
     slabs = span // count
+    unroll = UNROLL[mode]
     blocks = length // span
     side = table_ref[4 * blocks + 1, 0]
 
@@ -348,7 +350,7 @@
 
         return lax.fori_loop(0, steps, list_step, total)
 
-    total = lax.fori_loop(0, rows * blocks, list_block, jnp.int32(1))
+    total = lax.fori_loop(0, rows * blocks, list_block, jnp.int32(unroll - 1))
     if mode:
 
         @pl.when(trips_ref[0] > 0)
@@ -403,22 +405,23 @@
         whole = jnp.concatenate(done, axis=0).T.astype(jnp.bfloat16)
         o_ref[pl.ds(block * slabs, slabs), row] = whole.reshape(slabs, count, width)
 
-    @pl.when(total > 1)
+    @pl.when(total >= unroll)
     def _():
-        begin = total % 2
-        for field in range(4):
-            items[field, 0] = items[field, 1]
+        begin = total % unroll
+        for spare in range(unroll - 1):
+            for field in range(4):
+                items[field, spare] = items[field, unroll - 1]
         score(begin, even, even_peak)
 
-        def pair(index, carry):
-            at = begin + 2 * index
-            score(at + 1, odd, odd_peak)
-            weigh(at, even, even_peak)
-            score(jnp.minimum(at + 2, total - 1), even, even_peak)
-            weigh(at + 1, odd, odd_peak)
+        def several(index, carry):
+            at = begin + unroll * index
+            buffers = ((even, even_peak), (odd, odd_peak))
+            for ahead in range(unroll):
+                score(jnp.minimum(at + ahead + 1, total - 1), *buffers[(ahead + 1) % 2])
+                weigh(at + ahead, *buffers[ahead % 2])
             return carry
 
-        lax.fori_loop(0, (total - begin) // 2, pair, 0)
+        lax.fori_loop(0, (total - begin) // unroll, several, 0)
 
     if mode:
 
@@ -445,7 +448,7 @@
     numbers = rows * (length // span)
     state = [(numbers, heads, 1, span), (numbers, heads, TALL, span)]
     scratch = [
-        pltpu.SMEM((4, numbers * (2 * length // stride + 1) + 1), jnp.int32),
+        pltpu.SMEM((4, numbers * (2 * length // stride + 1) + UNROLL[mode]), jnp.int32),
         pltpu.VMEM((heads, stride, span), jnp.float32),
         pltpu.VMEM((heads, stride, span), jnp.float32),
         pltpu.VMEM((heads, 1, span), jnp.float32),

time: 168 us -> 168 us (level)
  Pallas kernels: 127 us -> 123 us
  waiting for transfers between devices: 12.1 us -> 15.5 us
    ppermute x1, waiting for transfers between devices: 2.53 us -> 5.88 us  [cross(): lax.ppermute(block, 'seq', [(i, (i + half) % group) for i in range(group)])]
    pallas_call x2, Pallas kernels: 31.9 us -> 28.7 us  [attend(): pl.pallas_call(functools.partial(attend_kernel, mode), in_specs=specs, ou...]
  transfers between devices with their start and end apart: 2 -> 2, of which waited for: 2 -> 2; matrix products, arithmetic and copies ran while one was open for 7% -> 7% of each run, Pallas kernels for 22% -> 20%
where the time goes in v6:
time: 168 us; the launch traced here: 167 us
  Pallas kernels  123 us (73%)
  waiting for transfers between devices  15.5 us (9%)
  local copies, waits for them, and re-layouts  8.18 us (5%)
  other arithmetic  7.18 us (4%)
  starting transfers between devices  6.2 us (4%)
  blocking collectives  5.98 us (4%)
    pallas_call x1, Pallas kernels, gather(): pl.pallas_call(functools.partial(gather_kernel, group), grid=(rows,), in_...  56 us
    pallas_call x2, Pallas kernels, attend(): pl.pallas_call(functools.partial(attend_kernel, mode), in_specs=specs, ou...  28.7 us
    pallas_call x1, Pallas kernels, give_back(): pl.pallas_call(functools.partial(give_back_kernel, group), in_specs=[pl.B...  27.3 us
    all_to_all x1, waiting for transfers between devices, whole(): lax.all_to_all(q_packed, 'seq', split_axis=0, concat_axis=0, axis_index_g...  9.57 us
    pallas_call x1, Pallas kernels, prepare(): pl.pallas_call(prepare_kernel, grid_spec=pltpu.PrefetchScalarGridSpec(num...  8.31 us
    pmax x1, blocking collectives, whole(): most = lax.pmax(most, 'dp')  5.98 us
    ppermute x1, waiting for transfers between devices, cross(): lax.ppermute(block, 'seq', [(i, (i + half) % group) for i in range(group)])  5.88 us
    all_to_all x1, starting transfers between devices, whole(): lax.all_to_all(q_packed, 'seq', split_axis=0, concat_axis=0, axis_index_g...  4.59 us
  transfers between devices with their start and end apart: 2, of which 2 were waited for; matrix products, arithmetic and copies ran while one was open for 7% of the time, Pallas kernels for 20%

profile of v6, /device:TPU:0, one launch (start us, length us, event | category | flops | bytes accessed | tf_op | source)
XLA Modules:
  0.0 167.2 jit_solution(3433378114675158226)
XLA Ops:
  0.0 56.0 %shard_map.55 = (bf16[4,8,256,128]{3,2,1,0:T(8,128)(2,1)S(1)}, bf16[4,8,256,128]{3,2,1,0:T(8,128)(2,1)}, s32[8,2,8,256]{3,2,1,0:T(8,128)}, bf16[4,8,256,128]{3,2,1,0:T(8,128)(2,1)}) custom-call(bf16[8,256,512]{2,1,0:T(8,128)(2,1)} %k_ref.1, bf16[8,256,512]{2,1,0:T(8,128)(2,1)} %v_ref.1, s32[8,256]{1,0:T(8,128)} %dec_ref.1, s32[8,256]{1,0:T(8,128)} %enc_ref.1, ...), custom_call_target="tpu_custom_call" | custom-call | tf_op jit(solution)/shard_map/pallas_call | solution.py:125
  56.0 4.6 %all-to-all-start = ((bf16[4,8,256,128]{3,2,1,0:T(8,128)(2,1)}), bf16[4,8,256,128]{3,2,1,0:T(8,128)(2,1)}, u32[]{:S(2)}, u32[]{:S(2)}) async-start(bf16[4,8,256,128]{3,2,1,0:T(8,128)(2,1)} %get-tuple-element.52), calls=%async_computation | async-start | bytes 4194304 | tf_op jit(solution)/shard_map/all_to_all | solution.py:552
  61.2 0.3 convert_reduce_fusion.3
  61.6 0.7 fusion.15
  62.3 0.6 broadcast_select_fusion
  62.8 0.1 select_reduce_fusion
  63.0 3.1 %shard_map.58 = bf16[2816,256]{1,0:T(8,128)(2,1)S(1)} custom-call(s32[3,8]{1,0:T(4,128)S(1)} %pad_add_fusion.3.table_ref, s32[1]{0:T(128)} %constant.130.clone.1.shift_ref, bf16[4,8,256,128]{3,2,1,0:T(8,128)(2,1)S(1)} %get-tuple-element.140.k_ref, bf16[4,8,256,128]{3,2,1,0:T(8,128)(2,1)} %get-tuple-element.141.v_ref), custom_call_target="tpu_custom_call" | custom-call | flops 2000000 | bytes 8388608 | tf_op jit(solution)/shard_map/pallas_call | solution.py:222
  66.1 1.6 collective-permute-start.1
  67.7 1.2 reduce_max.9
  69.0 6.0 %pmax.7 = s32[]{:T(128)} all-reduce(s32[]{:T(128)} %reduce_max.9), channel_id=1, replica_groups=mesh['dp'=4,'seq'=8] {'dp'}, use_global_device_ids=true, to_apply=%region_5.6 | all-reduce | flops 1 | bytes 8 | tf_op jit(solution)/shard_map/pmax | solution.py:554
  75.5 1.1 convert_reduce_fusion
  76.7 1.1 convert_reduce_fusion.1
  77.9 0.6 pad.6.bounds_ref.refs_1_
  78.5 0.8 select_reduce_fusion.1
  79.3 0.6 fusion.8
  79.9 3.8 %concatenate.17.table_ref = s32[18,8]{1,0:T(8,128)} concatenate(s32[4,8]{1,0:T(4,128)} %get-tuple-element.93, s32[4,8]{1,0:T(4,128)} %get-tuple-element.94, s32[4,8]{1,0:T(4,128)} %get-tuple-element.84, s32[4,8]{1,0:T(4,128)S(1)} %get-tuple-element.83, s32[1,8]{1,0:T(1,128)} %copy-done.3, s32[1,8]{1,0:T(1,128)S(1)} %broadcast_in_dim.48), dimensions={0} | concatenate | bytes 1152 | tf_op jit(solution)/shard_map/concatenate | solution.py:528
  83.7 8.3 %shard_map.56 = (bf16[8,1024,256]{2,1,0:T(8,128)(2,1)}, bf16[8,160,1024]{2,1,0:T(8,128)(2,1)}, bf16[8,16,1024]{2,1,0:T(8,128)(2,1)}, bf16[5632,256]{1,0:T(8,128)(2,1)}) custom-call(s32[18,8]{1,0:T(8,128)} %concatenate.17.table_ref, bf16[4,8,256,128]{3,2,1,0:T(8,128)(2,1)S(1)} %get-tuple-element.140.k_ref, bf16[4,8,256,128]{3,2,1,0:T(8,128)(2,1)} %get-tuple-element.141.v_ref, ...), custom_call_target="tpu_custom_call" | custom-call | flops 2000000 | bytes 10485760 | tf_op jit(solution)/shard_map/pallas_call | solution.py:265
  92.0 0.6 pad_add_fusion.4.refs_0_
  92.6 9.6 %all-to-all-done.refs_0_.refs_2_ = bf16[4,8,256,128]{3,2,1,0:T(8,128)(2,1)} async-done(((bf16[4,8,256,128]{3,2,1,0:T(8,128)(2,1)}), bf16[4,8,256,128]{3,2,1,0:T(8,128)(2,1)}, u32[]{:S(2)}, u32[]{:S(2)}) %all-to-all-start) | async-done | bytes 2097184 | tf_op jit(solution)/shard_map/all_to_all | solution.py:552
  102.2 22.5 %shard_map.57 = (bf16[4,8,256,128]{3,2,1,0:T(8,128)(2,1)}, f32[32,2,1,256]{3,2,1,0:T(1,128)}, f32[32,2,80,256]{3,2,1,0:T(8,128)}) custom-call(s32[18,8]{1,0:T(8,128)} %concatenate.17.table_ref, bf16[4,8,256,128]{3,2,1,0:T(8,128)(2,1)} %all-to-all-done.refs_0_.refs_2_, bf16[8,1024,256]{2,1,0:T(8,128)(2,1)} %get-tuple-element.56.refs_1_, ...), custom_call_target="tpu_custom_call" | custom-call | flops 2147483648 | bytes 8388608 | tf_op jit(solution)/shard_map/pallas_call | solution.py:476
  124.7 5.9 %collective-permute-done.1.refs_6_ = bf16[2816,256]{1,0:T(8,128)(2,1)} collective-permute-done((bf16[2816,256]{1,0:T(8,128)(2,1)S(1)}, bf16[2816,256]{1,0:T(8,128)(2,1)}, u32[]{:S(2)}, u32[]{:S(2)}) %collective-permute-start.1) | collective-permute-done | bytes 1441824 | tf_op jit(solution)/shard_map/ppermute | solution.py:542
  130.6 6.3 %shard_map.59.o_ref = bf16[4,8,256,128]{3,2,1,0:T(8,128)(2,1)} custom-call(s32[18,8]{1,0:T(8,128)} %concatenate.17.table_ref, s32[2]{0:T(128)} %pad_add_fusion.4.refs_0_, s32[8,4,128]{2,1,0:T(4,128)} %pad.6.bounds_ref.refs_1_, bf16[4,8,256,128]{3,2,1,0:T(8,128)(2,1)} %all-to-all-done.refs_0_.refs_2_, ...), custom_call_target="tpu_custom_call", output_to_operand_aliasing={{}: (9, {})} | custom-call | flops 536870912 | bytes 8388608 | tf_op jit(solution)/shard_map/pallas_call | solution.py:476
  136.8 27.3 %shard_map.60 = bf16[8,256,512]{2,1,0:T(8,128)(2,1)} custom-call(bf16[4,8,256,128]{3,2,1,0:T(8,128)(2,1)} %shard_map.59.o_ref), custom_call_target="tpu_custom_call" | custom-call | tf_op jit(solution)/shard_map/pallas_call | solution.py:171
  164.2 3.0 %copy.59 = bf16[8,256,512]{2,1,0:T(8,128)(2,1)} copy(bf16[8,256,512]{2,1,0:T(8,128)(2,1)} %shard_map.60) | data formatting | bytes 4194304
  (29 shorter events, 0.8 us)
Async XLA Ops:
  56.0 4.6 %copy-start.2 = (s32[8,2,8,256]{3,2,1,0:T(8,128)S(1)}, s32[8,2,8,256]{3,2,1,0:T(8,128)}, u32[]{:S(2)}) copy-start(s32[8,2,8,256]{3,2,1,0:T(8,128)} %get-tuple-element.51) | copy-start | bytes 393220
  56.0 46.2 %all-to-all-start = ((bf16[4,8,256,128]{3,2,1,0:T(8,128)(2,1)}), bf16[4,8,256,128]{3,2,1,0:T(8,128)(2,1)}, u32[]{:S(2)}, u32[]{:S(2)}) async-start(bf16[4,8,256,128]{3,2,1,0:T(8,128)(2,1)} %get-tuple-element.52), calls=%async_computation | async-start | bytes 4194304 | tf_op jit(solution)/shard_map/all_to_all | solution.py:552
  60.6 2.4 %copy-start = (s32[1,8,8,256]{3,1,0,2:T(8,128)}, s32[1,8,8,256]{3,1,0,2:T(8,128)S(1)}, u32[]{:S(2)}) copy-start(s32[1,8,8,256]{3,1,0,2:T(8,128)S(1)} %get-tuple-element.87) | copy-start | bytes 196612
  60.6 2.4 %copy-start.1 = (s32[1,8,8,256]{3,1,0,2:T(8,128)}, s32[1,8,8,256]{3,1,0,2:T(8,128)S(1)}, u32[]{:S(2)}) copy-start(s32[1,8,8,256]{3,1,0,2:T(8,128)S(1)} %get-tuple-element.88) | copy-start | bytes 196612
  66.1 64.5 %collective-permute-start.1 = (bf16[2816,256]{1,0:T(8,128)(2,1)S(1)}, bf16[2816,256]{1,0:T(8,128)(2,1)}, u32[]{:S(2)}, u32[]{:S(2)}) collective-permute-start(bf16[2816,256]{1,0:T(8,128)(2,1)S(1)} %shard_map.58), channel_id=1, source_target_pairs={{0,4},{1,5},{2,6},{3,7},{4,0},{5,1},{6,2},{7,3},{8,12},{9,13},{10,... | collective-permute-start | bytes 4325384 | tf_op jit(solution)/shard_map/ppermute | solution.py:542
  79.3 0.6 copy-start.3

commit v7 on v6

--- a/solution.py
+++ b/solution.py
@@ -24,14 +24,18 @@
 
 
 def peer(me, shift, half):
-    base, place = me // half * half, lax.rem(me, half)
+    base, place = me // half * half, me % half
     if half & (half - 1):
-        return base + lax.rem(place + shift, half)
+        return base + (place + shift) % half
     bit, flipped = 1, 0
     while bit < half:
-        flipped += bit * lax.rem(place // bit + shift // bit, 2)
+        flipped += bit * ((place // bit + shift // bit) % 2)
         bit *= 2
     return base + flipped
+
+
+def origin(me, shift, half):
+    return peer(me, (half - shift) % half if half & (half - 1) else shift, half)
 
 
 def greet(others):
@@ -53,10 +57,12 @@
 
 
 def gather_kernel(
-    group, k_ref, v_ref, dec_ref, enc_ref, q_ref, k_out, v_out, ids_out, q_out, held, ids_held, own_sem, ids_sem, send_sem, recv_sem, ids_send, ids_recv
+    group, k_ref, v_ref, dec_ref, enc_ref, q_ref, k_out, v_out, ids_out, *rest
 ):
     me = lax.axis_index("seq")
     half = group // 2
+    q_outs, rest = rest[:half], rest[half:]
+    held, ids_held, own_sem, ids_sem, send_sem, recv_sem, ids_send, ids_recv = rest
     width = k_out.shape[3]
     place = lax.rem(me, half)
     large = ((0, k_ref, k_out), (1, v_ref, v_out))
@@ -100,8 +106,9 @@
         for copy in own:
             copy.wait()
 
-    for target in range(half):
-        q_out[target, 0] = q_ref[0, :, target * width : (target + 1) * width]
+    for shift, q_out in enumerate(q_outs):
+        target = lax.rem(peer(me, shift, half), half)
+        q_out[0] = q_ref[0, :, pl.ds(pl.multiple_of(target * width, LANES), width)]
 
     @pl.when(pl.program_id(0) == pl.num_programs(0) - 1)
     def _():
@@ -118,7 +125,7 @@
     width = features // half
     anywhere = pl.BlockSpec(memory_space=pltpu.HBM)
     block = pl.BlockSpec((1, count, features), lambda r: (r, 0, 0))
-    packed = pl.BlockSpec((half, 1, count, width), lambda r: (0, r, 0, 0))
+    packed = pl.BlockSpec((1, count, width), lambda r: (r, 0, 0))
     spread = jax.ShapeDtypeStruct((half, rows, count, width), k.dtype)
     every = jax.ShapeDtypeStruct((group, 2, rows, count), dec_ids.dtype)
     dma = pltpu.SemaphoreType.DMA
@@ -126,8 +133,8 @@
         functools.partial(gather_kernel, group),
         grid=(rows,),
         in_specs=[anywhere] * 4 + [block],
-        out_specs=[anywhere] * 3 + [packed],
-        out_shape=[spread, spread, every, spread],
+        out_specs=[anywhere] * 3 + [packed] * half,
+        out_shape=[spread, spread, every] + [jax.ShapeDtypeStruct((rows, count, width), q.dtype)] * half,
         scratch_shapes=[
             pltpu.VMEM((2, rows, count, width), k.dtype),
             pltpu.VMEM((2, rows, count), dec_ids.dtype),
@@ -282,7 +289,11 @@
         trips_ref, bounds_ref, q_from, hot_from, peak_from, sum_from, more_from, late_from, _, o_to, *scratch = refs
         items, even, odd, even_peak, odd_peak, peak_of, sum_of, peak_now, sum_now, q_ref, hot_ref, o_ref, more_ref, sem = scratch
     else:
-        q_ref, keys, values, hot_ref, o_ref, peak_of, sum_of, items, even, odd, even_peak, odd_peak = refs
+        parts = refs[: len(refs) - 12]
+        keys, values, hot_ref, o_ref, q_ref, peak_of, sum_of, items, even, odd, even_peak, odd_peak = refs[len(parts) :]
+        place = lax.axis_index("seq")
+        for shift, part in enumerate(parts):
+            q_ref[lax.rem(origin(place, shift, len(parts)), len(parts))] = part[...]
     half, rows, count, width = q_ref.shape
     length = half * count
     heads = width // HEAD_DIM
@@ -437,6 +448,9 @@
 
 
 def attend(mode, table, q, *more):
+    parts = () if mode else q
+    if parts:
+        q = jax.ShapeDtypeStruct((len(parts), *parts[0].shape), parts[0].dtype)
     half, rows, count, width = q.shape
     length = half * count
     heads = width // HEAD_DIM
@@ -469,8 +483,9 @@
         specs, out_specs = [small] * 2 + [inside] + [outside] * 7, [outside]
     else:
         keys, values, hot = more
-        args = (table, q, keys, values, hot)
-        specs, out_specs = [small] + [inside] * 4, [inside] * 3
+        args = (table, *parts, keys, values, hot)
+        specs, out_specs = [small] + [inside] * (half + 3), [inside] * 4
+        shapes += [jax.ShapeDtypeStruct(q.shape, q.dtype)]
         shapes += [jax.ShapeDtypeStruct(shape, jnp.float32) for shape in state]
     share = 4 if mode else 1
     return pl.pallas_call(
@@ -535,13 +550,13 @@
     rows, count, _ = queries.shape
     length = half * count
     side = lax.axis_index("seq") // half
-    k, v, ids_all, q_packed = gather(queries, enc_keys, enc_values, dec_ids, enc_ids, group)
-    sides = [list(range(half)), list(range(half, group))]
+    k, v, ids_all, *queries = gather(queries, enc_keys, enc_values, dec_ids, enc_ids, group)
+    moves = [[(i, int(peer(i, shift, half))) for i in range(group)] for shift in range(1, half)]
 
     def cross(block):
         return lax.ppermute(block, "seq", [(i, (i + half) % group) for i in range(group)])
 
-    q = lax.all_to_all(q_packed, "seq", split_axis=0, concat_axis=0, axis_index_groups=sides, tiled=True)
+    parts = queries[:1] + [lax.ppermute(part, "seq", move) for part, move in zip(queries[1:], moves)]
     dec_rows, enc_rows = ids_all.transpose(1, 2, 0, 3).reshape(2, rows, 2 * length)
     send, known, bounds, most = tables(dec_rows, enc_rows, side)
     trip = min(TRIP, length)
@@ -549,10 +564,10 @@
     room = full * ROOM // 32 // LANES * LANES
     extra = -(-(full - room) // trip) * trip
     more = cross(pack(send, jnp.zeros((1,), jnp.int32), k, v, room))
-    q = lax.all_to_all(q_packed, "seq", split_axis=0, concat_axis=0, axis_index_groups=sides, tiled=True)
+    parts = queries[:1] + [lax.ppermute(part, "seq", move) for part, move in zip(queries[1:], moves)]
     keys, values, hot, empty = prepare(known, k, v, bounds, extra)
     most = lax.pmax(most, "dp")
-    early, peak, summed = attend(0, known, q, keys, values, hot)
+    early, q, peak, summed = attend(0, known, parts, keys, values, hot)
     trips = (jnp.maximum(most - room, 0) + trip - 1) // trip
     more, early = lax.optimization_barrier((more, early))
 

time: 168 us -> 180 us (1.071)
  waiting for transfers between devices: 15.5 us -> 24.4 us
  Pallas kernels: 123 us -> 126 us
    ppermute x0 -> x3, waiting for transfers between devices: none -> 24.4 us  [whole(): lax.ppermute(part, 'seq', move)]
    all_to_all x1 -> x0, waiting for transfers between devices: 9.57 us -> none  [whole(): lax.all_to_all(q_packed, 'seq', split_axis=0, concat_axis=0, axis_index_g...]
    ppermute x1, waiting for transfers between devices: 5.88 us -> 0.01 us  [cross(): lax.ppermute(block, 'seq', [(i, (i + half) % group) for i in range(group)])]
    all_to_all x1 -> x0, starting transfers between devices: 4.59 us -> none  [whole(): lax.all_to_all(q_packed, 'seq', split_axis=0, concat_axis=0, axis_index_g...]
    ppermute x0 -> x3, starting transfers between devices: none -> 3.49 us  [whole(): lax.ppermute(part, 'seq', move)]
    pallas_call x1, Pallas kernels: 27.3 us -> 29.5 us  [give_back(): pl.pallas_call(functools.partial(give_back_kernel, group), in_specs=[pl.B...]
  transfers between devices with their start and end apart: 2 -> 4, of which waited for: 2 -> 2; matrix products, arithmetic and copies ran while one was open for 7% -> 6% of each run, Pallas kernels for 20% -> 18%
where the time goes in v7:
time: 180 us; the launch traced here: 179 us
  Pallas kernels  126 us (70%)
  waiting for transfers between devices  24.4 us (14%)
  local copies, waits for them, and re-layouts  9.03 us (5%)
  other arithmetic  7.03 us (4%)
  blocking collectives  6.03 us (3%)
  starting transfers between devices  5.11 us (3%)
    pallas_call x1, Pallas kernels, gather(): pl.pallas_call(functools.partial(gather_kernel, group), grid=(rows,), in_...  55.9 us
    pallas_call x2, Pallas kernels, attend(): pl.pallas_call(functools.partial(attend_kernel, mode), in_specs=specs, ou...  29.6 us
    pallas_call x1, Pallas kernels, give_back(): pl.pallas_call(functools.partial(give_back_kernel, group), in_specs=[pl.B...  29.5 us
    ppermute x3, waiting for transfers between devices, whole(): lax.ppermute(part, 'seq', move)  24.4 us
    pallas_call x1, Pallas kernels, prepare(): pl.pallas_call(prepare_kernel, grid_spec=pltpu.PrefetchScalarGridSpec(num...  8.29 us
    pmax x1, blocking collectives, whole(): most = lax.pmax(most, 'dp')  6.03 us
    concatenate x1, local copies, waits for them, and re-layouts, tables(): jnp.concatenate([low, steps, start, more, base, jnp.full((1, rows), side,...  3.77 us
  transfers between devices with their start and end apart: 4, of which 2 were waited for; matrix products, arithmetic and copies ran while one was open for 6% of the time, Pallas kernels for 18%

profile of v7, /device:TPU:0, one launch (start us, length us, event | category | flops | bytes accessed | tf_op | source)
XLA Modules:
  0.0 178.8 jit_solution(15292641234063594557)
XLA Ops:
  0.0 55.9 %shard_map.55 = (bf16[4,8,256,128]{3,2,1,0:T(8,128)(2,1)S(1)}, bf16[4,8,256,128]{3,2,1,0:T(8,128)(2,1)}, s32[8,2,8,256]{3,2,1,0:T(8,128)}, bf16[8,256,128]{2,1,0...) custom-call(bf16[8,256,512]{2,1,0:T(8,128)(2,1)} %k_ref.1, ...), custom_call_target="tpu_custom_call" | custom-call | tf_op jit(solution)/shard_map/pallas_call | solution.py:132
  56.0 0.9 fusion.18
  57.8 0.6 fusion.15
  58.4 0.5 broadcast_select_fusion
  59.1 3.1 %shard_map.58 = bf16[2816,256]{1,0:T(8,128)(2,1)S(1)} custom-call(s32[3,8]{1,0:T(4,128)S(1)} %pad_add_fusion.3.table_ref, s32[1]{0:T(128)} %constant.130.clone.1.shift_ref, bf16[4,8,256,128]{3,2,1,0:T(8,128)(2,1)S(1)} %get-tuple-element.148.k_ref, bf16[4,8,256,128]{3,2,1,0:T(8,128)(2,1)} %get-tuple-element.149.v_ref), custom_call_target="tpu_custom_call" | custom-call | flops 2000000 | bytes 8388608 | tf_op jit(solution)/shard_map/pallas_call | solution.py:229
  62.2 1.6 collective-permute-start.4
  63.8 1.6 collective-permute-start.1
  65.4 1.8 %collective-permute-start.2 = (bf16[8,256,128]{2,1,0:T(8,128)(2,1)}, bf16[8,256,128]{2,1,0:T(8,128)(2,1)}, u32[]{:S(2)}, u32[]{:S(2)}) collective-permute-start(bf16[8,256,128]{2,1,0:T(8,128)(2,1)} %get-tuple-element.58), channel_id=1, source_target_pairs={{0,2},{1,3},{2,0},{3,1},{4,6},{5,7},{6,4},{7,5},{8,10},{9,11},{10,... | collective-permute-start | bytes 1572872 | tf_op jit(solution)/shard_map/ppermute | solution.py:567
  67.2 1.3 reduce_max.9
  68.6 6.0 %pmax.7 = s32[]{:T(128)} all-reduce(s32[]{:T(128)} %reduce_max.9), channel_id=1, replica_groups=mesh['dp'=4,'seq'=8] {'dp'}, use_global_device_ids=true, to_apply=%region_5.6 | all-reduce | flops 1 | bytes 8 | tf_op jit(solution)/shard_map/pmax | solution.py:569
  75.2 1.1 convert_reduce_fusion
  76.4 1.1 convert_reduce_fusion.1
  77.6 0.6 pad.6.bounds_ref.refs_1_
  78.2 0.7 select_reduce_fusion.1
  78.9 0.6 fusion.8
  79.6 3.8 %concatenate.17.table_ref = s32[18,8]{1,0:T(8,128)} concatenate(s32[4,8]{1,0:T(4,128)} %get-tuple-element.101, s32[4,8]{1,0:T(4,128)} %get-tuple-element.102, s32[4,8]{1,0:T(4,128)} %get-tuple-element.92, s32[4,8]{1,0:T(4,128)S(1)} %get-tuple-element.91, s32[1,8]{1,0:T(1,128)} %copy-done.2, s32[1,8]{1,0:T(1,128)S(1)} %broadcast_in_dim.48), dimensions={0} | concatenate | bytes 1152 | tf_op jit(solution)/shard_map/concatenate | solution.py:543
  83.3 8.3 %shard_map.56 = (bf16[8,1024,256]{2,1,0:T(8,128)(2,1)}, bf16[8,160,1024]{2,1,0:T(8,128)(2,1)}, bf16[8,16,1024]{2,1,0:T(8,128)(2,1)}, bf16[5632,256]{1,0:T(8,128)(2,1)}) custom-call(s32[18,8]{1,0:T(8,128)} %concatenate.17.table_ref, bf16[4,8,256,128]{3,2,1,0:T(8,128)(2,1)S(1)} %get-tuple-element.148.k_ref, bf16[4,8,256,128]{3,2,1,0:T(8,128)(2,1)} %get-tuple-element.149.v_ref, ...), custom_call_target="tpu_custom_call" | custom-call | flops 2000000 | bytes 10485760 | tf_op jit(solution)/shard_map/pallas_call | solution.py:272
  91.6 0.6 pad_add_fusion.4.refs_0_
  92.2 14.9 %collective-permute-done.2.refs_2_ = bf16[8,256,128]{2,1,0:T(8,128)(2,1)} collective-permute-done((bf16[8,256,128]{2,1,0:T(8,128)(2,1)}, bf16[8,256,128]{2,1,0:T(8,128)(2,1)}, u32[]{:S(2)}, u32[]{:S(2)}) %collective-permute-start.2) | collective-permute-done | bytes 524320 | tf_op jit(solution)/shard_map/ppermute | solution.py:567
  107.2 9.4 %collective-permute-done.3.refs_3_ = bf16[8,256,128]{2,1,0:T(8,128)(2,1)} collective-permute-done((bf16[8,256,128]{2,1,0:T(8,128)(2,1)}, bf16[8,256,128]{2,1,0:T(8,128)(2,1)}, u32[]{:S(2)}, u32[]{:S(2)}) %collective-permute-start.3) | collective-permute-done | bytes 524320 | tf_op jit(solution)/shard_map/ppermute | solution.py:567
  116.6 23.4 %shard_map.57 = (bf16[4,8,256,128]{3,2,1,0:T(8,128)(2,1)}, bf16[4,8,256,128]{3,2,1,0:T(8,128)(2,1)}, f32[32,2,1,256]{3,2,1,0:T(1,128)}, f32[32,2,80,256]{3,2,1,0:T(8,128)}) custom-call(s32[18,8]{1,0:T(8,128)} %concatenate.17.table_ref, bf16[8,256,128]{2,1,0:T(8,128)(2,1)} %get-tuple-element.56.refs_0_, bf16[8,256,128]{2,1,0:T(8,128)(2,1)} %collective-permute-done.1.refs_1_, ...), custom_call_target="tpu_custom_call" | custom-call | flops 2147483648 | bytes 8388608 | tf_op jit(solution)/shard_map/pallas_call | solution.py:491
  140.0 6.3 %shard_map.59.o_ref = bf16[4,8,256,128]{3,2,1,0:T(8,128)(2,1)} custom-call(s32[18,8]{1,0:T(8,128)} %concatenate.17.table_ref, s32[2]{0:T(128)} %pad_add_fusion.4.refs_0_, s32[8,4,128]{2,1,0:T(4,128)} %pad.6.bounds_ref.refs_1_, bf16[4,8,256,128]{3,2,1,0:T(8,128)(2,1)} %get-tuple-element.65.refs_2_, ...), custom_call_target="tpu_custom_call", output_to_operand_aliasing={{}: (9, {})} | custom-call | flops 536870912 | bytes 8388608 | tf_op jit(solution)/shard_map/pallas_call | solution.py:491
  146.2 29.5 %shard_map.60 = bf16[8,256,512]{2,1,0:T(8,128)(2,1)} custom-call(bf16[4,8,256,128]{3,2,1,0:T(8,128)(2,1)} %shard_map.59.o_ref), custom_call_target="tpu_custom_call" | custom-call | tf_op jit(solution)/shard_map/pallas_call | solution.py:178
  175.7 3.0 %copy.59 = bf16[8,256,512]{2,1,0:T(8,128)(2,1)} copy(bf16[8,256,512]{2,1,0:T(8,128)(2,1)} %shard_map.60) | data formatting | bytes 4194304
  (31 shorter events, 1.3 us)
Async XLA Ops:
  56.8 2.2 %copy-start = (s32[1,8,8,256]{3,1,0,2:T(8,128)}, s32[1,8,8,256]{3,1,0,2:T(8,128)S(1)}, u32[]{:S(2)}) copy-start(s32[1,8,8,256]{3,1,0,2:T(8,128)S(1)} %get-tuple-element.95) | copy-start | bytes 196612
  56.8 2.2 %copy-start.1 = (s32[1,8,8,256]{3,1,0,2:T(8,128)}, s32[1,8,8,256]{3,1,0,2:T(8,128)S(1)}, u32[]{:S(2)}) copy-start(s32[1,8,8,256]{3,1,0,2:T(8,128)S(1)} %get-tuple-element.96) | copy-start | bytes 196612
  62.2 77.8 %collective-permute-start.4 = (bf16[2816,256]{1,0:T(8,128)(2,1)S(1)}, bf16[2816,256]{1,0:T(8,128)(2,1)}, u32[]{:S(2)}, u32[]{:S(2)}) collective-permute-start(bf16[2816,256]{1,0:T(8,128)(2,1)S(1)} %shard_map.58), channel_id=1, source_target_pairs={{0,4},{1,5},{2,6},{3,7},{4,0},{5,1},{6,2},{7,3},{8,12},{9,13},{10,... | collective-permute-start | bytes 4325384 | tf_op jit(solution)/shard_map/ppermute | solution.py:557
  63.8 28.4 %collective-permute-start.1 = (bf16[8,256,128]{2,1,0:T(8,128)(2,1)}, bf16[8,256,128]{2,1,0:T(8,128)(2,1)}, u32[]{:S(2)}, u32[]{:S(2)}) collective-permute-start(bf16[8,256,128]{2,1,0:T(8,128)(2,1)} %get-tuple-element.57), channel_id=1, source_target_pairs={{0,1},{1,0},{2,3},{3,2},{4,5},{5,4},{6,7},{7,6},{8,9},{9,8},{10,11... | collective-permute-start | bytes 1572872 | tf_op jit(solution)/shard_map/ppermute | solution.py:567
  65.4 41.7 %collective-permute-start.2 = (bf16[8,256,128]{2,1,0:T(8,128)(2,1)}, bf16[8,256,128]{2,1,0:T(8,128)(2,1)}, u32[]{:S(2)}, u32[]{:S(2)}) collective-permute-start(bf16[8,256,128]{2,1,0:T(8,128)(2,1)} %get-tuple-element.58), channel_id=1, source_target_pairs={{0,2},{1,3},{2,0},{3,1},{4,6},{5,7},{6,4},{7,5},{8,10},{9,11},{10,... | collective-permute-start | bytes 1572872 | tf_op jit(solution)/shard_map/ppermute | solution.py:567
  68.5 48.1 %collective-permute-start.3 = (bf16[8,256,128]{2,1,0:T(8,128)(2,1)}, bf16[8,256,128]{2,1,0:T(8,128)(2,1)}, u32[]{:S(2)}, u32[]{:S(2)}) collective-permute-start(bf16[8,256,128]{2,1,0:T(8,128)(2,1)} %get-tuple-element.59), channel_id=1, source_target_pairs={{0,3},{1,2},{2,1},{3,0},{4,7},{5,6},{6,5},{7,4},{8,11},{9,10},{10,... | collective-permute-start | bytes 1572872 | tf_op jit(solution)/shard_map/ppermute | solution.py:567
  78.9 0.6 copy-start.2
